TPU v7x, 256 devices: a whole 4x4x8 slice. The times are simulated.
256 devices in a mesh: lat: 8 (over x_lo, y), lon: 32 (over z, x_hi, core).
Axes of the slice: x: 4 (x_hi: 2, x_lo: 2; x = x_hi * 2 + x_lo), y: 4, z: 8, core: 2. Of those that a mesh axis runs over, the one named last changes fastest.
Arguments:
- activations: bfloat16 [4, 32, 2880, 512], P(None, 'lat', 'lon'), may hold values from -48 to 48
- upstream: bfloat16 [4, 32, 2880, 512], P(None, 'lat', 'lon'), may hold values from -6 to 6
- master: float32 [512, 9, 512], P(('lat', 'lon')), may hold values from -0.09375 to 0.09375
- moment_one: float32 [512, 9, 512], P(('lat', 'lon')), may hold values from -2.5 to 2.5
- moment_two: float32 [512, 9, 512], P(('lat', 'lon')), may hold values from 0.01 to 1
Outputs:
- input_grad: bfloat16 [4, 32, 2880, 512], P(None, 'lat', 'lon')
- new_weights: bfloat16 [512, 9, 512], replicated
- new_master: float32 [512, 9, 512], P(('lat', 'lon'))
- new_moment_one: float32 [512, 9, 512], P(('lat', 'lon'))
- new_moment_two: float32 [512, 9, 512], P(('lat', 'lon'))
- clipped_grad: float32 [512, 9, 512], P(('lat', 'lon'))
All inputs are finite; a program needn't handle non-finite values.
Results may differ from a plain program's by a relative error of at most 0.0049.
Values may be sent and summed in bfloat16 or wider, within the bound.
No kernel may reach another device: no remote copies, remote signals or barrier semaphores. Data moves between devices by JAX's collectives and lax.ppermute only.
A program may use at most 128 MiB of HBM per device.

v0:
```python
import math

import jax
import jax.numpy as jnp
from jax import lax
from jax.experimental import pallas as pl
from jax.experimental.pallas import tpu as pltpu
from jax.sharding import Mesh
from jax.sharding import PartitionSpec as P


TAPS = 9
ALL = ("xl", "y", "z", "xh", "c")
LAT = ("xl", "y")
LON = ("z", "xh", "c")
PLANE = ("xl", "y", "xh")
BF16 = jnp.bfloat16
F32 = jnp.float32

learn_rate = 0.01
beta_one = 0.9
beta_two = 0.999
adam_eps = 1e-08
decay_rate = 0.1
step_count = 10.0
norm_eps = 1e-06


def rows_of(shape, dim):
    return lax.broadcasted_iota(jnp.int32, shape, dim)


def channel_of(core, plane, z, k):
    lat, xh = plane // 2, plane % 2
    return (((lat * 8 + z) * 2 + xh) * 2 + core) * 2 + k


def gather_order(p):
    z, core, plane, k = p // 64, (p // 32) % 2, (p // 2) % 16, p % 2
    return channel_of(core, plane, z, k)


def neighbours(count, circular):
    forward = [(i, i + 1) for i in range(count - 1)]
    if circular:
        forward.append((count - 1, 0))
    return forward, [(b, a) for a, b in forward]


def row_halo(rows):
    forward, backward = neighbours(8, False)
    above = lax.ppermute(rows[-1:], LAT, forward)
    below = lax.ppermute(rows[:1], LAT, backward)
    return above, below


def col_halo(above, rows, below):
    east = jnp.concatenate([part[:, :, -1:] for part in (above, rows, below)], axis=0)
    west = jnp.concatenate([part[:, :, :1] for part in (above, rows, below)], axis=0)
    forward, backward = neighbours(32, True)
    left = lax.ppermute(east, LON, forward)
    right = lax.ppermute(west, LON, backward)
    return left, right


def swap(array):
    return lax.ppermute(array, "c", [(0, 1), (1, 0)])


def store_halves(core_ref, lhs, window_of, keep_ref, send_ref):
    half = keep_ref.shape[1]
    own = pl.multiple_of(core_ref[0] * half, half)
    other = pl.multiple_of((1 - core_ref[0]) * half, half)
    send_ref[...] = window_of(lhs, pl.ds(other, half)).astype(BF16)
    keep_ref[...] = window_of(lhs, pl.ds(own, half))


def centre_kernel(core_ref, lhs_ref, above_ref, rows_ref, below_ref, keep_ref, send_ref):
    block = above_ref.shape[0]
    row = pl.program_id(0)

    def dots(pieces, outs):
        total = None
        for start, ref, first, count in pieces:
            part = jnp.dot(
                lhs_ref[:, start : start + count],
                ref[first : first + count, outs],
                preferred_element_type=F32,
            )
            total = part if total is None else total + part
        return total

    plans = (
        ((0, rows_ref, block, 3 * block), (3 * block, below_ref, 0, block)),
        ((0, rows_ref, 0, 4 * block),),
        ((0, above_ref, 0, block), (block, rows_ref, 0, 3 * block)),
    )
    for index, plan in enumerate(plans):

        @pl.when(row == index)
        def _(plan=plan):
            store_halves(core_ref, None, lambda _, outs: dots(plan, outs), keep_ref, send_ref)


def centre_grads(core, lhs, above, rows, below):
    chans, outs = lhs.shape[0], rows.shape[1]
    half = outs // 2
    whole = lambda array: pl.BlockSpec(array.shape, lambda t: (0,) * array.ndim)
    return pl.pallas_call(
        centre_kernel,
        grid=(3,),
        in_specs=[
            pl.BlockSpec(memory_space=pltpu.SMEM),
            whole(lhs),
            whole(above),
            whole(rows),
            whole(below),
        ],
        out_specs=[pl.BlockSpec((chans, half), lambda t: (0, t))] * 2,
        out_shape=[
            jax.ShapeDtypeStruct((chans, 3 * half), F32),
            jax.ShapeDtypeStruct((chans, 3 * half), BF16),
        ],
        compiler_params=pltpu.CompilerParams(vmem_limit_bytes=48 * 1024 * 1024),
        cost_estimate=pl.CostEstimate(
            flops=2 * chans * lhs.shape[1] * 3 * outs, bytes_accessed=8_000_000, transcendentals=0
        ),
        name="centre_grads",
    )(core, lhs, above, rows, below)


def side_kernel(
    core_ref, lhs_ref, above_ref, rows_ref, below_ref, left_ref, right_ref,
    field_ref, keep_ref, send_ref, *, cols, padded_cols,
):
    step = pl.program_id(0)
    block = above_ref.shape[0]
    batch = block // padded_cols

    @pl.when(step == 0)
    def _():
        index = lax.broadcasted_iota(jnp.int32, (padded_cols, 1), 0)
        for line in range(6 * batch):
            first = line * padded_cols
            if line < batch:
                ref, start = above_ref, first
            elif line < 5 * batch:
                ref, start = rows_ref, first - block
            else:
                ref, start = below_ref, first - 5 * block
            centre = ref[start : start + padded_cols, :]
            field_ref[1, first : first + padded_cols, :] = centre
            wide = centre.astype(F32)
            east = pltpu.roll(wide, padded_cols - 1, 0)
            east = jnp.where(index == cols - 1, right_ref[line : line + 1, :], east)
            field_ref[0, first : first + padded_cols, :] = east.astype(BF16)
            west = pltpu.roll(wide, 1, 0)
            west = jnp.where(index == 0, left_ref[line : line + 1, :], west)
            field_ref[2, first : first + padded_cols, :] = west.astype(BF16)

    row, side = step // 2, 2 * (step % 2)
    start = pl.multiple_of((2 - row) * block, block)

    def window_dot(_, outs):
        return jnp.dot(
            lhs_ref[...],
            field_ref[side, pl.ds(start, 4 * block), outs],
            preferred_element_type=F32,
        )

    store_halves(core_ref, None, window_dot, keep_ref, send_ref)


def side_grads(core, lhs, above, rows, below, left, right, cols, padded_cols):
    chans, outs = lhs.shape[0], rows.shape[1]
    half = outs // 2
    whole = lambda array: pl.BlockSpec(array.shape, lambda t: (0,) * array.ndim)
    length = rows.shape[0] * 3 // 2
    return pl.pallas_call(
        lambda *refs: side_kernel(*refs, cols=cols, padded_cols=padded_cols),
        grid=(6,),
        in_specs=[pl.BlockSpec(memory_space=pltpu.SMEM)]
        + [whole(array) for array in (lhs, above, rows, below, left, right)],
        out_specs=[pl.BlockSpec((3, length, outs), lambda t: (0, 0, 0))]
        + [pl.BlockSpec((chans, half), lambda t: (0, t))] * 2,
        out_shape=[
            jax.ShapeDtypeStruct((3, length, outs), BF16),
            jax.ShapeDtypeStruct((chans, 6 * half), F32),
            jax.ShapeDtypeStruct((chans, 6 * half), BF16),
        ],
        compiler_params=pltpu.CompilerParams(vmem_limit_bytes=56 * 1024 * 1024),
        cost_estimate=pl.CostEstimate(
            flops=2 * chans * lhs.shape[1] * 6 * outs, bytes_accessed=16_000_000, transcendentals=0
        ),
        name="side_grads",
    )(core, lhs, above, rows, below, left, right)


def pull_kernel(field_ref, weight_ref, order_ref, out_ref, *, block):
    step = pl.program_id(0)
    outs = field_ref.shape[2]
    total = jnp.zeros((block, weight_ref.shape[0]), F32)
    for tap in range(TAPS):
        row, col = divmod(tap, 3)
        start = pl.multiple_of((step + 2 - row) * block, block)
        total = total + lax.dot_general(
            field_ref[col, pl.ds(start, block), :],
            weight_ref[:, tap * outs : (tap + 1) * outs],
            (((1,), (1,)), ((), ())),
            preferred_element_type=F32,
        )
    out_ref[...] = jnp.dot(
        total.astype(BF16), order_ref[...], preferred_element_type=F32
    ).astype(BF16)


def pulled(fields, weights, order):
    block = fields.shape[1] // 6
    chans = weights.shape[0]
    return pl.pallas_call(
        lambda *refs: pull_kernel(*refs, block=block),
        grid=(4,),
        in_specs=[
            pl.BlockSpec(fields.shape, lambda i: (0, 0, 0)),
            pl.BlockSpec(weights.shape, lambda i: (0, 0)),
            pl.BlockSpec(order.shape, lambda i: (0, 0)),
        ],
        out_specs=pl.BlockSpec((block, chans), lambda i: (i, 0)),
        out_shape=jax.ShapeDtypeStruct((4 * block, chans), BF16),
        compiler_params=pltpu.CompilerParams(vmem_limit_bytes=48 * 1024 * 1024),
        cost_estimate=pl.CostEstimate(
            flops=2 * 4 * block * chans * weights.shape[1],
            bytes_accessed=14_000_000,
            transcendentals=0,
        ),
        name="pulled",
    )(fields, weights, order)


def join_kernel(core_ref, own_ref, other_ref, out_ref):
    half = own_ref.shape[1]
    own = pl.multiple_of(core_ref[0] * half, half)
    other = pl.multiple_of((1 - core_ref[0]) * half, half)
    out_ref[0, :, pl.ds(own, half)] = own_ref[...]
    out_ref[0, :, pl.ds(other, half)] = other_ref[...]


def joined(core, own, other):
    chans, wide = own.shape
    half = wide // TAPS
    return pl.pallas_call(
        join_kernel,
        grid=(TAPS,),
        in_specs=[
            pl.BlockSpec(memory_space=pltpu.SMEM),
            pl.BlockSpec((chans, half), lambda t: (0, t)),
            pl.BlockSpec((chans, half), lambda t: (0, t)),
        ],
        out_specs=pl.BlockSpec((1, chans, 2 * half), lambda t: (t, 0, 0)),
        out_shape=jax.ShapeDtypeStruct((TAPS, chans, 2 * half), BF16),
        name="joined",
    )(core, own, other)


def to_all(piece, axes, count):
    copies = jnp.broadcast_to(piece[None], (count, *piece.shape))
    return lax.all_to_all(copies, axes, 0, 0, tiled=True)


def halves(array, core):
    half = array.shape[-1] // 2
    low, high = array[..., :half], array[..., half:]
    return jnp.where(core == 0, low, high), jnp.where(core == 0, high, low)


def in_core_order(own, other, core, axis):
    return jnp.where(
        core == 0,
        jnp.concatenate([own, other], axis=axis),
        jnp.concatenate([other, own], axis=axis),
    )


def per_device(activations, upstream, master, moment_one, moment_two):
    batch, lat_rows, lon_cols, chans = activations.shape
    outs = upstream.shape[3]
    wide = TAPS * outs
    half = outs // 2
    padded_cols = -(-lon_cols // 32) * 32
    extra = padded_cols - lon_cols
    core = lax.axis_index("c")
    core_ref = core.reshape(1).astype(jnp.int32)

    def padded(rows):
        return jnp.pad(rows, ((0, 0), (0, 0), (0, extra), (0, 0))).reshape(-1, rows.shape[3])

    up_rows = jnp.transpose(upstream, (1, 0, 2, 3))
    above, below = row_halo(up_rows)

    old_piece = master.astype(BF16).reshape(2, wide)
    old_plane = to_all(old_piece, PLANE, 16).reshape(32, wide)
    state = jnp.stack([master, moment_one, moment_two])
    own_state, other_state = halves(state, core)
    state = in_core_order(own_state, swap(other_state), core, 1)
    above, below, old_plane, state = lax.optimization_barrier((above, below, old_plane, state))
    old_weights = lax.all_gather(old_plane, ("z", "c"), axis=0, tiled=True)

    left, right = col_halo(above, up_rows, below)
    lhs = padded(jnp.transpose(activations, (1, 0, 2, 3))).T
    pieces = (padded(above), padded(up_rows), padded(below))
    keep_one, send_one = centre_grads(core_ref, lhs, *pieces)
    swapped_one = swap(send_one)
    left, right, keep_one = lax.optimization_barrier((left, right, keep_one))
    sides = [side.reshape(-1, outs).astype(F32) for side in (left, right)]
    fields, keep_two, send_two = side_grads(core_ref, lhs, *pieces, *sides, lon_cols, padded_cols)
    swapped_two = swap(send_two)
    pair_sum = jnp.concatenate(
        [
            (keep_one + swapped_one.astype(F32)).astype(BF16),
            (keep_two + swapped_two.astype(F32)).astype(BF16),
        ],
        axis=1,
    ).reshape(8, 64, TAPS * half)
    parts = lax.all_to_all(pair_sum, LAT, 0, 0, tiled=True)
    lat_sum = jnp.sum(parts.astype(F32), axis=0).astype(BF16).reshape(16, 4, TAPS * half)
    parts = lax.all_to_all(lat_sum, ("z", "xh"), 0, 0, tiled=True)
    grad = jnp.sum(parts.astype(F32), axis=0).reshape(4, TAPS, half)
    square_sum = jnp.sum(grad * grad).reshape(1, 1)
    centre, sides = grad[:, :3], grad[:, 3:].reshape(4, 3, 2, half)
    grad = jnp.stack([sides[:, :, 0], centre, sides[:, :, 1]], axis=2).reshape(4, TAPS, half)

    square_sum = jnp.sum(to_all(square_sum, PLANE, 16)).reshape(1, 1)
    square_sum = jnp.sum(to_all(square_sum, ("z", "c"), 16))
    max_norm = math.sqrt(float(chans * TAPS * outs))
    clip_factor = jnp.minimum(1.0, max_norm / (jnp.sqrt(square_sum) + norm_eps))
    clipped = clip_factor * grad
    old_master, old_one, old_two = state
    new_one = beta_one * old_one + (1.0 - beta_one) * clipped
    new_two = beta_two * old_two + (1.0 - beta_two) * clipped * clipped
    first_hat = new_one / (1.0 - beta_one**step_count)
    second_hat = new_two / (1.0 - beta_two**step_count)
    new_master = old_master - learn_rate * (
        first_hat / (jnp.sqrt(second_hat) + adam_eps) + decay_rate * old_master
    )

    new_piece = new_master.astype(BF16).reshape(4, TAPS * half)
    line = to_all(new_piece, ("z", "xh"), 16).reshape(64, TAPS * half)
    line, fields, old_weights, results = lax.optimization_barrier(
        (line, fields, old_weights, jnp.stack([new_master, new_one, new_two, clipped]))
    )
    own = to_all(line, LAT, 8).reshape(chans, TAPS * half)
    mine = jnp.where(core == 0, results[:, :2], results[:, 2:])
    theirs = jnp.where(core == 0, results[:, 2:], results[:, :2])
    results = in_core_order(mine, swap(theirs), core, 3)

    square = (chans, chans)
    back = (gather_order(rows_of(square, 0)) == rows_of(square, 1)).astype(BF16)
    pulled_rows = pulled(fields, old_weights, back)
    input_grad = pulled_rows.reshape(lat_rows, batch, padded_cols, chans)[:, :, :lon_cols]
    input_grad = jnp.transpose(input_grad, (1, 0, 2, 3))

    new_weights = jnp.transpose(joined(core_ref, own, swap(own)), (1, 0, 2))
    return (input_grad, new_weights, *results)


def solution(mesh):
    split = Mesh(mesh.devices.reshape(2, 4, 8, 2, 2), ALL)
    field = P(None, LAT, LON, None)
    state = P(ALL, None, None)
    return jax.shard_map(
        per_device,
        mesh=split,
        in_specs=(field, field, state, state, state),
        out_specs=(field, P(), state, state, state, state),
        check_vma=False,
    )
```

profile of v0, /device:TPU:5, one launch (start us, length us, event | category | flops | bytes accessed | tf_op | source)
XLA Modules:
  0.0 235.6 jit_solution(10474277789496458596)
XLA Ops:
  7.2 1.7 copy.84
  9.9 4.0 %collective-permute-start = (bf16[1,4,90,512]{3,2,1,0:T(8,128)(2,1)}, bf16[1,4,90,512]{3,2,1,0:T(8,128)(2,1)}, u32[]{:S(2)}, u32[]{:S(2)}) collective-permute-start(bf16[1,4,90,512]{3,2,1,0:T(8,128)(2,1)} %get-tuple-element.44), channel_id=1, source_target_pairs={{0,32},{32,64},{64,96},{96,128},{128,160},{160,192},{192,224},{1,3... | collective-permute-start | bytes 1105928 | tf_op jit(solution)/shard_map/ppermute | solution.py:52
  16.0 7.2 %all-to-all-start = ((bf16[16,2,4608]{2,1,0:T(2,128)(2,1)}), bf16[16,2,4608]{2,1,0:T(2,128)(2,1)S(1)}, u32[]{:S(2)}, u32[]{:S(2)}) async-start(bf16[16,2,4608]{2,1,0:T(2,128)(2,1)} %broadcast_in_dim.13), calls=%async_computation | async-start | bytes 589824 | tf_op jit(solution)/shard_map/all_to_all | solution.py:267
  23.5 1.9 collective-permute-start.2
  28.6 1.8 maximum_select_fusion.1
  32.3 1.9 pad.17
  35.2 4.6 %collective-permute-start.3 = (bf16[6,4,1,512]{3,2,1,0:T(2,128)(2,1)S(1)}, bf16[6,4,1,512]{3,2,1,0:T(2,128)(2,1)S(1)}, u32[]{:S(2)}, u32[]{:S(2)}) collective-permute-start(bf16[6,4,1,512]{3,2,1,0:T(2,128)(2,1)S(1)} %pad_maximum_fusion.3), channel_id=1, source_target_pairs={{0,1},{1,2},{2,3},{3,4},{4,5},{5,6},{6,7},{7,8},{8,9},{9,10},{10,1... | collective-permute-start | bytes 73736 | tf_op jit(solution)/shard_map/ppermute | solution.py:61
  40.9 4.9 %centre_grads.1 = (f32[512,768]{1,0:T(8,128)S(1)}, bf16[512,768]{1,0:T(8,128)(2,1)S(1)}) custom-call(s32[1]{0:T(128)} %bitcast.7.core_ref.refs_0_, bf16[512,1536]{1,0:T(8,128)(2,1)S(1)} %bitcast.45, bf16[384,512]{1,0:T(8,128)(2,1)S(1)} %bitcast.48, bf16[1536,512]{1,0:T(8,128)(2,1)} %bitcast.61, bf16[384,512]{1,0:T(8,128)(2,1)S(1)} %bitcast.51), custom_call_target="tpu_custom_call" | custom-call | flops 2415919104 | bytes 8000000 | tf_op jit(solution)/shard_map/centre_grads/pallas_call | solution.py:109
  49.1 11.9 %side_grads.1 = (bf16[3,2304,512]{2,1,0:T(8,128)(2,1)}, f32[512,1536]{1,0:T(8,128)}, bf16[512,1536]{1,0:T(8,128)(2,1)}) custom-call(s32[1]{0:T(128)} %bitcast.7.core_ref.refs_0_, bf16[512,1536]{1,0:T(8,128)(2,1)} %bitcast.46, bf16[384,512]{1,0:T(8,128)(2,1)} %bitcast.49, bf16[1536,512]{1,0:T(8,128)(2,1)} %bitcast.62, bf16[384,512]{1,0:T(8,128)(2,1)} %bitcast.50, ...), custom_call_target="tpu_custom_call" | custom-call | flops 4831838208 | bytes 16000000 | tf_op jit(solution)/shard_map/side_grads/pallas_call | solution.py:179
  61.4 4.7 %collective-permute-done.5 = bf16[512,768]{1,0:T(8,128)(2,1)S(1)} collective-permute-done((bf16[512,768]{1,0:T(8,128)(2,1)S(1)}, bf16[512,768]{1,0:T(8,128)(2,1)S(1)}, u32[]{:S(2)}, u32[]{:S(2)}) %collective-permute-start.5) | collective-permute-done | bytes 786464 | tf_op jit(solution)/shard_map/ppermute | solution.py:67
  66.9 32.7 %all_to_all.35 = bf16[8,64,2304]{2,1,0:T(8,128)(2,1)S(1)} all-to-all(bf16[8,64,2304]{2,1,0:T(8,128)(2,1)S(1)} %bitcast.55), channel_id=1, replica_groups=mesh['xl'=2,'y'=4,'z'=8,'xh'=2,'c'=2] {'xl','y'}, dimensions={0} | all-to-all | bytes 4718592 | tf_op jit(solution)/shard_map/all_to_all | solution.py:324
  100.0 20.1 %all_to_all.36 = bf16[16,4,2304]{2,1,0:T(4,128)(2,1)S(1)} all-to-all(bf16[16,4,2304]{2,1,0:T(4,128)(2,1)S(1)} %reshape.146), channel_id=1, replica_groups=mesh['xl'=2,'y'=4,'z'=8,'xh'=2,'c'=2] {'z','xh'}, dimensions={0} | all-to-all | bytes 589824 | tf_op jit(solution)/shard_map/all_to_all | solution.py:326
  122.2 7.1 %all-to-all-start.3 = ((f32[16,1,1]{2,1,0:T(1,128)}), f32[16,1,1]{2,1,0:T(1,128)S(1)}, u32[]{:S(2)}, u32[]{:S(2)}) async-start(f32[16,1,1]{2,1,0:T(1,128)} %broadcast_in_dim.14), calls=%async_computation.3 | async-start | bytes 16384 | tf_op jit(solution)/shard_map/all_to_all | solution.py:267
  129.3 4.4 %all-to-all-done.3 = f32[16,1,1]{2,1,0:T(1,128)S(1)} async-done(((f32[16,1,1]{2,1,0:T(1,128)}), f32[16,1,1]{2,1,0:T(1,128)S(1)}, u32[]{:S(2)}, u32[]{:S(2)}) %all-to-all-start.3) | async-done | bytes 96 | tf_op jit(solution)/shard_map/all_to_all | solution.py:267
  135.5 7.8 %all-to-all-start.4 = ((f32[16,1,1]{2,1,0:T(1,128)}), f32[16,1,1]{2,1,0:T(1,128)S(1)}, u32[]{:S(2)}, u32[]{:S(2)}) async-start(f32[16,1,1]{2,1,0:T(1,128)} %broadcast_in_dim.15), calls=%async_computation.4 | async-start | bytes 16384 | tf_op jit(solution)/shard_map/all_to_all | solution.py:267
  143.3 7.0 %all-to-all-done.4 = f32[16,1,1]{2,1,0:T(1,128)S(1)} async-done(((f32[16,1,1]{2,1,0:T(1,128)}), f32[16,1,1]{2,1,0:T(1,128)S(1)}, u32[]{:S(2)}, u32[]{:S(2)}) %all-to-all-start.4) | async-done | bytes 96 | tf_op jit(solution)/shard_map/all_to_all | solution.py:267
  152.7 5.4 %all-to-all-start.5 = ((bf16[16,4,2304]{2,1,0:T(4,128)(2,1)}), bf16[16,4,2304]{2,1,0:T(4,128)(2,1)S(1)}, u32[]{:S(2)}, u32[]{:S(2)}) async-start(bf16[16,4,2304]{2,1,0:T(4,128)(2,1)} %broadcast_in_dim.32), calls=%async_computation.5 | async-start | bytes 589824 | tf_op jit(solution)/shard_map/all_to_all | solution.py:267
  158.1 10.5 %all-to-all-done.5 = bf16[16,4,2304]{2,1,0:T(4,128)(2,1)S(1)} async-done(((bf16[16,4,2304]{2,1,0:T(4,128)(2,1)}), bf16[16,4,2304]{2,1,0:T(4,128)(2,1)S(1)}, u32[]{:S(2)}, u32[]{:S(2)}) %all-to-all-start.5) | async-done | bytes 294944 | tf_op jit(solution)/shard_map/all_to_all | solution.py:267
  168.7 1.6 broadcast_in_dim.33
  170.3 3.6 %all-to-all-start.6 = ((bf16[8,64,2304]{2,1,0:T(8,128)(2,1)}), bf16[8,64,2304]{2,1,0:T(8,128)(2,1)S(1)}, u32[]{:S(2)}, u32[]{:S(2)}) async-start(bf16[8,64,2304]{2,1,0:T(8,128)(2,1)} %broadcast_in_dim.33), calls=%async_computation.6 | async-start | bytes 4718592 | tf_op jit(solution)/shard_map/all_to_all | solution.py:267
  173.9 28.9 %all-to-all-done.6 = bf16[8,64,2304]{2,1,0:T(8,128)(2,1)S(1)} async-done(((bf16[8,64,2304]{2,1,0:T(8,128)(2,1)}), bf16[8,64,2304]{2,1,0:T(8,128)(2,1)S(1)}, u32[]{:S(2)}, u32[]{:S(2)}) %all-to-all-start.6) | async-done | bytes 2359328 | tf_op jit(solution)/shard_map/all_to_all | solution.py:267
  205.0 13.5 %pulled.1 = bf16[1536,512]{1,0:T(8,128)(2,1)S(1)} custom-call(bf16[3,2304,512]{2,1,0:T(8,128)(2,1)} %get-tuple-element.34.refs_0_, bf16[512,4608]{1,0:T(8,128)(2,1)} %all-gather.2.cloned.1.call-done.refs_1_, bf16[512,512]{1,0:T(8,128)(2,1)S(1)} %fusion.15.refs_2_), custom_call_target="tpu_custom_call" | custom-call | flops 7247757312 | bytes 14000000 | tf_op jit(solution)/shard_map/pulled/pallas_call | solution.py:220
  218.5 2.3 copy.85
  221.5 7.3 %joined.1 = bf16[9,512,512]{2,1,0:T(8,128)(2,1)} custom-call(s32[1]{0:T(128)} %bitcast.7.core_ref.refs_0_, bf16[512,2304]{1,0:T(8,128)(2,1)} %bitcast.57, bf16[512,2304]{1,0:T(8,128)(2,1)} %collective-permute-done.7.other_ref), custom_call_target="tpu_custom_call" | custom-call | tf_op jit(solution)/shard_map/joined/pallas_call | solution.py:251
  (97 shorter events, 23.9 us)
Async XLA Ops:
  8.9 14.4 %copy-start.12 = (f32[2,9,512]{2,0,1:T(2,128)S(1)}, f32[2,9,512]{2,0,1:T(2,128)}, u32[]{:S(2)}) copy-start(f32[2,9,512]{2,0,1:T(2,128)} %param.9) | copy-start | bytes 110596
  8.9 14.4 %copy-start.13 = (f32[2,9,512]{2,0,1:T(2,128)S(1)}, f32[2,9,512]{2,0,1:T(2,128)}, u32[]{:S(2)}) copy-start(f32[2,9,512]{2,0,1:T(2,128)} %param.8) | copy-start | bytes 110596
  8.9 17.1 %copy-start.7 = (bf16[4,4,90,512]{3,1,2,0:T(4,128)(2,1)S(1)}, bf16[4,4,90,512]{3,1,2,0:T(4,128)(2,1)}, u32[]{:S(2)}) copy-start(bf16[4,4,90,512]{3,1,2,0:T(4,128)(2,1)} %param.5) | copy-start | bytes 4423684
  9.9 21.3 %collective-permute-start = (bf16[1,4,90,512]{3,2,1,0:T(8,128)(2,1)}, bf16[1,4,90,512]{3,2,1,0:T(8,128)(2,1)}, u32[]{:S(2)}, u32[]{:S(2)}) collective-permute-start(bf16[1,4,90,512]{3,2,1,0:T(8,128)(2,1)} %get-tuple-element.44), channel_id=1, source_target_pairs={{0,32},{32,64},{64,96},{96,128},{128,160},{160,192},{192,224},{1,3... | collective-permute-start | bytes 1105928 | tf_op jit(solution)/shard_map/ppermute | solution.py:52
  13.8 17.4 %collective-permute-start.1 = (bf16[1,4,90,512]{3,2,1,0:T(8,128)(2,1)}, bf16[1,4,90,512]{3,2,1,0:T(8,128)(2,1)}, u32[]{:S(2)}, u32[]{:S(2)}) collective-permute-start(bf16[1,4,90,512]{3,2,1,0:T(8,128)(2,1)} %get-tuple-element.43), channel_id=1, source_target_pairs={{32,0},{64,32},{96,64},{128,96},{160,128},{192,160},{224,192},{33,... | collective-permute-start | bytes 1105928 | tf_op jit(solution)/shard_map/ppermute | solution.py:53
  16.0 14.3 %all-to-all-start = ((bf16[16,2,4608]{2,1,0:T(2,128)(2,1)}), bf16[16,2,4608]{2,1,0:T(2,128)(2,1)S(1)}, u32[]{:S(2)}, u32[]{:S(2)}) async-start(bf16[16,2,4608]{2,1,0:T(2,128)(2,1)} %broadcast_in_dim.13), calls=%async_computation | async-start | bytes 589824 | tf_op jit(solution)/shard_map/all_to_all | solution.py:267
  23.3 145.4 %all-gather.2.cloned.1.call-start = ((), (), s32[]{:S(2)}) async-start(), calls=%async_computation.7 | async-start | bytes 5013504 | tf_op jit(solution)/shard_map/all_gather | solution.py:306
  23.5 5.1 %collective-permute-start.2 = (f32[3,2,9,256]{3,1,2,0:T(2,128)S(1)}, f32[3,2,9,256]{3,1,2,0:T(2,128)}, u32[]{:S(2)}, u32[]{:S(2)}) collective-permute-start(f32[3,2,9,256]{3,1,2,0:T(2,128)S(1)} %get-tuple-element.59), channel_id=1, source_target_pairs={{0,1},{1,0},{2,3},{3,2},{4,5},{5,4},{6,7},{7,6},{8,9},{9,8},{10,11... | collective-permute-start | bytes 165896 | tf_op jit(solution)/shard_map/ppermute | solution.py:67
  28.5 17.3 %copy-start = (bf16[1536,512]{0,1:T(8,128)(2,1)}, bf16[1536,512]{0,1:T(8,128)(2,1)S(1)}, u32[]{:S(2)}) copy-start(bf16[1536,512]{0,1:T(8,128)(2,1)S(1)} %copy.67) | copy-start | bytes 4718596
  28.6 11.2 %copy-start.10 = (bf16[4,4,1,512]{3,2,1,0:T(2,128)(2,1)S(1)}, bf16[4,4,1,512]{3,2,1,0:T(2,128)(2,1)}, u32[]{:S(2)}) copy-start(bf16[4,4,1,512]{3,2,1,0:T(2,128)(2,1)} %get-tuple-element.41) | copy-start | bytes 49156
  32.2 13.6 %copy-start.1 = (bf16[1,4,96,512]{3,2,1,0:T(8,128)(2,1)}, bf16[1,4,96,512]{3,2,1,0:T(8,128)(2,1)S(1)}, u32[]{:S(2)}) copy-start(bf16[1,4,96,512]{3,2,1,0:T(8,128)(2,1)S(1)} %pad.15) | copy-start | bytes 1179652
  35.2 11.5 %collective-permute-start.3 = (bf16[6,4,1,512]{3,2,1,0:T(2,128)(2,1)S(1)}, bf16[6,4,1,512]{3,2,1,0:T(2,128)(2,1)S(1)}, u32[]{:S(2)}, u32[]{:S(2)}) collective-permute-start(bf16[6,4,1,512]{3,2,1,0:T(2,128)(2,1)S(1)} %pad_maximum_fusion.3), channel_id=1, source_target_pairs={{0,1},{1,2},{2,3},{3,4},{4,5},{5,6},{6,7},{7,8},{8,9},{9,10},{10,1... | collective-permute-start | bytes 73736 | tf_op jit(solution)/shard_map/ppermute | solution.py:61
  39.8 6.9 %collective-permute-start.4 = (bf16[6,4,1,512]{3,2,1,0:T(2,128)(2,1)S(1)}, bf16[6,4,1,512]{3,2,1,0:T(2,128)(2,1)}, u32[]{:S(2)}, u32[]{:S(2)}) collective-permute-start(bf16[6,4,1,512]{3,2,1,0:T(2,128)(2,1)S(1)} %pad_maximum_fusion.4), channel_id=1, source_target_pairs={{1,0},{2,1},{3,2},{4,3},{5,4},{6,5},{7,6},{8,7},{9,8},{10,9},{11,1... | collective-permute-start | bytes 73736 | tf_op jit(solution)/shard_map/ppermute | solution.py:62
  49.1 11.9 %copy-start.4 = (bf16[512,768]{1,0:T(8,128)(2,1)S(1)}, bf16[512,768]{1,0:T(8,128)(2,1)}, u32[]{:S(2)}) copy-start(bf16[512,768]{1,0:T(8,128)(2,1)} %copy-done.3) | copy-start | bytes 2359300
  60.9 5.4 %collective-permute-start.6 = (bf16[512,1536]{1,0:T(8,128)(2,1)}, bf16[512,1536]{1,0:T(8,128)(2,1)S(1)}, u32[]{:S(2)}, u32[]{:S(2)}) collective-permute-start(bf16[512,1536]{1,0:T(8,128)(2,1)} %get-tuple-element.31), channel_id=1, source_target_pairs={{0,1},{1,0},{2,3},{3,2},{4,5},{5,4},{6,7},{7,6},{8,9},{9,8},{10,11... | collective-permute-start | bytes 4718600 | tf_op jit(solution)/shard_map/ppermute | solution.py:67
  61.0 5.1 %collective-permute-start.5 = (bf16[512,768]{1,0:T(8,128)(2,1)S(1)}, bf16[512,768]{1,0:T(8,128)(2,1)S(1)}, u32[]{:S(2)}, u32[]{:S(2)}) collective-permute-start(bf16[512,768]{1,0:T(8,128)(2,1)S(1)} %copy-done.4), channel_id=1, source_target_pairs={{0,1},{1,0},{2,3},{3,2},{4,5},{5,4},{6,7},{7,6},{8,9},{9,8},{10,11... | collective-permute-start | bytes 2359304 | tf_op jit(solution)/shard_map/ppermute | solution.py:67
  99.9 51.8 %copy-start.8 = (f32[3,4,9,256]{3,1,2,0:T(4,128)S(1)}, f32[3,4,9,256]{3,1,2,0:T(4,128)}, u32[]{:S(2)}) copy-start(f32[3,4,9,256]{3,1,2,0:T(4,128)} %maximum_select_fusion.1) | copy-start | bytes 331780
  122.2 11.5 %all-to-all-start.3 = ((f32[16,1,1]{2,1,0:T(1,128)}), f32[16,1,1]{2,1,0:T(1,128)S(1)}, u32[]{:S(2)}, u32[]{:S(2)}) async-start(f32[16,1,1]{2,1,0:T(1,128)} %broadcast_in_dim.14), calls=%async_computation.3 | async-start | bytes 16384 | tf_op jit(solution)/shard_map/all_to_all | solution.py:267
  135.5 14.8 %all-to-all-start.4 = ((f32[16,1,1]{2,1,0:T(1,128)}), f32[16,1,1]{2,1,0:T(1,128)S(1)}, u32[]{:S(2)}, u32[]{:S(2)}) async-start(f32[16,1,1]{2,1,0:T(1,128)} %broadcast_in_dim.15), calls=%async_computation.4 | async-start | bytes 16384 | tf_op jit(solution)/shard_map/all_to_all | solution.py:267
  152.7 15.9 %all-to-all-start.5 = ((bf16[16,4,2304]{2,1,0:T(4,128)(2,1)}), bf16[16,4,2304]{2,1,0:T(4,128)(2,1)S(1)}, u32[]{:S(2)}, u32[]{:S(2)}) async-start(bf16[16,4,2304]{2,1,0:T(4,128)(2,1)} %broadcast_in_dim.32), calls=%async_computation.5 | async-start | bytes 589824 | tf_op jit(solution)/shard_map/all_to_all | solution.py:267
  170.3 32.6 %all-to-all-start.6 = ((bf16[8,64,2304]{2,1,0:T(8,128)(2,1)}), bf16[8,64,2304]{2,1,0:T(8,128)(2,1)S(1)}, u32[]{:S(2)}, u32[]{:S(2)}) async-start(bf16[8,64,2304]{2,1,0:T(8,128)(2,1)} %broadcast_in_dim.33), calls=%async_computation.6 | async-start | bytes 4718592 | tf_op jit(solution)/shard_map/all_to_all | solution.py:267
  202.8 15.7 %copy-start.5 = (bf16[8,64,2304]{2,1,0:T(8,128)(2,1)}, bf16[8,64,2304]{2,1,0:T(8,128)(2,1)S(1)}, u32[]{:S(2)}) copy-start(bf16[8,64,2304]{2,1,0:T(8,128)(2,1)S(1)} %all-to-all-done.6) | copy-start | bytes 7077892
  202.8 18.7 %collective-permute-start.7 = (bf16[512,2304]{1,0:T(8,128)(2,1)S(1)}, bf16[512,2304]{1,0:T(8,128)(2,1)}, u32[]{:S(2)}, u32[]{:S(2)}) collective-permute-start(bf16[512,2304]{1,0:T(8,128)(2,1)S(1)} %bitcast.56), channel_id=1, source_target_pairs={{0,1},{1,0},{2,3},{3,2},{4,5},{5,4},{6,7},{7,6},{8,9},{9,8},{10,11... | collective-permute-start | bytes 7077896 | tf_op jit(solution)/shard_map/ppermute | solution.py:67
  204.9 15.8 %collective-permute-start.8 = (f32[4,2,9,256]{3,1,2,0:T(2,128)S(1)}, f32[4,2,9,256]{3,1,2,0:T(2,128)S(1)}, u32[]{:S(2)}, u32[]{:S(2)}) collective-permute-start(f32[4,2,9,256]{3,1,2,0:T(2,128)S(1)} %get-tuple-element.54), channel_id=1, source_target_pairs={{0,1},{1,0},{2,3},{3,2},{4,5},{5,4},{6,7},{7,6},{8,9},{9,8},{10,11... | collective-permute-start | bytes 221192 | tf_op jit(solution)/shard_map/ppermute | solution.py:67
  (5 other events, 21.7 us)
Sparse Core Ops, SparseCore 0:
  34.3 45.8 all-gather.1
where the time goes:
time: 240 us; the launch traced here: 236 us
  waiting for transfers between devices  55.5 us (23%)
  blocking collectives  52.8 us (22%)
  starting transfers between devices  44.4 us (18%)
  Pallas kernels  37.5 us (16%)
  local copies, waits for them, and re-layouts  22.5 us (9%)
  between operations  15.2 us (6%)
  other arithmetic  7.79 us (3%)
    all_to_all x5, waiting for transfers between devices, to_all(): return lax.all_to_all(copies, axes, 0, 0, tiled=True)  50.8 us
    all_to_all x1, blocking collectives, per_device(): parts = lax.all_to_all(pair_sum, LAT, 0, 0, tiled=True)  32.7 us
    all_to_all x5, starting transfers between devices, to_all(): return lax.all_to_all(copies, axes, 0, 0, tiled=True)  31.2 us
    all_to_all x1, blocking collectives, per_device(): parts = lax.all_to_all(lat_sum, ('z', 'xh'), 0, 0, tiled=True)  20.1 us
    pallas_call x1, Pallas kernels, pulled(): pl.pallas_call(lambda *refs: pull_kernel(*refs, block=block), grid=(4,),...  13.5 us
    pallas_call x1, Pallas kernels, side_grads(): pl.pallas_call(lambda *refs: side_kernel(*refs, cols=cols, padded_cols=pa...  11.9 us
    pallas_call x1, Pallas kernels, joined(): pl.pallas_call(join_kernel, grid=(TAPS,), in_specs=[pl.BlockSpec(memory_s...  7.3 us
    unnamed x31, local copies, waits for them, and re-layouts  6.19 us
  transfers between devices with their start and end apart: 15, of which 5 were waited for; matrix products, arithmetic and copies ran while one was open for 9% of the time, Pallas kernels for 13%

commit v1 on v0

--- a/solution.py
+++ b/solution.py
@@ -10,6 +10,7 @@
 
 
 TAPS = 9
+ORDER = (1, 4, 7, 0, 2, 3, 5, 6, 8)
 ALL = ("xl", "y", "z", "xh", "c")
 LAT = ("xl", "y")
 LON = ("z", "xh", "c")
@@ -40,6 +41,11 @@
     return channel_of(core, plane, z, k)
 
 
+def row_channel(p):
+    plane, z, rest = p // 32, (p // 4) % 8, p % 4
+    return channel_of(rest // 2, plane, z, rest % 2)
+
+
 def neighbours(count, circular):
     forward = [(i, i + 1) for i in range(count - 1)]
     if circular:
@@ -47,20 +53,16 @@
     return forward, [(b, a) for a, b in forward]
 
 
-def row_halo(rows):
+def row_halo(first, last):
     forward, backward = neighbours(8, False)
-    above = lax.ppermute(rows[-1:], LAT, forward)
-    below = lax.ppermute(rows[:1], LAT, backward)
-    return above, below
-
-
-def col_halo(above, rows, below):
-    east = jnp.concatenate([part[:, :, -1:] for part in (above, rows, below)], axis=0)
-    west = jnp.concatenate([part[:, :, :1] for part in (above, rows, below)], axis=0)
+    return lax.ppermute(last, LAT, forward), lax.ppermute(first, LAT, backward)
+
+
+def col_halo(parts, last_col):
+    east = jnp.concatenate([part[:, :, last_col : last_col + 1] for part in parts], axis=0)
+    west = jnp.concatenate([part[:, :, :1] for part in parts], axis=0)
     forward, backward = neighbours(32, True)
-    left = lax.ppermute(east, LON, forward)
-    right = lax.ppermute(west, LON, backward)
-    return left, right
+    return lax.ppermute(east, LON, forward), lax.ppermute(west, LON, backward)
 
 
 def swap(array):
@@ -152,10 +154,10 @@
             field_ref[1, first : first + padded_cols, :] = centre
             wide = centre.astype(F32)
             east = pltpu.roll(wide, padded_cols - 1, 0)
-            east = jnp.where(index == cols - 1, right_ref[line : line + 1, :], east)
+            east = jnp.where(index == cols - 1, right_ref[line // batch, line % batch].astype(F32), east)
             field_ref[0, first : first + padded_cols, :] = east.astype(BF16)
             west = pltpu.roll(wide, 1, 0)
-            west = jnp.where(index == 0, left_ref[line : line + 1, :], west)
+            west = jnp.where(index == 0, left_ref[line // batch, line % batch].astype(F32), west)
             field_ref[2, first : first + padded_cols, :] = west.astype(BF16)
 
     row, side = step // 2, 2 * (step % 2)
@@ -237,29 +239,66 @@
     )(fields, weights, order)
 
 
-def join_kernel(core_ref, own_ref, other_ref, out_ref):
-    half = own_ref.shape[1]
+def adam_kernel(sums_ref, grad_ref, master_ref, one_ref, two_ref, out_ref, *, max_norm):
+    clip = clip_factor(jnp.sum(sums_ref[...], keepdims=True), max_norm)
+    state = adam(clip, grad_ref[...], master_ref[...], one_ref[...], two_ref[...])
+    out_ref[...] = state[0].astype(BF16)
+
+
+def clip_factor(square_sum, max_norm):
+    return jnp.minimum(1.0, max_norm / (jnp.sqrt(square_sum) + norm_eps))
+
+
+def adam(clip, grad, master, moment_one, moment_two):
+    clipped = clip * grad
+    new_one = beta_one * moment_one + (1.0 - beta_one) * clipped
+    new_two = beta_two * moment_two + (1.0 - beta_two) * clipped * clipped
+    first_hat = new_one / (1.0 - beta_one**step_count)
+    second_hat = new_two / (1.0 - beta_two**step_count)
+    new_master = master - learn_rate * (
+        first_hat / (jnp.sqrt(second_hat) + adam_eps) + decay_rate * master
+    )
+    return new_master, new_one, new_two, clipped
+
+
+def stepped(sums, grad, state, max_norm):
+    return pl.pallas_call(
+        lambda *refs: adam_kernel(*refs, max_norm=max_norm),
+        out_shape=jax.ShapeDtypeStruct(grad.shape, BF16),
+        cost_estimate=pl.CostEstimate(
+            flops=20 * grad.size, bytes_accessed=18 * grad.size, transcendentals=0
+        ),
+        name="stepped",
+    )(sums, grad, *state)
+
+
+def join_kernel(core_ref, order_ref, own_ref, other_ref, out_ref):
+    half = own_ref.shape[1] // TAPS
     own = pl.multiple_of(core_ref[0] * half, half)
     other = pl.multiple_of((1 - core_ref[0]) * half, half)
-    out_ref[0, :, pl.ds(own, half)] = own_ref[...]
-    out_ref[0, :, pl.ds(other, half)] = other_ref[...]
-
-
-def joined(core, own, other):
+    for lane, ref in ((own, own_ref), (other, other_ref)):
+        rows = jnp.dot(order_ref[...], ref[...], preferred_element_type=F32).astype(BF16)
+        for index, tap in enumerate(ORDER):
+            out_ref[tap, :, pl.ds(lane, half)] = rows[:, index * half : (index + 1) * half]
+
+
+def joined(core, order, own, other):
     chans, wide = own.shape
     half = wide // TAPS
+    block = order.shape[0]
     return pl.pallas_call(
         join_kernel,
-        grid=(TAPS,),
+        grid=(chans // block,),
         in_specs=[
             pl.BlockSpec(memory_space=pltpu.SMEM),
-            pl.BlockSpec((chans, half), lambda t: (0, t)),
-            pl.BlockSpec((chans, half), lambda t: (0, t)),
-        ],
-        out_specs=pl.BlockSpec((1, chans, 2 * half), lambda t: (t, 0, 0)),
+            pl.BlockSpec(order.shape, lambda i: (0, 0)),
+            pl.BlockSpec((block, wide), lambda i: (i, 0)),
+            pl.BlockSpec((block, wide), lambda i: (i, 0)),
+        ],
+        out_specs=pl.BlockSpec((TAPS, block, 2 * half), lambda i: (0, i, 0)),
         out_shape=jax.ShapeDtypeStruct((TAPS, chans, 2 * half), BF16),
         name="joined",
-    )(core, own, other)
+    )(core, order, own, other)
 
 
 def to_all(piece, axes, count):
@@ -284,35 +323,46 @@
 def per_device(activations, upstream, master, moment_one, moment_two):
     batch, lat_rows, lon_cols, chans = activations.shape
     outs = upstream.shape[3]
-    wide = TAPS * outs
     half = outs // 2
+    wide = TAPS * half
     padded_cols = -(-lon_cols // 32) * 32
     extra = padded_cols - lon_cols
     core = lax.axis_index("c")
     core_ref = core.reshape(1).astype(jnp.int32)
-
-    def padded(rows):
-        return jnp.pad(rows, ((0, 0), (0, 0), (0, extra), (0, 0))).reshape(-1, rows.shape[3])
-
-    up_rows = jnp.transpose(upstream, (1, 0, 2, 3))
-    above, below = row_halo(up_rows)
-
-    old_piece = master.astype(BF16).reshape(2, wide)
-    old_plane = to_all(old_piece, PLANE, 16).reshape(32, wide)
+    square = (chans, chans)
+
+    def padded(field):
+        return jnp.pad(
+            jnp.transpose(field, (1, 0, 2, 3)), ((0, 0), (0, 0), (0, extra), (0, 0))
+        )
+
+    def flat(rows):
+        return rows.reshape(-1, rows.shape[3])
+
+    above, below = row_halo(padded(upstream[:, :1]), padded(upstream[:, -1:]))
+    up_rows = padded(upstream)
+    order = (row_channel(rows_of(square, 0)) == rows_of(square, 1)).astype(BF16)
+    lhs = lax.dot_general(
+        order, flat(padded(activations)), (((1,), (1,)), ((), ())), preferred_element_type=F32
+    ).astype(BF16)
     state = jnp.stack([master, moment_one, moment_two])
     own_state, other_state = halves(state, core)
-    state = in_core_order(own_state, swap(other_state), core, 1)
-    above, below, old_plane, state = lax.optimization_barrier((above, below, old_plane, state))
+    other_state = swap(other_state)
+    state = in_core_order(own_state, other_state, core, 1)
+    state = jnp.stack([state[:, :, tap] for tap in ORDER], axis=2).reshape(12, wide)
+    lines = lax.all_gather(jnp.pad(state, ((0, 4), (0, 0))), ("z",), axis=0, tiled=True)
+
+    left, right = col_halo((above, up_rows, below), lon_cols - 1)
+    pieces = (flat(above), flat(up_rows), flat(below))
+    old_piece = master.astype(BF16).reshape(2, TAPS * outs)
+    old_plane = to_all(old_piece, PLANE, 16).reshape(32, TAPS * outs)
     old_weights = lax.all_gather(old_plane, ("z", "c"), axis=0, tiled=True)
-
-    left, right = col_halo(above, up_rows, below)
-    lhs = padded(jnp.transpose(activations, (1, 0, 2, 3))).T
-    pieces = (padded(above), padded(up_rows), padded(below))
     keep_one, send_one = centre_grads(core_ref, lhs, *pieces)
     swapped_one = swap(send_one)
     left, right, keep_one = lax.optimization_barrier((left, right, keep_one))
-    sides = [side.reshape(-1, outs).astype(F32) for side in (left, right)]
-    fields, keep_two, send_two = side_grads(core_ref, lhs, *pieces, *sides, lon_cols, padded_cols)
+    fields, keep_two, send_two = side_grads(
+        core_ref, lhs, *pieces, left, right, lon_cols, padded_cols
+    )
     swapped_two = swap(send_two)
     pair_sum = jnp.concatenate(
         [
@@ -320,46 +370,38 @@
             (keep_two + swapped_two.astype(F32)).astype(BF16),
         ],
         axis=1,
-    ).reshape(8, 64, TAPS * half)
-    parts = lax.all_to_all(pair_sum, LAT, 0, 0, tiled=True)
-    lat_sum = jnp.sum(parts.astype(F32), axis=0).astype(BF16).reshape(16, 4, TAPS * half)
-    parts = lax.all_to_all(lat_sum, ("z", "xh"), 0, 0, tiled=True)
-    grad = jnp.sum(parts.astype(F32), axis=0).reshape(4, TAPS, half)
-    square_sum = jnp.sum(grad * grad).reshape(1, 1)
-    centre, sides = grad[:, :3], grad[:, 3:].reshape(4, 3, 2, half)
-    grad = jnp.stack([sides[:, :, 0], centre, sides[:, :, 1]], axis=2).reshape(4, TAPS, half)
-
-    square_sum = jnp.sum(to_all(square_sum, PLANE, 16)).reshape(1, 1)
-    square_sum = jnp.sum(to_all(square_sum, ("z", "c"), 16))
+    ).reshape(16, 32, wide)
+    parts = lax.all_to_all(pair_sum, PLANE, 0, 0, tiled=True)
+    lines = lines.reshape(8, 4, 4, wide)
+    lines = [lines[:, i].reshape(32, wide) for i in range(3)]
+    plane_sum = jnp.sum(parts.astype(F32), axis=0).astype(BF16).reshape(8, 4, wide)
+    parts = lax.all_to_all(plane_sum, ("z",), 0, 0, tiled=True)
+    grad = jnp.sum(parts.astype(F32), axis=0)
+    grad_line = to_all(grad, ("z",), 8).reshape(32, wide)
+
+    square_sum = jnp.sum(grad_line * grad_line).reshape(1, 1)
+    sums = to_all(square_sum, PLANE + ("c",), 32).reshape(1, 32)
     max_norm = math.sqrt(float(chans * TAPS * outs))
-    clip_factor = jnp.minimum(1.0, max_norm / (jnp.sqrt(square_sum) + norm_eps))
-    clipped = clip_factor * grad
-    old_master, old_one, old_two = state
-    new_one = beta_one * old_one + (1.0 - beta_one) * clipped
-    new_two = beta_two * old_two + (1.0 - beta_two) * clipped * clipped
-    first_hat = new_one / (1.0 - beta_one**step_count)
-    second_hat = new_two / (1.0 - beta_two**step_count)
-    new_master = old_master - learn_rate * (
-        first_hat / (jnp.sqrt(second_hat) + adam_eps) + decay_rate * old_master
-    )
-
-    new_piece = new_master.astype(BF16).reshape(4, TAPS * half)
-    line = to_all(new_piece, ("z", "xh"), 16).reshape(64, TAPS * half)
-    line, fields, old_weights, results = lax.optimization_barrier(
-        (line, fields, old_weights, jnp.stack([new_master, new_one, new_two, clipped]))
-    )
-    own = to_all(line, LAT, 8).reshape(chans, TAPS * half)
+    new_line = stepped(sums, grad_line, lines, max_norm)
+    own = to_all(new_line, PLANE, 16).reshape(chans, wide)
+
+    clip = clip_factor(jnp.sum(sums).reshape(1, 1), max_norm)
+    results = jnp.stack(adam(clip, grad, *state.reshape(3, 4, wide)))
+    results = results.reshape(4, 4, TAPS, half)
+    results = jnp.stack([results[:, :, ORDER.index(tap)] for tap in range(TAPS)], axis=2)
     mine = jnp.where(core == 0, results[:, :2], results[:, 2:])
     theirs = jnp.where(core == 0, results[:, 2:], results[:, :2])
     results = in_core_order(mine, swap(theirs), core, 3)
 
-    square = (chans, chans)
-    back = (gather_order(rows_of(square, 0)) == rows_of(square, 1)).astype(BF16)
-    pulled_rows = pulled(fields, old_weights, back)
+    fields, old_weights, _ = lax.optimization_barrier((fields, old_weights, new_line))
+    old_order = (gather_order(rows_of(square, 0)) == rows_of(square, 1)).astype(BF16)
+    pulled_rows = pulled(fields, old_weights, old_order)
     input_grad = pulled_rows.reshape(lat_rows, batch, padded_cols, chans)[:, :, :lon_cols]
     input_grad = jnp.transpose(input_grad, (1, 0, 2, 3))
 
-    new_weights = jnp.transpose(joined(core_ref, own, swap(own)), (1, 0, 2))
+    lat_block = (chans // 8, chans // 8)
+    back = (rows_of(lat_block, 0) == row_channel(rows_of(lat_block, 1))).astype(BF16)
+    new_weights = jnp.transpose(joined(core_ref, back, own, swap(own)), (1, 0, 2))
     return (input_grad, new_weights, *results)
 
 

time: 240 us -> 238 us (level)
  the two profiles are of different devices: /device:TPU:5 before, /device:TPU:1 now
where the time goes in v1:
time: 238 us
  waiting for transfers between devices  58.4 us (25%)
  blocking collectives  44.7 us (19%)
  starting transfers between devices  41.6 us (17%)
  Pallas kernels  40.3 us (17%)
  local copies, waits for them, and re-layouts  25.2 us (11%)
  between operations  15.4 us (6%)
  other arithmetic  7.98 us (3%)
  matrix products  4.01 us (2%)
    all_to_all x3, waiting for transfers between devices, to_all(): return lax.all_to_all(copies, axes, 0, 0, tiled=True)  48.1 us
    all_to_all x1, blocking collectives, per_device(): parts = lax.all_to_all(pair_sum, PLANE, 0, 0, tiled=True)  31.5 us
    all_to_all x3, starting transfers between devices, to_all(): return lax.all_to_all(copies, axes, 0, 0, tiled=True)  17.6 us
    pallas_call x1, Pallas kernels, pulled(): pl.pallas_call(lambda *refs: pull_kernel(*refs, block=block), grid=(4,),...  13.4 us
    all_to_all x1, blocking collectives, to_all(): return lax.all_to_all(copies, axes, 0, 0, tiled=True)  13.2 us
    pallas_call x1, Pallas kernels, side_grads(): pl.pallas_call(lambda *refs: side_kernel(*refs, cols=cols, padded_cols=pa...  11.9 us
    unnamed x30, local copies, waits for them, and re-layouts  11.1 us
    pallas_call x1, Pallas kernels, joined(): pl.pallas_call(join_kernel, grid=(chans // block,), in_specs=[pl.BlockSpe...  7.72 us
  transfers between devices with their start and end apart: 15, of which 6 were waited for; matrix products, arithmetic and copies ran while one was open for 14% of the time, Pallas kernels for 14%

profile of v1, /device:TPU:1, one launch (start us, length us, event | category | flops | bytes accessed | tf_op | source)
XLA Modules:
  0.0 237.5 jit_solution(6675314553335172223)
XLA Ops:
  7.2 1.7 copy.95
  9.1 4.0 %collective-permute-start = (bf16[1,4,96,512]{3,2,1,0:T(8,128)(2,1)S(1)}, bf16[1,4,96,512]{3,2,1,0:T(8,128)(2,1)S(1)}, u32[]{:S(2)}, u32[]{:S(2)}) collective-permute-start(bf16[1,4,96,512]{3,2,1,0:T(8,128)(2,1)S(1)} %pad.19), channel_id=1, source_target_pairs={{0,32},{32,64},{64,96},{96,128},{128,160},{160,192},{192,224},{1,3... | collective-permute-start | bytes 1179656 | tf_op jit(solution)/shard_map/ppermute | solution.py:58
  17.5 4.0 %convolution_convert_fusion.lhs_ref.refs_1_ = bf16[512,1536]{1,0:T(8,128)(2,1)} fusion(bf16[1536,512]{1,0:T(8,128)(2,1)S(1)} %bitcast.60, s32[512]{0:T(512)S(1)} %get-tuple-element.84, s32[512]{0:T(512)S(1)} %get-tuple-element.87, s32[512]{0:T(512)S(1)} %get-tuple-element.83, s32[512]{0:T(512)S(1)} %get-tuple-element.88, s32[512]{0:T(512)S(1)} %get-tuple-element.85, ...), kind=kOutput, calls=%fused_computation.1 | convolution fusion | flops 822083584 | bytes 3159552 | tf_op jit(solution)/shard_map/dot_general | solution.py:345
  24.9 4.5 %collective-permute-start.2 = (bf16[6,4,1,512]{3,2,1,0:T(2,128)(2,1)S(1)}, bf16[6,4,1,512]{3,2,1,0:T(2,128)(2,1)S(1)}, u32[]{:S(2)}, u32[]{:S(2)}) collective-permute-start(bf16[6,4,1,512]{3,2,1,0:T(2,128)(2,1)S(1)} %pad_maximum_fusion.2), channel_id=1, source_target_pairs={{0,1},{1,2},{2,3},{3,4},{4,5},{5,6},{6,7},{7,8},{8,9},{9,10},{10,1... | collective-permute-start | bytes 73736 | tf_op jit(solution)/shard_map/ppermute | solution.py:65
  31.0 4.9 %centre_grads.1 = (f32[512,768]{1,0:T(8,128)S(1)}, bf16[512,768]{1,0:T(8,128)(2,1)S(1)}) custom-call(s32[1]{0:T(128)} %bitcast.core_ref.refs_0_, bf16[512,1536]{1,0:T(8,128)(2,1)S(1)} %copy-done.2, bf16[384,512]{1,0:T(8,128)(2,1)S(1)} %bitcast.46, bf16[1536,512]{1,0:T(8,128)(2,1)} %bitcast.58, bf16[384,512]{1,0:T(8,128)(2,1)S(1)} %bitcast.48), custom_call_target="tpu_custom_call" | custom-call | flops 2415919104 | bytes 8000000 | tf_op jit(solution)/shard_map/centre_grads/pallas_call | solution.py:111
  36.5 11.9 %side_grads.1 = (bf16[3,2304,512]{2,1,0:T(8,128)(2,1)}, f32[512,1536]{1,0:T(8,128)}, bf16[512,1536]{1,0:T(8,128)(2,1)}) custom-call(s32[1]{0:T(128)} %bitcast.core_ref.refs_0_, bf16[512,1536]{1,0:T(8,128)(2,1)} %convolution_convert_fusion.lhs_ref.refs_1_, bf16[384,512]{1,0:T(8,128)(2,1)} %bitcast.47, bf16[1536,512]{1,0:T(8,128)(2,1)} %bitcast.59, ...), custom_call_target="tpu_custom_call" | custom-call | flops 4831838208 | bytes 16000000 | tf_op jit(solution)/shard_map/side_grads/pallas_call | solution.py:181
  48.4 4.0 %collective-permute-start.5 = (bf16[512,1536]{1,0:T(8,128)(2,1)}, bf16[512,1536]{1,0:T(8,128)(2,1)}, u32[]{:S(2)}, u32[]{:S(2)}) collective-permute-start(bf16[512,1536]{1,0:T(8,128)(2,1)} %get-tuple-element.23), channel_id=1, source_target_pairs={{0,1},{1,0},{2,3},{3,2},{4,5},{5,4},{6,7},{7,6},{8,9},{9,8},{10,11... | collective-permute-start | bytes 4718600 | tf_op jit(solution)/shard_map/ppermute | solution.py:69
  52.6 13.2 %all_to_all.30 = bf16[16,2,4608]{2,1,0:T(2,128)(2,1)S(1)} all-to-all(bf16[16,2,4608]{2,1,0:T(2,128)(2,1)S(1)} %broadcast_in_dim.11), channel_id=1, replica_groups=mesh['xl'=2,'y'=4,'z'=8,'xh'=2,'c'=2] {'xl','y','xh'}, dimensions={0} | all-to-all | bytes 589824 | tf_op jit(solution)/shard_map/all_to_all | solution.py:306
  68.8 2.0 add_convert_fusion
  70.9 31.5 %all_to_all.31 = bf16[16,32,2304]{2,1,0:T(8,128)(2,1)S(1)} all-to-all(bf16[16,32,2304]{2,1,0:T(8,128)(2,1)S(1)} %bitcast.52), channel_id=1, replica_groups=mesh['xl'=2,'y'=4,'z'=8,'xh'=2,'c'=2] {'xl','y','xh'}, dimensions={0} | all-to-all | bytes 4718592 | tf_op jit(solution)/shard_map/all_to_all | solution.py:374
  103.5 7.3 %all-to-all-start.2 = ((bf16[8,4,2304]{2,1,0:T(4,128)(2,1)}), bf16[8,4,2304]{2,1,0:T(4,128)(2,1)S(1)}, u32[]{:S(2)}, u32[]{:S(2)}) async-start(bf16[8,4,2304]{2,1,0:T(4,128)(2,1)} %reshape.126), calls=%async_computation.2 | async-start | bytes 294912 | tf_op jit(solution)/shard_map/all_to_all | solution.py:378
  112.4 6.4 %all-to-all-done.2 = bf16[8,4,2304]{2,1,0:T(4,128)(2,1)S(1)} async-done(((bf16[8,4,2304]{2,1,0:T(4,128)(2,1)}), bf16[8,4,2304]{2,1,0:T(4,128)(2,1)S(1)}, u32[]{:S(2)}, u32[]{:S(2)}) %all-to-all-start.2) | async-done | bytes 147488 | tf_op jit(solution)/shard_map/all_to_all | solution.py:378
  119.7 3.4 %all-to-all-start.3 = ((f32[8,4,2304]{2,1,0:T(4,128)}), f32[8,4,2304]{2,1,0:T(4,128)S(1)}, u32[]{:S(2)}, u32[]{:S(2)}) async-start(f32[8,4,2304]{2,1,0:T(4,128)} %broadcast_in_dim.12), calls=%async_computation.3 | async-start | bytes 589824 | tf_op jit(solution)/shard_map/all_to_all | solution.py:306
  124.9 7.9 %all-to-all-done.3 = f32[8,4,2304]{2,1,0:T(4,128)S(1)} async-done(((f32[8,4,2304]{2,1,0:T(4,128)}), f32[8,4,2304]{2,1,0:T(4,128)S(1)}, u32[]{:S(2)}, u32[]{:S(2)}) %all-to-all-start.3) | async-done | bytes 294944 | tf_op jit(solution)/shard_map/all_to_all | solution.py:306
  134.7 10.5 %all-to-all-start.4 = ((f32[32,1,1]{2,1,0:T(1,128)}), f32[32,1,1]{2,1,0:T(1,128)S(1)}, u32[]{:S(2)}, u32[]{:S(2)}) async-start(f32[32,1,1]{2,1,0:T(1,128)} %broadcast_in_dim.13), calls=%async_computation.4 | async-start | bytes 32768 | tf_op jit(solution)/shard_map/all_to_all | solution.py:306
  146.9 5.2 %all-to-all-done.4 = f32[32,1,1]{2,1,0:T(1,128)S(1)} async-done(((f32[32,1,1]{2,1,0:T(1,128)}), f32[32,1,1]{2,1,0:T(1,128)S(1)}, u32[]{:S(2)}, u32[]{:S(2)}) %all-to-all-start.4) | async-done | bytes 160 | tf_op jit(solution)/shard_map/all_to_all | solution.py:306
  152.9 2.4 %stepped.1 = bf16[32,2304]{1,0:T(8,128)(2,1)} custom-call(f32[1,32]{1,0:T(1,128)} %bitcast.66, f32[32,2304]{1,0:T(8,128)} %reshape.128.refs_1_, f32[32,2304]{1,0:T(8,128)} %reshape_squeeze.9.refs_2_, f32[32,2304]{1,0:T(8,128)} %reshape_squeeze.10.refs_3_, f32[32,2304]{1,0:T(8,128)} %reshape_squeeze.11.refs_4_), custom_call_target="tpu_custom_call" | custom-call | flops 1474560 | bytes 1327104 | tf_op jit(solution)/shard_map/stepped/pallas_call | solution.py:265
  155.4 2.5 %broadcast_in_dim.28 = bf16[16,32,2304]{2,1,0:T(8,128)(2,1)} broadcast(bf16[32,2304]{1,0:T(8,128)(2,1)} %stepped.1), dimensions={1,2} | broadcast | bytes 2506752 | tf_op jit(solution)/shard_map/broadcast_in_dim | solution.py:305
  157.9 3.7 %all-to-all-start.5 = ((bf16[16,32,2304]{2,1,0:T(8,128)(2,1)}), bf16[16,32,2304]{2,1,0:T(8,128)(2,1)S(1)}, u32[]{:S(2)}, u32[]{:S(2)}) async-start(bf16[16,32,2304]{2,1,0:T(8,128)(2,1)} %broadcast_in_dim.28), calls=%async_computation.5 | async-start | bytes 4718592 | tf_op jit(solution)/shard_map/all_to_all | solution.py:306
  163.7 35.0 %all-to-all-done.5 = bf16[16,32,2304]{2,1,0:T(8,128)(2,1)S(1)} async-done(((bf16[16,32,2304]{2,1,0:T(8,128)(2,1)}), bf16[16,32,2304]{2,1,0:T(8,128)(2,1)S(1)}, u32[]{:S(2)}, u32[]{:S(2)}) %all-to-all-start.5) | async-done | bytes 2359328 | tf_op jit(solution)/shard_map/all_to_all | solution.py:306
  201.4 3.2 %collective-permute-done.8 = f32[4,2,9,256]{3,2,1,0:T(8,128)S(1)} collective-permute-done((f32[4,2,9,256]{3,2,1,0:T(8,128)S(1)}, f32[4,2,9,256]{3,2,1,0:T(8,128)S(1)}, u32[]{:S(2)}, u32[]{:S(2)}) %collective-permute-start.8) | collective-permute-done | bytes 73760 | tf_op jit(solution)/shard_map/ppermute | solution.py:69
  207.2 13.4 %pulled.1 = bf16[1536,512]{1,0:T(8,128)(2,1)S(1)} custom-call(bf16[3,2304,512]{2,1,0:T(8,128)(2,1)} %get-tuple-element.24.refs_0_, bf16[512,4608]{1,0:T(8,128)(2,1)} %all-gather.3.cloned.1.call-done.refs_1_, bf16[512,512]{1,0:T(8,128)(2,1)S(1)} %fusion.36.refs_2_), custom_call_target="tpu_custom_call" | custom-call | flops 7247757312 | bytes 14000000 | tf_op jit(solution)/shard_map/pulled/pallas_call | solution.py:222
  220.7 2.3 copy.93
  222.9 7.7 %joined.1 = bf16[9,512,512]{2,1,0:T(8,128)(2,1)} custom-call(s32[1]{0:T(128)} %bitcast.core_ref.refs_0_, bf16[64,64]{1,0:T(8,128)(2,1)} %fusion.74.order_ref, bf16[512,2304]{1,0:T(8,128)(2,1)} %bitcast.54, bf16[512,2304]{1,0:T(8,128)(2,1)} %collective-permute-done.7.other_ref), custom_call_target="tpu_custom_call" | custom-call | tf_op jit(solution)/shard_map/joined/pallas_call | solution.py:289
  (111 shorter events, 29.5 us)
Async XLA Ops:
  7.2 103.6 %all-gather.5.cloned.1.call-start = ((), (), s32[]{:S(2)}) async-start(), calls=%async_computation.7 | async-start | bytes 1327104 | tf_op jit(solution)/shard_map/all_gather | solution.py:353
  8.9 5.5 %copy-start.5 = (f32[2,9,512]{2,0,1:T(2,128)S(1)}, f32[2,9,512]{2,0,1:T(2,128)}, u32[]{:S(2)}) copy-start(f32[2,9,512]{2,0,1:T(2,128)} %param.7) | copy-start | bytes 110596
  8.9 5.6 %copy-start.6 = (f32[2,9,512]{2,0,1:T(2,128)S(1)}, f32[2,9,512]{2,0,1:T(2,128)}, u32[]{:S(2)}) copy-start(f32[2,9,512]{2,0,1:T(2,128)} %param.9) | copy-start | bytes 110596
  8.9 5.6 %copy-start.7 = (f32[2,9,512]{2,0,1:T(2,128)S(1)}, f32[2,9,512]{2,0,1:T(2,128)}, u32[]{:S(2)}) copy-start(f32[2,9,512]{2,0,1:T(2,128)} %param.8) | copy-start | bytes 110596
  9.1 15.0 %collective-permute-start = (bf16[1,4,96,512]{3,2,1,0:T(8,128)(2,1)S(1)}, bf16[1,4,96,512]{3,2,1,0:T(8,128)(2,1)S(1)}, u32[]{:S(2)}, u32[]{:S(2)}) collective-permute-start(bf16[1,4,96,512]{3,2,1,0:T(8,128)(2,1)S(1)} %pad.19), channel_id=1, source_target_pairs={{0,32},{32,64},{64,96},{96,128},{128,160},{160,192},{192,224},{1,3... | collective-permute-start | bytes 1179656 | tf_op jit(solution)/shard_map/ppermute | solution.py:58
  13.2 11.6 %collective-permute-start.1 = (bf16[1,4,96,512]{3,2,1,0:T(8,128)(2,1)S(1)}, bf16[1,4,96,512]{3,2,1,0:T(8,128)(2,1)S(1)}, u32[]{:S(2)}, u32[]{:S(2)}) collective-permute-start(bf16[1,4,96,512]{3,2,1,0:T(8,128)(2,1)S(1)} %pad.21), channel_id=1, source_target_pairs={{32,0},{64,32},{96,64},{128,96},{160,128},{192,160},{224,192},{33,... | collective-permute-start | bytes 1179656 | tf_op jit(solution)/shard_map/ppermute | solution.py:58
  14.6 8.4 %collective-permute-start.6 = (f32[3,2,9,256]{3,2,1,0:T(8,128)S(1)}, f32[3,2,9,256]{3,2,1,0:T(8,128)S(1)}, u32[]{:S(2)}, u32[]{:S(2)}) collective-permute-start(f32[3,2,9,256]{3,2,1,0:T(8,128)S(1)} %get-tuple-element.82), channel_id=1, source_target_pairs={{0,1},{1,0},{2,3},{3,2},{4,5},{5,4},{6,7},{7,6},{8,9},{9,8},{10,11... | collective-permute-start | bytes 165896 | tf_op jit(solution)/shard_map/ppermute | solution.py:69
  24.0 183.2 %all-gather.3.cloned.1.call-start = ((), (), s32[]{:S(2)}) async-start(), calls=%async_computation.6 | async-start | bytes 5013504 | tf_op jit(solution)/shard_map/all_gather | solution.py:359
  24.1 11.7 %copy-start = (bf16[1,4,96,512]{3,2,1,0:T(8,128)(2,1)}, bf16[1,4,96,512]{3,2,1,0:T(8,128)(2,1)S(1)}, u32[]{:S(2)}) copy-start(bf16[1,4,96,512]{3,2,1,0:T(8,128)(2,1)S(1)} %collective-permute-done) | copy-start | bytes 1179652
  24.8 11.1 %copy-start.1 = (bf16[1,4,96,512]{3,2,1,0:T(8,128)(2,1)}, bf16[1,4,96,512]{3,2,1,0:T(8,128)(2,1)S(1)}, u32[]{:S(2)}) copy-start(bf16[1,4,96,512]{3,2,1,0:T(8,128)(2,1)S(1)} %collective-permute-done.1) | copy-start | bytes 1179652
  24.9 11.0 %collective-permute-start.2 = (bf16[6,4,1,512]{3,2,1,0:T(2,128)(2,1)S(1)}, bf16[6,4,1,512]{3,2,1,0:T(2,128)(2,1)S(1)}, u32[]{:S(2)}, u32[]{:S(2)}) collective-permute-start(bf16[6,4,1,512]{3,2,1,0:T(2,128)(2,1)S(1)} %pad_maximum_fusion.2), channel_id=1, source_target_pairs={{0,1},{1,2},{2,3},{3,4},{4,5},{5,6},{6,7},{7,8},{8,9},{9,10},{10,1... | collective-permute-start | bytes 73736 | tf_op jit(solution)/shard_map/ppermute | solution.py:65
  29.5 6.4 %collective-permute-start.3 = (bf16[6,4,1,512]{3,2,1,0:T(2,128)(2,1)S(1)}, bf16[6,4,1,512]{3,2,1,0:T(2,128)(2,1)S(1)}, u32[]{:S(2)}, u32[]{:S(2)}) collective-permute-start(bf16[6,4,1,512]{3,2,1,0:T(2,128)(2,1)S(1)} %pad_maximum_fusion.3), channel_id=1, source_target_pairs={{1,0},{2,1},{3,2},{4,3},{5,4},{6,5},{7,6},{8,7},{9,8},{10,9},{11,1... | collective-permute-start | bytes 73736 | tf_op jit(solution)/shard_map/ppermute | solution.py:65
  29.6 1.4 copy-start.2
  35.9 0.6 copy-start.9
  48.4 19.7 %collective-permute-start.5 = (bf16[512,1536]{1,0:T(8,128)(2,1)}, bf16[512,1536]{1,0:T(8,128)(2,1)}, u32[]{:S(2)}, u32[]{:S(2)}) collective-permute-start(bf16[512,1536]{1,0:T(8,128)(2,1)} %get-tuple-element.23), channel_id=1, source_target_pairs={{0,1},{1,0},{2,3},{3,2},{4,5},{5,4},{6,7},{7,6},{8,9},{9,8},{10,11... | collective-permute-start | bytes 4718600 | tf_op jit(solution)/shard_map/ppermute | solution.py:69
  52.4 14.3 %collective-permute-start.4 = (bf16[512,768]{1,0:T(8,128)(2,1)S(1)}, bf16[512,768]{1,0:T(8,128)(2,1)}, u32[]{:S(2)}, u32[]{:S(2)}) collective-permute-start(bf16[512,768]{1,0:T(8,128)(2,1)S(1)} %get-tuple-element.21), channel_id=1, source_target_pairs={{0,1},{1,0},{2,3},{3,2},{4,5},{5,4},{6,7},{7,6},{8,9},{9,8},{10,11... | collective-permute-start | bytes 2359304 | tf_op jit(solution)/shard_map/ppermute | solution.py:69
  66.6 2.1 copy-start.4
  103.5 15.4 %all-to-all-start.2 = ((bf16[8,4,2304]{2,1,0:T(4,128)(2,1)}), bf16[8,4,2304]{2,1,0:T(4,128)(2,1)S(1)}, u32[]{:S(2)}, u32[]{:S(2)}) async-start(bf16[8,4,2304]{2,1,0:T(4,128)(2,1)} %reshape.126), calls=%async_computation.2 | async-start | bytes 294912 | tf_op jit(solution)/shard_map/all_to_all | solution.py:378
  119.7 13.0 %all-to-all-start.3 = ((f32[8,4,2304]{2,1,0:T(4,128)}), f32[8,4,2304]{2,1,0:T(4,128)S(1)}, u32[]{:S(2)}, u32[]{:S(2)}) async-start(f32[8,4,2304]{2,1,0:T(4,128)} %broadcast_in_dim.12), calls=%async_computation.3 | async-start | bytes 589824 | tf_op jit(solution)/shard_map/all_to_all | solution.py:306
  134.7 17.4 %all-to-all-start.4 = ((f32[32,1,1]{2,1,0:T(1,128)}), f32[32,1,1]{2,1,0:T(1,128)S(1)}, u32[]{:S(2)}, u32[]{:S(2)}) async-start(f32[32,1,1]{2,1,0:T(1,128)} %broadcast_in_dim.13), calls=%async_computation.4 | async-start | bytes 32768 | tf_op jit(solution)/shard_map/all_to_all | solution.py:306
  157.9 40.8 %all-to-all-start.5 = ((bf16[16,32,2304]{2,1,0:T(8,128)(2,1)}), bf16[16,32,2304]{2,1,0:T(8,128)(2,1)S(1)}, u32[]{:S(2)}, u32[]{:S(2)}) async-start(bf16[16,32,2304]{2,1,0:T(8,128)(2,1)} %broadcast_in_dim.28), calls=%async_computation.5 | async-start | bytes 4718592 | tf_op jit(solution)/shard_map/all_to_all | solution.py:306
  198.7 5.9 %copy-start.3 = (bf16[16,32,2304]{2,1,0:T(8,128)(2,1)}, bf16[16,32,2304]{2,1,0:T(8,128)(2,1)S(1)}, u32[]{:S(2)}) copy-start(bf16[16,32,2304]{2,1,0:T(8,128)(2,1)S(1)} %all-to-all-done.5) | copy-start | bytes 7077892
  198.7 24.2 %collective-permute-start.7 = (bf16[512,2304]{1,0:T(8,128)(2,1)S(1)}, bf16[512,2304]{1,0:T(8,128)(2,1)}, u32[]{:S(2)}, u32[]{:S(2)}) collective-permute-start(bf16[512,2304]{1,0:T(8,128)(2,1)S(1)} %bitcast.53), channel_id=1, source_target_pairs={{0,1},{1,0},{2,3},{3,2},{4,5},{5,4},{6,7},{7,6},{8,9},{9,8},{10,11... | collective-permute-start | bytes 7077896 | tf_op jit(solution)/shard_map/ppermute | solution.py:69
  200.7 3.9 %collective-permute-start.8 = (f32[4,2,9,256]{3,2,1,0:T(8,128)S(1)}, f32[4,2,9,256]{3,2,1,0:T(8,128)S(1)}, u32[]{:S(2)}, u32[]{:S(2)}) collective-permute-start(f32[4,2,9,256]{3,2,1,0:T(8,128)S(1)} %get-tuple-element.67), channel_id=1, source_target_pairs={{0,1},{1,0},{2,3},{3,2},{4,5},{5,4},{6,7},{7,6},{8,9},{9,8},{10,11... | collective-permute-start | bytes 221192 | tf_op jit(solution)/shard_map/ppermute | solution.py:69
  (1 other events, 0.6 us)
Sparse Core Ops, SparseCore 0:
  24.2 37.3 all-gather.4
  66.7 42.9 all-gather.2

commit v2 on v1

--- a/solution.py
+++ b/solution.py
@@ -36,9 +36,10 @@
     return (((lat * 8 + z) * 2 + xh) * 2 + core) * 2 + k
 
 
-def gather_order(p):
-    z, core, plane, k = p // 64, (p // 32) % 2, (p // 2) % 16, p % 2
-    return channel_of(core, plane, z, k)
+def ring_channel(p, core, z):
+    arrival, plane, k = p // 32, (p // 2) % 16, p % 2
+    step = jnp.where(arrival <= 4, -arrival, arrival - 4)
+    return channel_of(core, plane, (z + step + 8) % 8, k)
 
 
 def row_channel(p):
@@ -198,51 +199,47 @@
     )(core, lhs, above, rows, below, left, right)
 
 
-def pull_kernel(field_ref, weight_ref, order_ref, out_ref, *, block):
+def pull_kernel(
+    field_ref, own_ref, other_ref, own_order_ref, other_order_ref, out_ref, *, block
+):
     step = pl.program_id(0)
     outs = field_ref.shape[2]
-    total = jnp.zeros((block, weight_ref.shape[0]), F32)
-    for tap in range(TAPS):
-        row, col = divmod(tap, 3)
-        start = pl.multiple_of((step + 2 - row) * block, block)
-        total = total + lax.dot_general(
-            field_ref[col, pl.ds(start, block), :],
-            weight_ref[:, tap * outs : (tap + 1) * outs],
-            (((1,), (1,)), ((), ())),
-            preferred_element_type=F32,
-        )
-    out_ref[...] = jnp.dot(
-        total.astype(BF16), order_ref[...], preferred_element_type=F32
-    ).astype(BF16)
-
-
-def pulled(fields, weights, order):
+    result = None
+    for weight_ref, order_ref in ((own_ref, own_order_ref), (other_ref, other_order_ref)):
+        total = jnp.zeros((block, weight_ref.shape[0]), F32)
+        for tap in range(TAPS):
+            row, col = divmod(tap, 3)
+            start = pl.multiple_of((step + 2 - row) * block, block)
+            total = total + lax.dot_general(
+                field_ref[col, pl.ds(start, block), :],
+                weight_ref[:, tap * outs : (tap + 1) * outs],
+                (((1,), (1,)), ((), ())),
+                preferred_element_type=F32,
+            )
+        part = jnp.dot(total.astype(BF16), order_ref[...], preferred_element_type=F32)
+        result = part if result is None else result + part
+    out_ref[...] = result.astype(BF16)
+
+
+def pulled(fields, own, other, own_order, other_order):
     block = fields.shape[1] // 6
-    chans = weights.shape[0]
+    chans = own_order.shape[1]
+    operands = (fields, own, other, own_order, other_order)
+    whole = lambda array: pl.BlockSpec(array.shape, lambda i: (0,) * array.ndim)
     return pl.pallas_call(
         lambda *refs: pull_kernel(*refs, block=block),
         grid=(4,),
-        in_specs=[
-            pl.BlockSpec(fields.shape, lambda i: (0, 0, 0)),
-            pl.BlockSpec(weights.shape, lambda i: (0, 0)),
-            pl.BlockSpec(order.shape, lambda i: (0, 0)),
-        ],
+        in_specs=[whole(array) for array in operands],
         out_specs=pl.BlockSpec((block, chans), lambda i: (i, 0)),
         out_shape=jax.ShapeDtypeStruct((4 * block, chans), BF16),
         compiler_params=pltpu.CompilerParams(vmem_limit_bytes=48 * 1024 * 1024),
         cost_estimate=pl.CostEstimate(
-            flops=2 * 4 * block * chans * weights.shape[1],
+            flops=2 * 4 * block * chans * own.shape[1],
             bytes_accessed=14_000_000,
             transcendentals=0,
         ),
         name="pulled",
-    )(fields, weights, order)
-
-
-def adam_kernel(sums_ref, grad_ref, master_ref, one_ref, two_ref, out_ref, *, max_norm):
-    clip = clip_factor(jnp.sum(sums_ref[...], keepdims=True), max_norm)
-    state = adam(clip, grad_ref[...], master_ref[...], one_ref[...], two_ref[...])
-    out_ref[...] = state[0].astype(BF16)
+    )(*operands)
 
 
 def clip_factor(square_sum, max_norm):
@@ -259,17 +256,6 @@
         first_hat / (jnp.sqrt(second_hat) + adam_eps) + decay_rate * master
     )
     return new_master, new_one, new_two, clipped
-
-
-def stepped(sums, grad, state, max_norm):
-    return pl.pallas_call(
-        lambda *refs: adam_kernel(*refs, max_norm=max_norm),
-        out_shape=jax.ShapeDtypeStruct(grad.shape, BF16),
-        cost_estimate=pl.CostEstimate(
-            flops=20 * grad.size, bytes_accessed=18 * grad.size, transcendentals=0
-        ),
-        name="stepped",
-    )(sums, grad, *state)
 
 
 def join_kernel(core_ref, order_ref, own_ref, other_ref, out_ref):
@@ -301,6 +287,18 @@
     )(core, order, own, other)
 
 
+def around_ring(chunk, after):
+    chunk, _ = lax.optimization_barrier((chunk, after))
+    up = [(i, (i + 1) % 8) for i in range(8)]
+    down = [(i, (i - 1) % 8) for i in range(8)]
+    below, above = [chunk], [chunk]
+    for _ in range(4):
+        below.append(lax.ppermute(below[-1], "z", up))
+    for _ in range(3):
+        above.append(lax.ppermute(above[-1], "z", down))
+    return jnp.concatenate(below + above[1:], axis=0)
+
+
 def to_all(piece, axes, count):
     copies = jnp.broadcast_to(piece[None], (count, *piece.shape))
     return lax.all_to_all(copies, axes, 0, 0, tiled=True)
@@ -350,13 +348,10 @@
     other_state = swap(other_state)
     state = in_core_order(own_state, other_state, core, 1)
     state = jnp.stack([state[:, :, tap] for tap in ORDER], axis=2).reshape(12, wide)
-    lines = lax.all_gather(jnp.pad(state, ((0, 4), (0, 0))), ("z",), axis=0, tiled=True)
-
     left, right = col_halo((above, up_rows, below), lon_cols - 1)
     pieces = (flat(above), flat(up_rows), flat(below))
     old_piece = master.astype(BF16).reshape(2, TAPS * outs)
     old_plane = to_all(old_piece, PLANE, 16).reshape(32, TAPS * outs)
-    old_weights = lax.all_gather(old_plane, ("z", "c"), axis=0, tiled=True)
     keep_one, send_one = centre_grads(core_ref, lhs, *pieces)
     swapped_one = swap(send_one)
     left, right, keep_one = lax.optimization_barrier((left, right, keep_one))
@@ -372,34 +367,38 @@
         axis=1,
     ).reshape(16, 32, wide)
     parts = lax.all_to_all(pair_sum, PLANE, 0, 0, tiled=True)
-    lines = lines.reshape(8, 4, 4, wide)
-    lines = [lines[:, i].reshape(32, wide) for i in range(3)]
+    old_own = around_ring(old_plane, pair_sum)
     plane_sum = jnp.sum(parts.astype(F32), axis=0).astype(BF16).reshape(8, 4, wide)
     parts = lax.all_to_all(plane_sum, ("z",), 0, 0, tiled=True)
     grad = jnp.sum(parts.astype(F32), axis=0)
-    grad_line = to_all(grad, ("z",), 8).reshape(32, wide)
-
-    square_sum = jnp.sum(grad_line * grad_line).reshape(1, 1)
-    sums = to_all(square_sum, PLANE + ("c",), 32).reshape(1, 32)
-    max_norm = math.sqrt(float(chans * TAPS * outs))
-    new_line = stepped(sums, grad_line, lines, max_norm)
+
+    square_sum = jnp.sum(to_all(jnp.sum(grad * grad).reshape(1, 1), ALL, 256)).reshape(1, 1)
+    clip = clip_factor(square_sum, math.sqrt(float(chans * TAPS * outs)))
+    results = jnp.stack(adam(clip, grad, *state.reshape(3, 4, wide)))
+    new_line = to_all(results[0].astype(BF16), ("z",), 8).reshape(32, wide)
     own = to_all(new_line, PLANE, 16).reshape(chans, wide)
 
-    clip = clip_factor(jnp.sum(sums).reshape(1, 1), max_norm)
-    results = jnp.stack(adam(clip, grad, *state.reshape(3, 4, wide)))
     results = results.reshape(4, 4, TAPS, half)
     results = jnp.stack([results[:, :, ORDER.index(tap)] for tap in range(TAPS)], axis=2)
     mine = jnp.where(core == 0, results[:, :2], results[:, 2:])
     theirs = jnp.where(core == 0, results[:, 2:], results[:, :2])
     results = in_core_order(mine, swap(theirs), core, 3)
 
-    fields, old_weights, _ = lax.optimization_barrier((fields, old_weights, new_line))
-    old_order = (gather_order(rows_of(square, 0)) == rows_of(square, 1)).astype(BF16)
-    pulled_rows = pulled(fields, old_weights, old_order)
-    input_grad = pulled_rows.reshape(lat_rows, batch, padded_cols, chans)[:, :, :lon_cols]
-    input_grad = jnp.transpose(input_grad, (1, 0, 2, 3))
-
-    lat_block = (chans // 8, chans // 8)
+    old_other = swap(old_own)
+    fields, old_own, old_other, _ = lax.optimization_barrier(
+        (fields, old_own, old_other, new_line)
+    )
+    z = lax.axis_index("z")
+    across = (chans // 2, chans)
+    old_orders = [
+        (ring_channel(rows_of(across, 0), which, z) == rows_of(across, 1)).astype(BF16)
+        for which in (core, 1 - core)
+    ]
+    pulled_rows = pulled(fields, old_own, old_other, *old_orders)
+    input_grad = pulled_rows.reshape(lat_rows, batch, padded_cols, chans)
+    input_grad = jnp.transpose(input_grad[:, :, :lon_cols], (1, 0, 2, 3))
+
+    lat_block = (chans // 4, chans // 4)
     back = (rows_of(lat_block, 0) == row_channel(rows_of(lat_block, 1))).astype(BF16)
     new_weights = jnp.transpose(joined(core_ref, back, own, swap(own)), (1, 0, 2))
     return (input_grad, new_weights, *results)

time: 238 us -> 223 us (0.937)
  the two profiles are of different devices: /device:TPU:1 before, /device:TPU:5 now
where the time goes in v2:
time: 223 us; the launch traced here: 222 us
  waiting for transfers between devices  83.5 us (37%)
  starting transfers between devices  66.6 us (30%)
  Pallas kernels  35.3 us (16%)
  local copies, waits for them, and re-layouts  20 us (9%)
  other arithmetic  10.4 us (5%)
  matrix products  3.98 us (2%)
    all_to_all x4, waiting for transfers between devices, to_all(): return lax.all_to_all(copies, axes, 0, 0, tiled=True)  47.3 us
    all_to_all x4, starting transfers between devices, to_all(): return lax.all_to_all(copies, axes, 0, 0, tiled=True)  27.2 us
    all_to_all x1, waiting for transfers between devices, per_device(): parts = lax.all_to_all(pair_sum, PLANE, 0, 0, tiled=True)  13.9 us
    pallas_call x1, Pallas kernels, pulled(): pl.pallas_call(lambda *refs: pull_kernel(*refs, block=block), grid=(4,),...  12.8 us
    ppermute x3, starting transfers between devices, around_ring(): above.append(lax.ppermute(above[-1], 'z', down))  11.9 us
    pallas_call x1, Pallas kernels, side_grads(): pl.pallas_call(lambda *refs: side_kernel(*refs, cols=cols, padded_cols=pa...  11.9 us
    unnamed x38, local copies, waits for them, and re-layouts  11.4 us
    ppermute x3, waiting for transfers between devices, around_ring(): above.append(lax.ppermute(above[-1], 'z', down))  7.87 us
  transfers between devices with their start and end apart: 23, of which 12 were waited for; matrix products, arithmetic and copies ran while one was open for 14% of the time, Pallas kernels for 8%

profile of v2, /device:TPU:5, one launch (start us, length us, event | category | flops | bytes accessed | tf_op | source)
XLA Modules:
  0.0 221.7 jit_solution(8439289766312206903)
XLA Ops:
  2.6 3.2 %collective-permute-start = (bf16[1,4,96,512]{3,2,1,0:T(8,128)(2,1)S(1)}, bf16[1,4,96,512]{3,2,1,0:T(8,128)(2,1)S(1)}, u32[]{:S(2)}, u32[]{:S(2)}) collective-permute-start(bf16[1,4,96,512]{3,2,1,0:T(8,128)(2,1)S(1)} %pad.15), channel_id=1, source_target_pairs={{0,32},{32,64},{64,96},{96,128},{128,160},{160,192},{192,224},{1,3... | collective-permute-start | bytes 1179656 | tf_op jit(solution)/shard_map/ppermute | solution.py:59
  7.7 4.0 %convolution_convert_fusion.lhs_ref.refs_1_ = bf16[512,1536]{1,0:T(8,128)(2,1)} fusion(bf16[1536,512]{1,0:T(8,128)(2,1)S(1)} %bitcast.63, s32[512]{0:T(512)S(1)} %get-tuple-element.102, s32[512]{0:T(512)S(1)} %get-tuple-element.104, s32[512]{0:T(512)S(1)} %get-tuple-element.101, s32[512]{0:T(512)S(1)} %get-tuple-element.107, s32[512]{0:T(512)S(1)} %get-tuple-element.103, ...), kind=kOutput, calls=%fused_computation.1 | convolution fusion | flops 822083584 | bytes 3159552 | tf_op jit(solution)/shard_map/dot_general | solution.py:343
  13.6 3.9 %collective-permute-done.1 = bf16[1,4,96,512]{3,2,1,0:T(8,128)(2,1)S(1)} collective-permute-done((bf16[1,4,96,512]{3,2,1,0:T(8,128)(2,1)S(1)}, bf16[1,4,96,512]{3,2,1,0:T(8,128)(2,1)S(1)}, u32[]{:S(2)}, u32[]{:S(2)}) %collective-permute-start.1) | collective-permute-done | bytes 393248 | tf_op jit(solution)/shard_map/ppermute | solution.py:59
  17.6 3.4 %collective-permute-start.2 = (bf16[6,4,1,512]{3,2,1,0:T(2,128)(2,1)S(1)}, bf16[6,4,1,512]{3,2,1,0:T(2,128)(2,1)S(1)}, u32[]{:S(2)}, u32[]{:S(2)}) collective-permute-start(bf16[6,4,1,512]{3,2,1,0:T(2,128)(2,1)S(1)} %pad_maximum_fusion.2), channel_id=1, source_target_pairs={{0,1},{1,2},{2,3},{3,4},{4,5},{5,6},{6,7},{7,8},{8,9},{9,10},{10,1... | collective-permute-start | bytes 73736 | tf_op jit(solution)/shard_map/ppermute | solution.py:66
  21.1 4.9 %centre_grads.1 = (f32[512,768]{1,0:T(8,128)S(1)}, bf16[512,768]{1,0:T(8,128)(2,1)S(1)}) custom-call(s32[1]{0:T(128)} %bitcast.core_ref.refs_0_, bf16[512,1536]{1,0:T(8,128)(2,1)S(1)} %copy-done.2, bf16[384,512]{1,0:T(8,128)(2,1)S(1)} %bitcast.53, bf16[1536,512]{1,0:T(8,128)(2,1)} %bitcast.61, bf16[384,512]{1,0:T(8,128)(2,1)S(1)} %bitcast.55), custom_call_target="tpu_custom_call" | custom-call | flops 2415919104 | bytes 8000000 | tf_op jit(solution)/shard_map/centre_grads/pallas_call | solution.py:112
  27.6 11.9 %side_grads.1 = (bf16[3,2304,512]{2,1,0:T(8,128)(2,1)}, f32[512,1536]{1,0:T(8,128)}, bf16[512,1536]{1,0:T(8,128)(2,1)}) custom-call(s32[1]{0:T(128)} %bitcast.core_ref.refs_0_, bf16[512,1536]{1,0:T(8,128)(2,1)} %convolution_convert_fusion.lhs_ref.refs_1_, bf16[384,512]{1,0:T(8,128)(2,1)} %bitcast.54, bf16[1536,512]{1,0:T(8,128)(2,1)} %bitcast.62, ...), custom_call_target="tpu_custom_call" | custom-call | flops 4831838208 | bytes 16000000 | tf_op jit(solution)/shard_map/side_grads/pallas_call | solution.py:182
  41.9 9.0 %all-to-all-start = ((bf16[16,2,4608]{2,1,0:T(2,128)(2,1)}), bf16[16,2,4608]{2,1,0:T(2,128)(2,1)S(1)}, u32[]{:S(2)}, u32[]{:S(2)}) async-start(bf16[16,2,4608]{2,1,0:T(2,128)(2,1)} %broadcast_in_dim.26), calls=%async_computation | async-start | bytes 589824 | tf_op jit(solution)/shard_map/all_to_all | solution.py:304
  57.8 5.5 %all-to-all-start.1 = ((bf16[16,32,2304]{2,1,0:T(8,128)(2,1)}), bf16[16,32,2304]{2,1,0:T(8,128)(2,1)}, u32[]{:S(2)}, u32[]{:S(2)}) async-start(bf16[16,32,2304]{2,1,0:T(8,128)(2,1)} %bitcast.10), calls=%async_computation.1 | async-start | bytes 4718592 | tf_op jit(solution)/shard_map/all_to_all | solution.py:369
  63.8 4.9 %collective-permute-start.10 = (bf16[32,4608]{1,0:T(8,128)(2,1)S(1)}, bf16[32,4608]{1,0:T(8,128)(2,1)S(1)}, u32[]{:S(2)}, u32[]{:S(2)}) collective-permute-start(bf16[32,4608]{1,0:T(8,128)(2,1)S(1)} %reshape.151), channel_id=1, source_target_pairs={{0,28},{4,0},{8,4},{12,8},{16,12},{20,16},{24,20},{28,24},{1,29},{... | collective-permute-start | bytes 884744 | tf_op jit(solution)/shard_map/ppermute | solution.py:298
  68.8 4.2 %collective-permute-done.10 = bf16[32,4608]{1,0:T(8,128)(2,1)S(1)} collective-permute-done((bf16[32,4608]{1,0:T(8,128)(2,1)S(1)}, bf16[32,4608]{1,0:T(8,128)(2,1)S(1)}, u32[]{:S(2)}, u32[]{:S(2)}) %collective-permute-start.10) | collective-permute-done | bytes 294944 | tf_op jit(solution)/shard_map/ppermute | solution.py:298
  73.0 3.5 %collective-permute-start.11 = (bf16[32,4608]{1,0:T(8,128)(2,1)S(1)}, bf16[32,4608]{1,0:T(8,128)(2,1)}, u32[]{:S(2)}, u32[]{:S(2)}) collective-permute-start(bf16[32,4608]{1,0:T(8,128)(2,1)S(1)} %collective-permute-done.10), channel_id=1, source_target_pairs={{0,28},{4,0},{8,4},{12,8},{16,12},{20,16},{24,20},{28,24},{1,29},{... | collective-permute-start | bytes 884744 | tf_op jit(solution)/shard_map/ppermute | solution.py:298
  76.5 3.6 %collective-permute-done.11 = bf16[32,4608]{1,0:T(8,128)(2,1)} collective-permute-done((bf16[32,4608]{1,0:T(8,128)(2,1)S(1)}, bf16[32,4608]{1,0:T(8,128)(2,1)}, u32[]{:S(2)}, u32[]{:S(2)}) %collective-permute-start.11) | collective-permute-done | bytes 294944 | tf_op jit(solution)/shard_map/ppermute | solution.py:298
  80.2 3.5 %collective-permute-start.12 = (bf16[32,4608]{1,0:T(8,128)(2,1)}, bf16[32,4608]{1,0:T(8,128)(2,1)}, u32[]{:S(2)}, u32[]{:S(2)}) collective-permute-start(bf16[32,4608]{1,0:T(8,128)(2,1)} %collective-permute-done.11), channel_id=1, source_target_pairs={{0,28},{4,0},{8,4},{12,8},{16,12},{20,16},{24,20},{28,24},{1,29},{... | collective-permute-start | bytes 884744 | tf_op jit(solution)/shard_map/ppermute | solution.py:298
  83.7 13.9 %all-to-all-done.1 = bf16[16,32,2304]{2,1,0:T(8,128)(2,1)} async-done(((bf16[16,32,2304]{2,1,0:T(8,128)(2,1)}), bf16[16,32,2304]{2,1,0:T(8,128)(2,1)}, u32[]{:S(2)}, u32[]{:S(2)}) %all-to-all-start.1) | async-done | bytes 2359328 | tf_op jit(solution)/shard_map/all_to_all | solution.py:369
  100.3 7.3 %all-to-all-start.2 = ((bf16[8,4,2304]{2,1,0:T(4,128)(2,1)}), bf16[8,4,2304]{2,1,0:T(4,128)(2,1)S(1)}, u32[]{:S(2)}, u32[]{:S(2)}) async-start(bf16[8,4,2304]{2,1,0:T(4,128)(2,1)} %reshape.154), calls=%async_computation.2 | async-start | bytes 294912 | tf_op jit(solution)/shard_map/all_to_all | solution.py:372
  109.1 6.5 %all-to-all-done.2 = bf16[8,4,2304]{2,1,0:T(4,128)(2,1)S(1)} async-done(((bf16[8,4,2304]{2,1,0:T(4,128)(2,1)}), bf16[8,4,2304]{2,1,0:T(4,128)(2,1)S(1)}, u32[]{:S(2)}, u32[]{:S(2)}) %all-to-all-start.2) | async-done | bytes 147488 | tf_op jit(solution)/shard_map/all_to_all | solution.py:372
  117.7 8.6 %all-to-all-start.3 = ((f32[256,1,1]{2,1,0:T(1,128)}), f32[256,1,1]{2,1,0:T(1,128)S(1)}, u32[]{:S(2)}, u32[]{:S(2)}) async-start(f32[256,1,1]{2,1,0:T(1,128)} %broadcast_in_dim.27), calls=%async_computation.3 | async-start | bytes 262144 | tf_op jit(solution)/shard_map/all_to_all | solution.py:304
  127.3 9.8 %all-to-all-done.3 = f32[256,1,1]{2,1,0:T(1,128)S(1)} async-done(((f32[256,1,1]{2,1,0:T(1,128)}), f32[256,1,1]{2,1,0:T(1,128)S(1)}, u32[]{:S(2)}, u32[]{:S(2)}) %all-to-all-start.3) | async-done | bytes 1056 | tf_op jit(solution)/shard_map/all_to_all | solution.py:304
  139.5 3.4 %all-to-all-start.4 = ((bf16[8,4,2304]{2,1,0:T(4,128)(2,1)}), bf16[8,4,2304]{2,1,0:T(4,128)(2,1)S(1)}, u32[]{:S(2)}, u32[]{:S(2)}) async-start(bf16[8,4,2304]{2,1,0:T(4,128)(2,1)} %broadcast_in_dim.28), calls=%async_computation.4 | async-start | bytes 294912 | tf_op jit(solution)/shard_map/all_to_all | solution.py:304
  143.9 6.8 %all-to-all-done.4 = bf16[8,4,2304]{2,1,0:T(4,128)(2,1)S(1)} async-done(((bf16[8,4,2304]{2,1,0:T(4,128)(2,1)}), bf16[8,4,2304]{2,1,0:T(4,128)(2,1)S(1)}, u32[]{:S(2)}, u32[]{:S(2)}) %all-to-all-start.4) | async-done | bytes 147488 | tf_op jit(solution)/shard_map/all_to_all | solution.py:304
  152.4 6.3 %all-to-all-start.5 = ((bf16[16,32,2304]{2,1,0:T(8,128)(2,1)}), bf16[16,32,2304]{2,1,0:T(8,128)(2,1)}, u32[]{:S(2)}, u32[]{:S(2)}) async-start(bf16[16,32,2304]{2,1,0:T(8,128)(2,1)} %broadcast_in_dim.30), calls=%async_computation.5 | async-start | bytes 4718592 | tf_op jit(solution)/shard_map/all_to_all | solution.py:304
  163.6 29.6 %all-to-all-done.5 = bf16[16,32,2304]{2,1,0:T(8,128)(2,1)} async-done(((bf16[16,32,2304]{2,1,0:T(8,128)(2,1)}), bf16[16,32,2304]{2,1,0:T(8,128)(2,1)}, u32[]{:S(2)}, u32[]{:S(2)}) %all-to-all-start.5) | async-done | bytes 2359328 | tf_op jit(solution)/shard_map/all_to_all | solution.py:304
  200.9 12.8 %pulled.1 = bf16[1536,512]{1,0:T(8,128)(2,1)S(1)} custom-call(bf16[3,2304,512]{2,1,0:T(8,128)(2,1)} %get-tuple-element.27.refs_0_, bf16[256,4608]{1,0:T(8,128)(2,1)S(1)} %constant_dynamic-update-slice_fusion.refs_1_, bf16[256,4608]{1,0:T(8,128)(2,1)} %collective-permute-done.13.refs_2_, bf16[256,512]{1,0:T(8,128)(2,1)S(1)} %get-tuple-element.100.refs_3_, ...), custom_call_target="tpu_custom_call" | custom-call | flops 7247757312 | bytes 14000000 | tf_op jit(solution)/shard_map/pulled/pallas_call | solution.py:229
  215.9 5.8 %joined.1 = bf16[9,512,512]{2,1,0:T(8,128)(2,1)} custom-call(s32[1]{0:T(128)} %bitcast.core_ref.refs_0_, bf16[128,128]{1,0:T(8,128)(2,1)} %fusion.77.order_ref, bf16[512,2304]{1,0:T(8,128)(2,1)} %bitcast.16.own_ref, bf16[512,2304]{1,0:T(8,128)(2,1)} %collective-permute-done.15.other_ref), custom_call_target="tpu_custom_call" | custom-call | tf_op jit(solution)/shard_map/joined/pallas_call | solution.py:275
  (126 shorter events, 43.6 us)
Async XLA Ops:
  2.6 11.0 %collective-permute-start = (bf16[1,4,96,512]{3,2,1,0:T(8,128)(2,1)S(1)}, bf16[1,4,96,512]{3,2,1,0:T(8,128)(2,1)S(1)}, u32[]{:S(2)}, u32[]{:S(2)}) collective-permute-start(bf16[1,4,96,512]{3,2,1,0:T(8,128)(2,1)S(1)} %pad.15), channel_id=1, source_target_pairs={{0,32},{32,64},{64,96},{96,128},{128,160},{160,192},{192,224},{1,3... | collective-permute-start | bytes 1179656 | tf_op jit(solution)/shard_map/ppermute | solution.py:59
  5.8 11.6 %collective-permute-start.1 = (bf16[1,4,96,512]{3,2,1,0:T(8,128)(2,1)S(1)}, bf16[1,4,96,512]{3,2,1,0:T(8,128)(2,1)S(1)}, u32[]{:S(2)}, u32[]{:S(2)}) collective-permute-start(bf16[1,4,96,512]{3,2,1,0:T(8,128)(2,1)S(1)} %pad.17), channel_id=1, source_target_pairs={{32,0},{64,32},{96,64},{128,96},{160,128},{192,160},{224,192},{33,... | collective-permute-start | bytes 1179656 | tf_op jit(solution)/shard_map/ppermute | solution.py:59
  17.6 8.4 %collective-permute-start.2 = (bf16[6,4,1,512]{3,2,1,0:T(2,128)(2,1)S(1)}, bf16[6,4,1,512]{3,2,1,0:T(2,128)(2,1)S(1)}, u32[]{:S(2)}, u32[]{:S(2)}) collective-permute-start(bf16[6,4,1,512]{3,2,1,0:T(2,128)(2,1)S(1)} %pad_maximum_fusion.2), channel_id=1, source_target_pairs={{0,1},{1,2},{2,3},{3,4},{4,5},{5,6},{6,7},{7,8},{8,9},{9,10},{10,1... | collective-permute-start | bytes 73736 | tf_op jit(solution)/shard_map/ppermute | solution.py:66
  21.0 6.0 %collective-permute-start.3 = (bf16[6,4,1,512]{3,2,1,0:T(2,128)(2,1)S(1)}, bf16[6,4,1,512]{3,2,1,0:T(2,128)(2,1)S(1)}, u32[]{:S(2)}, u32[]{:S(2)}) collective-permute-start(bf16[6,4,1,512]{3,2,1,0:T(2,128)(2,1)S(1)} %pad_maximum_fusion.3), channel_id=1, source_target_pairs={{1,0},{2,1},{3,2},{4,3},{5,4},{6,5},{7,6},{8,7},{9,8},{10,9},{11,1... | collective-permute-start | bytes 73736 | tf_op jit(solution)/shard_map/ppermute | solution.py:66
  27.6 12.8 %copy-start.7 = (f32[2,9,512]{2,0,1:T(2,128)S(1)}, f32[2,9,512]{2,0,1:T(2,128)}, u32[]{:S(2)}) copy-start(f32[2,9,512]{2,0,1:T(2,128)} %param.8) | copy-start | bytes 110596
  39.5 12.9 %collective-permute-start.5 = (bf16[512,1536]{1,0:T(8,128)(2,1)}, bf16[512,1536]{1,0:T(8,128)(2,1)}, u32[]{:S(2)}, u32[]{:S(2)}) collective-permute-start(bf16[512,1536]{1,0:T(8,128)(2,1)} %get-tuple-element.25), channel_id=1, source_target_pairs={{0,1},{1,0},{2,3},{3,2},{4,5},{5,4},{6,7},{7,6},{8,9},{9,8},{10,11... | collective-permute-start | bytes 4718600 | tf_op jit(solution)/shard_map/ppermute | solution.py:70
  40.3 10.6 %collective-permute-start.4 = (bf16[512,768]{1,0:T(8,128)(2,1)S(1)}, bf16[512,768]{1,0:T(8,128)(2,1)}, u32[]{:S(2)}, u32[]{:S(2)}) collective-permute-start(bf16[512,768]{1,0:T(8,128)(2,1)S(1)} %get-tuple-element.23), channel_id=1, source_target_pairs={{0,1},{1,0},{2,3},{3,2},{4,5},{5,4},{6,7},{7,6},{8,9},{9,8},{10,11... | collective-permute-start | bytes 2359304 | tf_op jit(solution)/shard_map/ppermute | solution.py:70
  40.5 22.8 %collective-permute-start.14 = (f32[3,2,9,256]{3,2,1,0:T(8,128)S(1)}, f32[3,2,9,256]{3,2,1,0:T(8,128)S(1)}, u32[]{:S(2)}, u32[]{:S(2)}) collective-permute-start(f32[3,2,9,256]{3,2,1,0:T(8,128)S(1)} %get-tuple-element.98), channel_id=1, source_target_pairs={{0,1},{1,0},{2,3},{3,2},{4,5},{5,4},{6,7},{7,6},{8,9},{9,8},{10,11... | collective-permute-start | bytes 165896 | tf_op jit(solution)/shard_map/ppermute | solution.py:70
  41.9 15.8 %all-to-all-start = ((bf16[16,2,4608]{2,1,0:T(2,128)(2,1)}), bf16[16,2,4608]{2,1,0:T(2,128)(2,1)S(1)}, u32[]{:S(2)}, u32[]{:S(2)}) async-start(bf16[16,2,4608]{2,1,0:T(2,128)(2,1)} %broadcast_in_dim.26), calls=%async_computation | async-start | bytes 589824 | tf_op jit(solution)/shard_map/all_to_all | solution.py:304
  57.8 39.8 %all-to-all-start.1 = ((bf16[16,32,2304]{2,1,0:T(8,128)(2,1)}), bf16[16,32,2304]{2,1,0:T(8,128)(2,1)}, u32[]{:S(2)}, u32[]{:S(2)}) async-start(bf16[16,32,2304]{2,1,0:T(8,128)(2,1)} %bitcast.10), calls=%async_computation.1 | async-start | bytes 4718592 | tf_op jit(solution)/shard_map/all_to_all | solution.py:369
  63.8 9.2 %collective-permute-start.10 = (bf16[32,4608]{1,0:T(8,128)(2,1)S(1)}, bf16[32,4608]{1,0:T(8,128)(2,1)S(1)}, u32[]{:S(2)}, u32[]{:S(2)}) collective-permute-start(bf16[32,4608]{1,0:T(8,128)(2,1)S(1)} %reshape.151), channel_id=1, source_target_pairs={{0,28},{4,0},{8,4},{12,8},{16,12},{20,16},{24,20},{28,24},{1,29},{... | collective-permute-start | bytes 884744 | tf_op jit(solution)/shard_map/ppermute | solution.py:298
  68.7 7.8 %collective-permute-start.6 = (bf16[32,4608]{1,0:T(8,128)(2,1)S(1)}, bf16[32,4608]{1,0:T(8,128)(2,1)S(1)}, u32[]{:S(2)}, u32[]{:S(2)}) collective-permute-start(bf16[32,4608]{1,0:T(8,128)(2,1)S(1)} %reshape.151), channel_id=1, source_target_pairs={{0,4},{4,8},{8,12},{12,16},{16,20},{20,24},{24,28},{28,0},{1,5},{5... | collective-permute-start | bytes 884744 | tf_op jit(solution)/shard_map/ppermute | solution.py:296
  73.0 7.2 %collective-permute-start.11 = (bf16[32,4608]{1,0:T(8,128)(2,1)S(1)}, bf16[32,4608]{1,0:T(8,128)(2,1)}, u32[]{:S(2)}, u32[]{:S(2)}) collective-permute-start(bf16[32,4608]{1,0:T(8,128)(2,1)S(1)} %collective-permute-done.10), channel_id=1, source_target_pairs={{0,28},{4,0},{8,4},{12,8},{16,12},{20,16},{24,20},{28,24},{1,29},{... | collective-permute-start | bytes 884744 | tf_op jit(solution)/shard_map/ppermute | solution.py:298
  76.5 7.2 %collective-permute-start.7 = (bf16[32,4608]{1,0:T(8,128)(2,1)S(1)}, bf16[32,4608]{1,0:T(8,128)(2,1)S(1)}, u32[]{:S(2)}, u32[]{:S(2)}) collective-permute-start(bf16[32,4608]{1,0:T(8,128)(2,1)S(1)} %collective-permute-done.6), channel_id=1, source_target_pairs={{0,4},{4,8},{8,12},{12,16},{16,20},{20,24},{24,28},{28,0},{1,5},{5... | collective-permute-start | bytes 884744 | tf_op jit(solution)/shard_map/ppermute | solution.py:296
  80.2 79.5 %collective-permute-start.12 = (bf16[32,4608]{1,0:T(8,128)(2,1)}, bf16[32,4608]{1,0:T(8,128)(2,1)}, u32[]{:S(2)}, u32[]{:S(2)}) collective-permute-start(bf16[32,4608]{1,0:T(8,128)(2,1)} %collective-permute-done.11), channel_id=1, source_target_pairs={{0,28},{4,0},{8,4},{12,8},{16,12},{20,16},{24,20},{28,24},{1,29},{... | collective-permute-start | bytes 884744 | tf_op jit(solution)/shard_map/ppermute | solution.py:298
  83.7 23.9 %collective-permute-start.8 = (bf16[32,4608]{1,0:T(8,128)(2,1)S(1)}, bf16[32,4608]{1,0:T(8,128)(2,1)}, u32[]{:S(2)}, u32[]{:S(2)}) collective-permute-start(bf16[32,4608]{1,0:T(8,128)(2,1)S(1)} %collective-permute-done.7), channel_id=1, source_target_pairs={{0,4},{4,8},{8,12},{12,16},{16,20},{20,24},{24,28},{28,0},{1,5},{5... | collective-permute-start | bytes 884744 | tf_op jit(solution)/shard_map/ppermute | solution.py:296
  100.3 15.4 %all-to-all-start.2 = ((bf16[8,4,2304]{2,1,0:T(4,128)(2,1)}), bf16[8,4,2304]{2,1,0:T(4,128)(2,1)S(1)}, u32[]{:S(2)}, u32[]{:S(2)}) async-start(bf16[8,4,2304]{2,1,0:T(4,128)(2,1)} %reshape.154), calls=%async_computation.2 | async-start | bytes 294912 | tf_op jit(solution)/shard_map/all_to_all | solution.py:372
  107.6 35.3 %collective-permute-start.9 = (bf16[32,4608]{1,0:T(8,128)(2,1)}, bf16[32,4608]{1,0:T(8,128)(2,1)}, u32[]{:S(2)}, u32[]{:S(2)}) collective-permute-start(bf16[32,4608]{1,0:T(8,128)(2,1)} %collective-permute-done.8), channel_id=1, source_target_pairs={{0,4},{4,8},{8,12},{12,16},{16,20},{20,24},{24,28},{28,0},{1,5},{5... | collective-permute-start | bytes 884744 | tf_op jit(solution)/shard_map/ppermute | solution.py:296
  117.7 19.4 %all-to-all-start.3 = ((f32[256,1,1]{2,1,0:T(1,128)}), f32[256,1,1]{2,1,0:T(1,128)S(1)}, u32[]{:S(2)}, u32[]{:S(2)}) async-start(f32[256,1,1]{2,1,0:T(1,128)} %broadcast_in_dim.27), calls=%async_computation.3 | async-start | bytes 262144 | tf_op jit(solution)/shard_map/all_to_all | solution.py:304
  139.5 11.2 %all-to-all-start.4 = ((bf16[8,4,2304]{2,1,0:T(4,128)(2,1)}), bf16[8,4,2304]{2,1,0:T(4,128)(2,1)S(1)}, u32[]{:S(2)}, u32[]{:S(2)}) async-start(bf16[8,4,2304]{2,1,0:T(4,128)(2,1)} %broadcast_in_dim.28), calls=%async_computation.4 | async-start | bytes 294912 | tf_op jit(solution)/shard_map/all_to_all | solution.py:304
  152.4 40.8 %all-to-all-start.5 = ((bf16[16,32,2304]{2,1,0:T(8,128)(2,1)}), bf16[16,32,2304]{2,1,0:T(8,128)(2,1)}, u32[]{:S(2)}, u32[]{:S(2)}) async-start(bf16[16,32,2304]{2,1,0:T(8,128)(2,1)} %broadcast_in_dim.30), calls=%async_computation.5 | async-start | bytes 4718592 | tf_op jit(solution)/shard_map/all_to_all | solution.py:304
  160.6 40.2 %collective-permute-start.13 = (bf16[256,4608]{1,0:T(8,128)(2,1)S(1)}, bf16[256,4608]{1,0:T(8,128)(2,1)}, u32[]{:S(2)}, u32[]{:S(2)}) collective-permute-start(bf16[256,4608]{1,0:T(8,128)(2,1)S(1)} %constant_dynamic-update-slice_fusion.refs_1_), channel_id=1, source_target_pairs={{0,1},{1,0},{2,3},{3,2},{4,5},{5,4},{6,7},{7,6},{8,9},{9,8},{10,11... | collective-permute-start | bytes 7077896 | tf_op jit(solution)/shard_map/ppermute | solution.py:70
  193.1 22.8 %collective-permute-start.15 = (bf16[512,2304]{1,0:T(8,128)(2,1)}, bf16[512,2304]{1,0:T(8,128)(2,1)}, u32[]{:S(2)}, u32[]{:S(2)}) collective-permute-start(bf16[512,2304]{1,0:T(8,128)(2,1)} %bitcast.16.own_ref), channel_id=1, source_target_pairs={{0,1},{1,0},{2,3},{3,2},{4,5},{5,4},{6,7},{7,6},{8,9},{9,8},{10,11... | collective-permute-start | bytes 7077896 | tf_op jit(solution)/shard_map/ppermute | solution.py:70
  194.8 3.5 %collective-permute-start.16 = (f32[4,2,9,256]{3,2,1,0:T(8,128)S(1)}, f32[4,2,9,256]{3,2,1,0:T(8,128)S(1)}, u32[]{:S(2)}, u32[]{:S(2)}) collective-permute-start(f32[4,2,9,256]{3,2,1,0:T(8,128)S(1)} %get-tuple-element.80), channel_id=1, source_target_pairs={{0,1},{1,0},{2,3},{3,2},{4,5},{5,4},{6,7},{7,6},{8,9},{9,8},{10,11... | collective-permute-start | bytes 221192 | tf_op jit(solution)/shard_map/ppermute | solution.py:70
  (9 other events, 66.3 us)

commit v3 on v2

--- a/solution.py
+++ b/solution.py
@@ -2,6 +2,7 @@
 
 import jax
 import jax.numpy as jnp
+import numpy as np
 from jax import lax
 from jax.experimental import pallas as pl
 from jax.experimental.pallas import tpu as pltpu
@@ -258,45 +259,52 @@
     return new_master, new_one, new_two, clipped
 
 
-def join_kernel(core_ref, order_ref, own_ref, other_ref, out_ref):
-    half = own_ref.shape[1] // TAPS
-    own = pl.multiple_of(core_ref[0] * half, half)
-    other = pl.multiple_of((1 - core_ref[0]) * half, half)
-    for lane, ref in ((own, own_ref), (other, other_ref)):
-        rows = jnp.dot(order_ref[...], ref[...], preferred_element_type=F32).astype(BF16)
-        for index, tap in enumerate(ORDER):
-            out_ref[tap, :, pl.ds(lane, half)] = rows[:, index * half : (index + 1) * half]
-
-
-def joined(core, order, own, other):
-    chans, wide = own.shape
+def join_kernel(_, order_ref, part_ref, *refs):
+    out_ref = refs[-1]
+    half = out_ref.shape[2]
+    rows = jnp.dot(order_ref[...], part_ref[...], preferred_element_type=F32).astype(BF16)
+    for index, tap in enumerate(ORDER):
+        out_ref[tap] = rows[:, index * half : (index + 1) * half]
+
+
+def joined(lane, order, part, out):
+    chans, wide = part.shape
     half = wide // TAPS
     block = order.shape[0]
+    operands = (order, part) if out is None else (order, part, out)
     return pl.pallas_call(
         join_kernel,
-        grid=(chans // block,),
-        in_specs=[
-            pl.BlockSpec(memory_space=pltpu.SMEM),
-            pl.BlockSpec(order.shape, lambda i: (0, 0)),
-            pl.BlockSpec((block, wide), lambda i: (i, 0)),
-            pl.BlockSpec((block, wide), lambda i: (i, 0)),
-        ],
-        out_specs=pl.BlockSpec((TAPS, block, 2 * half), lambda i: (0, i, 0)),
+        grid_spec=pltpu.PrefetchScalarGridSpec(
+            num_scalar_prefetch=1,
+            grid=(chans // block,),
+            in_specs=[
+                pl.BlockSpec(order.shape, lambda i, lane_ref: (0, 0)),
+                pl.BlockSpec((block, wide), lambda i, lane_ref: (i, 0)),
+                pl.BlockSpec(memory_space=pl.ANY),
+            ][: len(operands)],
+            out_specs=pl.BlockSpec((TAPS, block, half), lambda i, lane_ref: (0, i, lane_ref[0])),
+        ),
         out_shape=jax.ShapeDtypeStruct((TAPS, chans, 2 * half), BF16),
+        input_output_aliases={} if out is None else {3: 0},
+        cost_estimate=pl.CostEstimate(
+            flops=2 * part.size * block, bytes_accessed=8 * part.size, transcendentals=0
+        ),
         name="joined",
-    )(core, order, own, other)
-
-
-def around_ring(chunk, after):
-    chunk, _ = lax.optimization_barrier((chunk, after))
+    )(lane, *operands)
+
+
+def around_ring(chunk, early, late):
     up = [(i, (i + 1) % 8) for i in range(8)]
     down = [(i, (i - 1) % 8) for i in range(8)]
-    below, above = [chunk], [chunk]
-    for _ in range(4):
+    chunk, _ = lax.optimization_barrier((chunk, early))
+    first = lax.ppermute(chunk, "z", up), lax.ppermute(chunk, "z", down)
+    first, _ = lax.optimization_barrier((first, late))
+    below, above = [chunk, first[0]], [first[1]]
+    for _ in range(3):
         below.append(lax.ppermute(below[-1], "z", up))
-    for _ in range(3):
+    for _ in range(2):
         above.append(lax.ppermute(above[-1], "z", down))
-    return jnp.concatenate(below + above[1:], axis=0)
+    return jnp.concatenate(below + above, axis=0)
 
 
 def to_all(piece, axes, count):
@@ -327,7 +335,6 @@
     extra = padded_cols - lon_cols
     core = lax.axis_index("c")
     core_ref = core.reshape(1).astype(jnp.int32)
-    square = (chans, chans)
 
     def padded(field):
         return jnp.pad(
@@ -339,15 +346,11 @@
 
     above, below = row_halo(padded(upstream[:, :1]), padded(upstream[:, -1:]))
     up_rows = padded(upstream)
-    order = (row_channel(rows_of(square, 0)) == rows_of(square, 1)).astype(BF16)
+    rows = np.arange(chans)
+    order = jnp.asarray(row_channel(rows)[:, None] == rows[None, :], BF16)
     lhs = lax.dot_general(
         order, flat(padded(activations)), (((1,), (1,)), ((), ())), preferred_element_type=F32
     ).astype(BF16)
-    state = jnp.stack([master, moment_one, moment_two])
-    own_state, other_state = halves(state, core)
-    other_state = swap(other_state)
-    state = in_core_order(own_state, other_state, core, 1)
-    state = jnp.stack([state[:, :, tap] for tap in ORDER], axis=2).reshape(12, wide)
     left, right = col_halo((above, up_rows, below), lon_cols - 1)
     pieces = (flat(above), flat(up_rows), flat(below))
     old_piece = master.astype(BF16).reshape(2, TAPS * outs)
@@ -366,8 +369,14 @@
         ],
         axis=1,
     ).reshape(16, 32, wide)
+    state = jnp.stack([master, moment_one, moment_two])
+    state, pair_sum = lax.optimization_barrier((state, pair_sum))
+    own_state, other_state = halves(state, core)
+    other_state = swap(other_state)
+    state = in_core_order(own_state, other_state, core, 1)
+    state = jnp.stack([state[:, :, tap] for tap in ORDER], axis=2).reshape(12, wide)
     parts = lax.all_to_all(pair_sum, PLANE, 0, 0, tiled=True)
-    old_own = around_ring(old_plane, pair_sum)
+    old_own = around_ring(old_plane, keep_one, pair_sum)
     plane_sum = jnp.sum(parts.astype(F32), axis=0).astype(BF16).reshape(8, 4, wide)
     parts = lax.all_to_all(plane_sum, ("z",), 0, 0, tiled=True)
     grad = jnp.sum(parts.astype(F32), axis=0)
@@ -379,10 +388,11 @@
     own = to_all(new_line, PLANE, 16).reshape(chans, wide)
 
     results = results.reshape(4, 4, TAPS, half)
-    results = jnp.stack([results[:, :, ORDER.index(tap)] for tap in range(TAPS)], axis=2)
-    mine = jnp.where(core == 0, results[:, :2], results[:, 2:])
-    theirs = jnp.where(core == 0, results[:, 2:], results[:, :2])
+    results = jnp.stack([results[:, :, ORDER.index(tap)] for tap in range(TAPS)], axis=1)
+    mine = jnp.where(core == 0, results[:, :, :2], results[:, :, 2:])
+    theirs = jnp.where(core == 0, results[:, :, 2:], results[:, :, :2])
     results = in_core_order(mine, swap(theirs), core, 3)
+    results = [jnp.transpose(result, (1, 0, 2)) for result in results]
 
     old_other = swap(old_own)
     fields, old_own, old_other, _ = lax.optimization_barrier(
@@ -398,9 +408,12 @@
     input_grad = pulled_rows.reshape(lat_rows, batch, padded_cols, chans)
     input_grad = jnp.transpose(input_grad[:, :, :lon_cols], (1, 0, 2, 3))
 
-    lat_block = (chans // 4, chans // 4)
-    back = (rows_of(lat_block, 0) == row_channel(rows_of(lat_block, 1))).astype(BF16)
-    new_weights = jnp.transpose(joined(core_ref, back, own, swap(own)), (1, 0, 2))
+    rows = np.arange(chans // 4)
+    back = jnp.asarray(rows[:, None] == row_channel(rows)[None, :], BF16)
+    other = swap(own)
+    out = joined(core_ref, back, own, None)
+    out = joined(1 - core_ref, back, other, out)
+    new_weights = jnp.transpose(out, (1, 0, 2))
     return (input_grad, new_weights, *results)
 
 

time: 223 us -> 227 us (1.018)
  Pallas kernels: 35.3 us -> 38.4 us
  matrix products: 3.98 us -> 1.04 us
    ppermute x3 -> x2, starting transfers between devices: 11.9 us -> 3.93 us  [around_ring(): above.append(lax.ppermute(above[-1], 'z', down))]
    ppermute x3 -> x2, waiting for transfers between devices: 7.87 us -> 0.01 us  [around_ring(): above.append(lax.ppermute(above[-1], 'z', down))]
    ppermute x0 -> x2, waiting for transfers between devices: none -> 5.43 us  [around_ring(): first = (lax.ppermute(chunk, 'z', up), lax.ppermute(chunk, 'z', down))]
    ppermute x0 -> x2, starting transfers between devices: none -> 4.99 us  [around_ring(): first = (lax.ppermute(chunk, 'z', up), lax.ppermute(chunk, 'z', down))]
    pallas_call x1 -> x2, Pallas kernels: 5.77 us -> 8.84 us  [joined(): pl.pallas_call(join_kernel, grid_spec=pltpu.PrefetchScalarGridSpec(num_sc...]
    dot_general x1, matrix products: 3.98 us -> 1.04 us  [per_device(): lax.dot_general(order, flat(padded(activations)), (((1,), (1,)), ((), ())...]
    ppermute x6, starting transfers between devices: 5.11 us -> 7.48 us  [swap(): return lax.ppermute(array, 'c', [(0, 1), (1, 0)])]
    unnamed x38 -> x40, local copies, waits for them, and re-layouts: 11.4 us -> 13 us
  transfers between devices with their start and end apart: 23 -> 23, of which waited for: 12 -> 11; matrix products, arithmetic and copies ran while one was open for 14% -> 14% of each run, Pallas kernels for 8% -> 10%
where the time goes in v3:
time: 227 us; the launch traced here: 225 us
  waiting for transfers between devices  84.2 us (37%)
  starting transfers between devices  67 us (30%)
  Pallas kernels  38.4 us (17%)
  local copies, waits for them, and re-layouts  21.5 us (9%)
  other arithmetic  10.6 us (5%)
    all_to_all x4, waiting for transfers between devices, to_all(): return lax.all_to_all(copies, axes, 0, 0, tiled=True)  47.7 us
    all_to_all x4, starting transfers between devices, to_all(): return lax.all_to_all(copies, axes, 0, 0, tiled=True)  27.7 us
    all_to_all x1, waiting for transfers between devices, per_device(): parts = lax.all_to_all(pair_sum, PLANE, 0, 0, tiled=True)  15.8 us
    unnamed x40, local copies, waits for them, and re-layouts  13 us
    pallas_call x1, Pallas kernels, pulled(): pl.pallas_call(lambda *refs: pull_kernel(*refs, block=block), grid=(4,),...  12.8 us
    pallas_call x1, Pallas kernels, side_grads(): pl.pallas_call(lambda *refs: side_kernel(*refs, cols=cols, padded_cols=pa...  11.9 us
    pallas_call x2, Pallas kernels, joined(): pl.pallas_call(join_kernel, grid_spec=pltpu.PrefetchScalarGridSpec(num_sc...  8.84 us
    ppermute x6, starting transfers between devices, swap(): return lax.ppermute(array, 'c', [(0, 1), (1, 0)])  7.48 us
  transfers between devices with their start and end apart: 23, of which 11 were waited for; matrix products, arithmetic and copies ran while one was open for 14% of the time, Pallas kernels for 10%

profile of v3, /device:TPU:5, one launch (start us, length us, event | category | flops | bytes accessed | tf_op | source)
XLA Modules:
  0.0 224.7 jit_solution(5707759906193697135)
XLA Ops:
  2.4 3.2 %collective-permute-start = (bf16[1,4,96,512]{3,2,1,0:T(8,128)(2,1)S(1)}, bf16[1,4,96,512]{3,2,1,0:T(8,128)(2,1)S(1)}, u32[]{:S(2)}, u32[]{:S(2)}) collective-permute-start(bf16[1,4,96,512]{3,2,1,0:T(8,128)(2,1)S(1)} %pad.15), channel_id=1, source_target_pairs={{0,32},{32,64},{64,96},{96,128},{128,160},{160,192},{192,224},{1,3... | collective-permute-start | bytes 1179656 | tf_op jit(solution)/shard_map/ppermute | solution.py:60
  11.3 6.0 %collective-permute-done.1 = bf16[1,4,96,512]{3,2,1,0:T(8,128)(2,1)S(1)} collective-permute-done((bf16[1,4,96,512]{3,2,1,0:T(8,128)(2,1)S(1)}, bf16[1,4,96,512]{3,2,1,0:T(8,128)(2,1)S(1)}, u32[]{:S(2)}, u32[]{:S(2)}) %collective-permute-start.1) | collective-permute-done | bytes 393248 | tf_op jit(solution)/shard_map/ppermute | solution.py:60
  17.5 3.4 %collective-permute-start.2 = (bf16[6,4,1,512]{3,2,1,0:T(2,128)(2,1)S(1)}, bf16[6,4,1,512]{3,2,1,0:T(2,128)(2,1)S(1)}, u32[]{:S(2)}, u32[]{:S(2)}) collective-permute-start(bf16[6,4,1,512]{3,2,1,0:T(2,128)(2,1)S(1)} %pad_maximum_fusion.2), channel_id=1, source_target_pairs={{0,1},{1,2},{2,3},{3,4},{4,5},{5,6},{6,7},{7,8},{8,9},{9,10},{10,1... | collective-permute-start | bytes 73736 | tf_op jit(solution)/shard_map/ppermute | solution.py:67
  21.0 4.9 %centre_grads.1 = (f32[512,768]{1,0:T(8,128)S(1)}, bf16[512,768]{1,0:T(8,128)(2,1)S(1)}) custom-call(s32[1]{0:T(128)} %bitcast.core_ref.refs_0_._, bf16[512,1536]{1,0:T(8,128)(2,1)S(1)} %fusion.lhs_ref.refs_1_, bf16[384,512]{1,0:T(8,128)(2,1)S(1)} %bitcast.82, bf16[1536,512]{1,0:T(8,128)(2,1)} %bitcast.90, bf16[384,512]{1,0:T(8,128)(2,1)S(1)} %bitcast.84), custom_call_target="tpu_custom_call" | custom-call | flops 2415919104 | bytes 8000000 | tf_op jit(solution)/shard_map/centre_grads/pallas_call | solution.py:113
  27.5 11.9 %side_grads.1 = (bf16[3,2304,512]{2,1,0:T(8,128)(2,1)}, f32[512,1536]{1,0:T(8,128)}, bf16[512,1536]{1,0:T(8,128)(2,1)}) custom-call(s32[1]{0:T(128)} %bitcast.core_ref.refs_0_._, bf16[512,1536]{1,0:T(8,128)(2,1)} %copy-done.2, bf16[384,512]{1,0:T(8,128)(2,1)} %bitcast.83, bf16[1536,512]{1,0:T(8,128)(2,1)} %bitcast.91, bf16[384,512]{1,0:T(8,128)(2,1)} %bitcast.85, ...), custom_call_target="tpu_custom_call" | custom-call | flops 4831838208 | bytes 16000000 | tf_op jit(solution)/shard_map/side_grads/pallas_call | solution.py:183
  41.2 9.0 %all-to-all-start = ((bf16[16,2,4608]{2,1,0:T(2,128)(2,1)}), bf16[16,2,4608]{2,1,0:T(2,128)(2,1)S(1)}, u32[]{:S(2)}, u32[]{:S(2)}) async-start(bf16[16,2,4608]{2,1,0:T(2,128)(2,1)} %broadcast_in_dim.26), calls=%async_computation | async-start | bytes 589824 | tf_op jit(solution)/shard_map/all_to_all | solution.py:312
  56.6 6.3 %all-to-all-start.1 = ((bf16[16,32,2304]{2,1,0:T(8,128)(2,1)}), bf16[16,32,2304]{2,1,0:T(8,128)(2,1)}, u32[]{:S(2)}, u32[]{:S(2)}) async-start(bf16[16,32,2304]{2,1,0:T(8,128)(2,1)} %bitcast.14), calls=%async_computation.1 | async-start | bytes 4718592 | tf_op jit(solution)/shard_map/all_to_all | solution.py:378
  63.8 4.2 %collective-permute-start.5 = (bf16[32,4608]{1,0:T(8,128)(2,1)S(1)}, bf16[32,4608]{1,0:T(8,128)(2,1)S(1)}, u32[]{:S(2)}, u32[]{:S(2)}) collective-permute-start(bf16[32,4608]{1,0:T(8,128)(2,1)S(1)} %reshape.151), channel_id=1, source_target_pairs={{0,28},{4,0},{8,4},{12,8},{16,12},{20,16},{24,20},{28,24},{1,29},{... | collective-permute-start | bytes 884744 | tf_op jit(solution)/shard_map/ppermute | solution.py:300
  68.0 5.4 %collective-permute-done.4 = bf16[32,4608]{1,0:T(8,128)(2,1)} collective-permute-done((bf16[32,4608]{1,0:T(8,128)(2,1)S(1)}, bf16[32,4608]{1,0:T(8,128)(2,1)}, u32[]{:S(2)}, u32[]{:S(2)}) %collective-permute-start.4) | collective-permute-done | bytes 294944 | tf_op jit(solution)/shard_map/ppermute | solution.py:300
  74.9 2.9 %collective-permute-start.14 = (f32[3,2,9,256]{3,2,1,0:T(8,128)S(1)}, f32[3,2,9,256]{3,2,1,0:T(8,128)S(1)}, u32[]{:S(2)}, u32[]{:S(2)}) collective-permute-start(f32[3,2,9,256]{3,2,1,0:T(8,128)S(1)} %get-tuple-element.108), channel_id=1, source_target_pairs={{0,1},{1,0},{2,3},{3,2},{4,5},{5,4},{6,7},{7,6},{8,9},{9,8},{10,11... | collective-permute-start | bytes 165896 | tf_op jit(solution)/shard_map/ppermute | solution.py:71
  81.2 15.8 %all-to-all-done.1 = bf16[16,32,2304]{2,1,0:T(8,128)(2,1)} async-done(((bf16[16,32,2304]{2,1,0:T(8,128)(2,1)}), bf16[16,32,2304]{2,1,0:T(8,128)(2,1)}, u32[]{:S(2)}, u32[]{:S(2)}) %all-to-all-start.1) | async-done | bytes 2359328 | tf_op jit(solution)/shard_map/all_to_all | solution.py:378
  99.7 7.3 %all-to-all-start.2 = ((bf16[8,4,2304]{2,1,0:T(4,128)(2,1)}), bf16[8,4,2304]{2,1,0:T(4,128)(2,1)S(1)}, u32[]{:S(2)}, u32[]{:S(2)}) async-start(bf16[8,4,2304]{2,1,0:T(4,128)(2,1)} %reshape.154), calls=%async_computation.2 | async-start | bytes 294912 | tf_op jit(solution)/shard_map/all_to_all | solution.py:381
  110.7 4.3 %all-to-all-done.2 = bf16[8,4,2304]{2,1,0:T(4,128)(2,1)S(1)} async-done(((bf16[8,4,2304]{2,1,0:T(4,128)(2,1)}), bf16[8,4,2304]{2,1,0:T(4,128)(2,1)S(1)}, u32[]{:S(2)}, u32[]{:S(2)}) %all-to-all-start.2) | async-done | bytes 147488 | tf_op jit(solution)/shard_map/all_to_all | solution.py:381
  117.2 9.1 %all-to-all-start.3 = ((f32[256,1,1]{2,1,0:T(1,128)}), f32[256,1,1]{2,1,0:T(1,128)S(1)}, u32[]{:S(2)}, u32[]{:S(2)}) async-start(f32[256,1,1]{2,1,0:T(1,128)} %broadcast_in_dim.27), calls=%async_computation.3 | async-start | bytes 262144 | tf_op jit(solution)/shard_map/all_to_all | solution.py:312
  127.2 9.8 %all-to-all-done.3 = f32[256,1,1]{2,1,0:T(1,128)S(1)} async-done(((f32[256,1,1]{2,1,0:T(1,128)}), f32[256,1,1]{2,1,0:T(1,128)S(1)}, u32[]{:S(2)}, u32[]{:S(2)}) %all-to-all-start.3) | async-done | bytes 1056 | tf_op jit(solution)/shard_map/all_to_all | solution.py:312
  139.4 3.4 %all-to-all-start.4 = ((bf16[8,4,2304]{2,1,0:T(4,128)(2,1)}), bf16[8,4,2304]{2,1,0:T(4,128)(2,1)S(1)}, u32[]{:S(2)}, u32[]{:S(2)}) async-start(bf16[8,4,2304]{2,1,0:T(4,128)(2,1)} %broadcast_in_dim.28), calls=%async_computation.4 | async-start | bytes 294912 | tf_op jit(solution)/shard_map/all_to_all | solution.py:312
  143.8 6.8 %all-to-all-done.4 = bf16[8,4,2304]{2,1,0:T(4,128)(2,1)S(1)} async-done(((bf16[8,4,2304]{2,1,0:T(4,128)(2,1)}), bf16[8,4,2304]{2,1,0:T(4,128)(2,1)S(1)}, u32[]{:S(2)}, u32[]{:S(2)}) %all-to-all-start.4) | async-done | bytes 147488 | tf_op jit(solution)/shard_map/all_to_all | solution.py:312
  152.3 6.3 %all-to-all-start.5 = ((bf16[16,32,2304]{2,1,0:T(8,128)(2,1)}), bf16[16,32,2304]{2,1,0:T(8,128)(2,1)}, u32[]{:S(2)}, u32[]{:S(2)}) async-start(bf16[16,32,2304]{2,1,0:T(8,128)(2,1)} %broadcast_in_dim.30), calls=%async_computation.5 | async-start | bytes 4718592 | tf_op jit(solution)/shard_map/all_to_all | solution.py:312
  159.6 2.9 %collective-permute-start.13 = (bf16[256,4608]{1,0:T(8,128)(2,1)S(1)}, bf16[256,4608]{1,0:T(8,128)(2,1)}, u32[]{:S(2)}, u32[]{:S(2)}) collective-permute-start(bf16[256,4608]{1,0:T(8,128)(2,1)S(1)} %constant_dynamic-update-slice_fusion.refs_1_), channel_id=1, source_target_pairs={{0,1},{1,0},{2,3},{3,2},{4,5},{5,4},{6,7},{7,6},{8,9},{9,8},{10,11... | collective-permute-start | bytes 7077896 | tf_op jit(solution)/shard_map/ppermute | solution.py:71
  162.5 30.6 %all-to-all-done.5 = bf16[16,32,2304]{2,1,0:T(8,128)(2,1)} async-done(((bf16[16,32,2304]{2,1,0:T(8,128)(2,1)}), bf16[16,32,2304]{2,1,0:T(8,128)(2,1)}, u32[]{:S(2)}, u32[]{:S(2)}) %all-to-all-start.5) | async-done | bytes 2359328 | tf_op jit(solution)/shard_map/all_to_all | solution.py:312
  195.1 3.1 %collective-permute-done.16 = f32[4,9,2,256]{3,1,2,0:T(8,128)S(1)} collective-permute-done((f32[4,9,2,256]{3,1,2,0:T(8,128)S(1)}, f32[4,9,2,256]{3,1,2,0:T(8,128)S(1)}, u32[]{:S(2)}, u32[]{:S(2)}) %collective-permute-start.16) | collective-permute-done | bytes 73760 | tf_op jit(solution)/shard_map/ppermute | solution.py:71
  200.8 12.8 %pulled.1 = bf16[1536,512]{1,0:T(8,128)(2,1)S(1)} custom-call(bf16[3,2304,512]{2,1,0:T(8,128)(2,1)} %get-tuple-element.34.refs_0_, bf16[256,4608]{1,0:T(8,128)(2,1)S(1)} %constant_dynamic-update-slice_fusion.refs_1_, bf16[256,4608]{1,0:T(8,128)(2,1)} %collective-permute-done.13.refs_2_, bf16[256,512]{1,0:T(8,128)(2,1)S(1)} %get-tuple-element.110.refs_3_, ...), custom_call_target="tpu_custom_call" | custom-call | flops 7247757312 | bytes 14000000 | tf_op jit(solution)/shard_map/pulled/pallas_call | solution.py:230
  215.8 4.4 %joined.2.refs_0_ = bf16[9,512,512]{2,1,0:T(8,128)(2,1)} custom-call(s32[1]{0:T(128)} %bitcast.core_ref.refs_0_._, bf16[128,128]{1,0:T(8,128)(2,1)} %constant.153.clone.order_ref, bf16[512,2304]{1,0:T(8,128)(2,1)} %bitcast.17.part_ref), custom_call_target="tpu_custom_call" | custom-call | flops 301989888 | bytes 9437184 | tf_op jit(solution)/shard_map/joined/pallas_call | solution.py:275
  220.3 4.4 %joined.3 = bf16[9,512,512]{2,1,0:T(8,128)(2,1)} custom-call(s32[1]{0:T(128)S(6)} %sub.50._, bf16[128,128]{1,0:T(8,128)(2,1)} %constant.153.clone.order_ref, bf16[512,2304]{1,0:T(8,128)(2,1)} %collective-permute-done.15.part_ref, bf16[9,512,512]{2,1,0:T(8,128)(2,1)} %joined.2.refs_0_), custom_call_target="tpu_custom_call", output_to_operand_aliasing={{}: (3, {})} | custom-call | flops 301989888 | bytes 9437184 | tf_op jit(solution)/shard_map/joined/pallas_call | solution.py:275
  (118 shorter events, 44.9 us)
Async XLA Ops:
  2.4 14.9 %collective-permute-start = (bf16[1,4,96,512]{3,2,1,0:T(8,128)(2,1)S(1)}, bf16[1,4,96,512]{3,2,1,0:T(8,128)(2,1)S(1)}, u32[]{:S(2)}, u32[]{:S(2)}) collective-permute-start(bf16[1,4,96,512]{3,2,1,0:T(8,128)(2,1)S(1)} %pad.15), channel_id=1, source_target_pairs={{0,32},{32,64},{64,96},{96,128},{128,160},{160,192},{192,224},{1,3... | collective-permute-start | bytes 1179656 | tf_op jit(solution)/shard_map/ppermute | solution.py:60
  5.7 11.6 %collective-permute-start.1 = (bf16[1,4,96,512]{3,2,1,0:T(8,128)(2,1)S(1)}, bf16[1,4,96,512]{3,2,1,0:T(8,128)(2,1)S(1)}, u32[]{:S(2)}, u32[]{:S(2)}) collective-permute-start(bf16[1,4,96,512]{3,2,1,0:T(8,128)(2,1)S(1)} %pad.17), channel_id=1, source_target_pairs={{32,0},{64,32},{96,64},{128,96},{160,128},{192,160},{224,192},{33,... | collective-permute-start | bytes 1179656 | tf_op jit(solution)/shard_map/ppermute | solution.py:60
  17.5 8.4 %collective-permute-start.2 = (bf16[6,4,1,512]{3,2,1,0:T(2,128)(2,1)S(1)}, bf16[6,4,1,512]{3,2,1,0:T(2,128)(2,1)S(1)}, u32[]{:S(2)}, u32[]{:S(2)}) collective-permute-start(bf16[6,4,1,512]{3,2,1,0:T(2,128)(2,1)S(1)} %pad_maximum_fusion.2), channel_id=1, source_target_pairs={{0,1},{1,2},{2,3},{3,4},{4,5},{5,6},{6,7},{7,8},{8,9},{9,10},{10,1... | collective-permute-start | bytes 73736 | tf_op jit(solution)/shard_map/ppermute | solution.py:67
  20.9 6.0 %collective-permute-start.3 = (bf16[6,4,1,512]{3,2,1,0:T(2,128)(2,1)S(1)}, bf16[6,4,1,512]{3,2,1,0:T(2,128)(2,1)S(1)}, u32[]{:S(2)}, u32[]{:S(2)}) collective-permute-start(bf16[6,4,1,512]{3,2,1,0:T(2,128)(2,1)S(1)} %pad_maximum_fusion.3), channel_id=1, source_target_pairs={{1,0},{2,1},{3,2},{4,3},{5,4},{6,5},{7,6},{8,7},{9,8},{10,9},{11,1... | collective-permute-start | bytes 73736 | tf_op jit(solution)/shard_map/ppermute | solution.py:67
  27.5 22.7 %copy-start.7 = (f32[2,9,512]{2,0,1:T(2,128)S(1)}, f32[2,9,512]{2,0,1:T(2,128)}, u32[]{:S(2)}) copy-start(f32[2,9,512]{2,0,1:T(2,128)} %param.10) | copy-start | bytes 110596
  39.4 13.1 %collective-permute-start.7 = (bf16[512,1536]{1,0:T(8,128)(2,1)}, bf16[512,1536]{1,0:T(8,128)(2,1)}, u32[]{:S(2)}, u32[]{:S(2)}) collective-permute-start(bf16[512,1536]{1,0:T(8,128)(2,1)} %get-tuple-element.30), channel_id=1, source_target_pairs={{0,1},{1,0},{2,3},{3,2},{4,5},{5,4},{6,7},{7,6},{8,9},{9,8},{10,11... | collective-permute-start | bytes 4718600 | tf_op jit(solution)/shard_map/ppermute | solution.py:71
  40.2 10.7 %collective-permute-start.6 = (bf16[512,768]{1,0:T(8,128)(2,1)S(1)}, bf16[512,768]{1,0:T(8,128)(2,1)}, u32[]{:S(2)}, u32[]{:S(2)}) collective-permute-start(bf16[512,768]{1,0:T(8,128)(2,1)S(1)} %get-tuple-element.28), channel_id=1, source_target_pairs={{0,1},{1,0},{2,3},{3,2},{4,5},{5,4},{6,7},{7,6},{8,9},{9,8},{10,11... | collective-permute-start | bytes 2359304 | tf_op jit(solution)/shard_map/ppermute | solution.py:71
  41.2 15.4 %all-to-all-start = ((bf16[16,2,4608]{2,1,0:T(2,128)(2,1)}), bf16[16,2,4608]{2,1,0:T(2,128)(2,1)S(1)}, u32[]{:S(2)}, u32[]{:S(2)}) async-start(bf16[16,2,4608]{2,1,0:T(2,128)(2,1)} %broadcast_in_dim.26), calls=%async_computation | async-start | bytes 589824 | tf_op jit(solution)/shard_map/all_to_all | solution.py:312
  56.6 40.4 %all-to-all-start.1 = ((bf16[16,32,2304]{2,1,0:T(8,128)(2,1)}), bf16[16,32,2304]{2,1,0:T(8,128)(2,1)}, u32[]{:S(2)}, u32[]{:S(2)}) async-start(bf16[16,32,2304]{2,1,0:T(8,128)(2,1)} %bitcast.14), calls=%async_computation.1 | async-start | bytes 4718592 | tf_op jit(solution)/shard_map/all_to_all | solution.py:378
  63.0 10.4 %collective-permute-start.4 = (bf16[32,4608]{1,0:T(8,128)(2,1)S(1)}, bf16[32,4608]{1,0:T(8,128)(2,1)}, u32[]{:S(2)}, u32[]{:S(2)}) collective-permute-start(bf16[32,4608]{1,0:T(8,128)(2,1)S(1)} %reshape.151), channel_id=1, source_target_pairs={{0,4},{4,8},{8,12},{12,16},{16,20},{20,24},{24,28},{28,0},{1,5},{5... | collective-permute-start | bytes 884744 | tf_op jit(solution)/shard_map/ppermute | solution.py:300
  63.8 9.7 %collective-permute-start.5 = (bf16[32,4608]{1,0:T(8,128)(2,1)S(1)}, bf16[32,4608]{1,0:T(8,128)(2,1)S(1)}, u32[]{:S(2)}, u32[]{:S(2)}) collective-permute-start(bf16[32,4608]{1,0:T(8,128)(2,1)S(1)} %reshape.151), channel_id=1, source_target_pairs={{0,28},{4,0},{8,4},{12,8},{16,12},{20,16},{24,20},{28,24},{1,29},{... | collective-permute-start | bytes 884744 | tf_op jit(solution)/shard_map/ppermute | solution.py:300
  73.4 7.8 %collective-permute-start.8 = (bf16[32,4608]{1,0:T(8,128)(2,1)}, bf16[32,4608]{1,0:T(8,128)(2,1)}, u32[]{:S(2)}, u32[]{:S(2)}) collective-permute-start(bf16[32,4608]{1,0:T(8,128)(2,1)} %collective-permute-done.4), channel_id=1, source_target_pairs={{0,4},{4,8},{8,12},{12,16},{16,20},{20,24},{24,28},{28,0},{1,5},{5... | collective-permute-start | bytes 884744 | tf_op jit(solution)/shard_map/ppermute | solution.py:304
  74.9 5.0 %collective-permute-start.14 = (f32[3,2,9,256]{3,2,1,0:T(8,128)S(1)}, f32[3,2,9,256]{3,2,1,0:T(8,128)S(1)}, u32[]{:S(2)}, u32[]{:S(2)}) collective-permute-start(f32[3,2,9,256]{3,2,1,0:T(8,128)S(1)} %get-tuple-element.108), channel_id=1, source_target_pairs={{0,1},{1,0},{2,3},{3,2},{4,5},{5,4},{6,7},{7,6},{8,9},{9,8},{10,11... | collective-permute-start | bytes 165896 | tf_op jit(solution)/shard_map/ppermute | solution.py:71
  78.7 29.2 %collective-permute-start.11 = (bf16[32,4608]{1,0:T(8,128)(2,1)S(1)}, bf16[32,4608]{1,0:T(8,128)(2,1)S(1)}, u32[]{:S(2)}, u32[]{:S(2)}) collective-permute-start(bf16[32,4608]{1,0:T(8,128)(2,1)S(1)} %collective-permute-done.5), channel_id=1, source_target_pairs={{0,28},{4,0},{8,4},{12,8},{16,12},{20,16},{24,20},{28,24},{1,29},{... | collective-permute-start | bytes 884744 | tf_op jit(solution)/shard_map/ppermute | solution.py:306
  81.2 29.5 %collective-permute-start.9 = (bf16[32,4608]{1,0:T(8,128)(2,1)}, bf16[32,4608]{1,0:T(8,128)(2,1)}, u32[]{:S(2)}, u32[]{:S(2)}) collective-permute-start(bf16[32,4608]{1,0:T(8,128)(2,1)} %collective-permute-done.8), channel_id=1, source_target_pairs={{0,4},{4,8},{8,12},{12,16},{16,20},{20,24},{24,28},{28,0},{1,5},{5... | collective-permute-start | bytes 884744 | tf_op jit(solution)/shard_map/ppermute | solution.py:304
  99.7 15.4 %all-to-all-start.2 = ((bf16[8,4,2304]{2,1,0:T(4,128)(2,1)}), bf16[8,4,2304]{2,1,0:T(4,128)(2,1)S(1)}, u32[]{:S(2)}, u32[]{:S(2)}) async-start(bf16[8,4,2304]{2,1,0:T(4,128)(2,1)} %reshape.154), calls=%async_computation.2 | async-start | bytes 294912 | tf_op jit(solution)/shard_map/all_to_all | solution.py:381
  108.0 50.7 %collective-permute-start.12 = (bf16[32,4608]{1,0:T(8,128)(2,1)S(1)}, bf16[32,4608]{1,0:T(8,128)(2,1)}, u32[]{:S(2)}, u32[]{:S(2)}) collective-permute-start(bf16[32,4608]{1,0:T(8,128)(2,1)S(1)} %collective-permute-done.11), channel_id=1, source_target_pairs={{0,28},{4,0},{8,4},{12,8},{16,12},{20,16},{24,20},{28,24},{1,29},{... | collective-permute-start | bytes 884744 | tf_op jit(solution)/shard_map/ppermute | solution.py:306
  110.7 32.1 %collective-permute-start.10 = (bf16[32,4608]{1,0:T(8,128)(2,1)}, bf16[32,4608]{1,0:T(8,128)(2,1)}, u32[]{:S(2)}, u32[]{:S(2)}) collective-permute-start(bf16[32,4608]{1,0:T(8,128)(2,1)} %collective-permute-done.9), channel_id=1, source_target_pairs={{0,4},{4,8},{8,12},{12,16},{16,20},{20,24},{24,28},{28,0},{1,5},{5... | collective-permute-start | bytes 884744 | tf_op jit(solution)/shard_map/ppermute | solution.py:304
  117.2 19.9 %all-to-all-start.3 = ((f32[256,1,1]{2,1,0:T(1,128)}), f32[256,1,1]{2,1,0:T(1,128)S(1)}, u32[]{:S(2)}, u32[]{:S(2)}) async-start(f32[256,1,1]{2,1,0:T(1,128)} %broadcast_in_dim.27), calls=%async_computation.3 | async-start | bytes 262144 | tf_op jit(solution)/shard_map/all_to_all | solution.py:312
  139.4 11.2 %all-to-all-start.4 = ((bf16[8,4,2304]{2,1,0:T(4,128)(2,1)}), bf16[8,4,2304]{2,1,0:T(4,128)(2,1)S(1)}, u32[]{:S(2)}, u32[]{:S(2)}) async-start(bf16[8,4,2304]{2,1,0:T(4,128)(2,1)} %broadcast_in_dim.28), calls=%async_computation.4 | async-start | bytes 294912 | tf_op jit(solution)/shard_map/all_to_all | solution.py:312
  152.3 40.8 %all-to-all-start.5 = ((bf16[16,32,2304]{2,1,0:T(8,128)(2,1)}), bf16[16,32,2304]{2,1,0:T(8,128)(2,1)}, u32[]{:S(2)}, u32[]{:S(2)}) async-start(bf16[16,32,2304]{2,1,0:T(8,128)(2,1)} %broadcast_in_dim.30), calls=%async_computation.5 | async-start | bytes 4718592 | tf_op jit(solution)/shard_map/all_to_all | solution.py:312
  159.6 41.2 %collective-permute-start.13 = (bf16[256,4608]{1,0:T(8,128)(2,1)S(1)}, bf16[256,4608]{1,0:T(8,128)(2,1)}, u32[]{:S(2)}, u32[]{:S(2)}) collective-permute-start(bf16[256,4608]{1,0:T(8,128)(2,1)S(1)} %constant_dynamic-update-slice_fusion.refs_1_), channel_id=1, source_target_pairs={{0,1},{1,0},{2,3},{3,2},{4,5},{5,4},{6,7},{7,6},{8,9},{9,8},{10,11... | collective-permute-start | bytes 7077896 | tf_op jit(solution)/shard_map/ppermute | solution.py:71
  193.1 27.2 %collective-permute-start.15 = (bf16[512,2304]{1,0:T(8,128)(2,1)}, bf16[512,2304]{1,0:T(8,128)(2,1)}, u32[]{:S(2)}, u32[]{:S(2)}) collective-permute-start(bf16[512,2304]{1,0:T(8,128)(2,1)} %bitcast.17.part_ref), channel_id=1, source_target_pairs={{0,1},{1,0},{2,3},{3,2},{4,5},{5,4},{6,7},{7,6},{8,9},{9,8},{10,11... | collective-permute-start | bytes 7077896 | tf_op jit(solution)/shard_map/ppermute | solution.py:71
  194.1 4.0 %collective-permute-start.16 = (f32[4,9,2,256]{3,1,2,0:T(8,128)S(1)}, f32[4,9,2,256]{3,1,2,0:T(8,128)S(1)}, u32[]{:S(2)}, u32[]{:S(2)}) collective-permute-start(f32[4,9,2,256]{3,1,2,0:T(8,128)S(1)} %get-tuple-element.88), channel_id=1, source_target_pairs={{0,1},{1,0},{2,3},{3,2},{4,5},{5,4},{6,7},{7,6},{8,9},{9,8},{10,11... | collective-permute-start | bytes 221192 | tf_op jit(solution)/shard_map/ppermute | solution.py:71
  (10 other events, 91.3 us)

commit v4 on v2

--- a/solution.py
+++ b/solution.py
@@ -2,6 +2,7 @@
 
 import jax
 import jax.numpy as jnp
+import numpy as np
 from jax import lax
 from jax.experimental import pallas as pl
 from jax.experimental.pallas import tpu as pltpu
@@ -258,7 +259,8 @@
     return new_master, new_one, new_two, clipped
 
 
-def join_kernel(core_ref, order_ref, own_ref, other_ref, out_ref):
+def join_kernel(core_ref, order_ref, own_ref, other_ref, *refs):
+    out_ref = refs[-1]
     half = own_ref.shape[1] // TAPS
     own = pl.multiple_of(core_ref[0] * half, half)
     other = pl.multiple_of((1 - core_ref[0]) * half, half)
@@ -268,23 +270,29 @@
             out_ref[tap, :, pl.ds(lane, half)] = rows[:, index * half : (index + 1) * half]
 
 
-def joined(core, order, own, other):
-    chans, wide = own.shape
+def joined(core, order, own, other, first, out):
+    count, wide = other.shape
     half = wide // TAPS
     block = order.shape[0]
+    operands = (core, order, own, other) if out is None else (core, order, own, other, out)
     return pl.pallas_call(
         join_kernel,
-        grid=(chans // block,),
+        grid=(count // block,),
         in_specs=[
             pl.BlockSpec(memory_space=pltpu.SMEM),
             pl.BlockSpec(order.shape, lambda i: (0, 0)),
+            pl.BlockSpec((block, wide), lambda i: (i + first, 0)),
             pl.BlockSpec((block, wide), lambda i: (i, 0)),
-            pl.BlockSpec((block, wide), lambda i: (i, 0)),
-        ],
-        out_specs=pl.BlockSpec((TAPS, block, 2 * half), lambda i: (0, i, 0)),
-        out_shape=jax.ShapeDtypeStruct((TAPS, chans, 2 * half), BF16),
+            pl.BlockSpec(memory_space=pl.ANY),
+        ][: len(operands)],
+        out_specs=pl.BlockSpec((TAPS, block, 2 * half), lambda i: (0, i + first, 0)),
+        out_shape=jax.ShapeDtypeStruct((TAPS, own.shape[0], 2 * half), BF16),
+        input_output_aliases={} if out is None else {4: 0},
+        cost_estimate=pl.CostEstimate(
+            flops=2 * count * wide * block, bytes_accessed=8 * count * wide, transcendentals=0
+        ),
         name="joined",
-    )(core, order, own, other)
+    )(*operands)
 
 
 def around_ring(chunk, after):
@@ -327,7 +335,6 @@
     extra = padded_cols - lon_cols
     core = lax.axis_index("c")
     core_ref = core.reshape(1).astype(jnp.int32)
-    square = (chans, chans)
 
     def padded(field):
         return jnp.pad(
@@ -339,15 +346,11 @@
 
     above, below = row_halo(padded(upstream[:, :1]), padded(upstream[:, -1:]))
     up_rows = padded(upstream)
-    order = (row_channel(rows_of(square, 0)) == rows_of(square, 1)).astype(BF16)
+    rows = np.arange(chans)
+    order = jnp.asarray(row_channel(rows)[:, None] == rows[None, :], BF16)
     lhs = lax.dot_general(
         order, flat(padded(activations)), (((1,), (1,)), ((), ())), preferred_element_type=F32
     ).astype(BF16)
-    state = jnp.stack([master, moment_one, moment_two])
-    own_state, other_state = halves(state, core)
-    other_state = swap(other_state)
-    state = in_core_order(own_state, other_state, core, 1)
-    state = jnp.stack([state[:, :, tap] for tap in ORDER], axis=2).reshape(12, wide)
     left, right = col_halo((above, up_rows, below), lon_cols - 1)
     pieces = (flat(above), flat(up_rows), flat(below))
     old_piece = master.astype(BF16).reshape(2, TAPS * outs)
@@ -366,6 +369,12 @@
         ],
         axis=1,
     ).reshape(16, 32, wide)
+    *state, pair_sum = lax.optimization_barrier((master, moment_one, moment_two, pair_sum))
+    state = jnp.stack(state)
+    own_state, other_state = halves(state, core)
+    other_state = swap(other_state)
+    state = in_core_order(own_state, other_state, core, 1)
+    state = jnp.stack([state[:, :, tap] for tap in ORDER], axis=2).reshape(12, wide)
     parts = lax.all_to_all(pair_sum, PLANE, 0, 0, tiled=True)
     old_own = around_ring(old_plane, pair_sum)
     plane_sum = jnp.sum(parts.astype(F32), axis=0).astype(BF16).reshape(8, 4, wide)
@@ -379,10 +388,11 @@
     own = to_all(new_line, PLANE, 16).reshape(chans, wide)
 
     results = results.reshape(4, 4, TAPS, half)
-    results = jnp.stack([results[:, :, ORDER.index(tap)] for tap in range(TAPS)], axis=2)
-    mine = jnp.where(core == 0, results[:, :2], results[:, 2:])
-    theirs = jnp.where(core == 0, results[:, 2:], results[:, :2])
+    results = jnp.stack([results[:, :, ORDER.index(tap)] for tap in range(TAPS)], axis=1)
+    mine = jnp.where(core == 0, results[:, :, :2], results[:, :, 2:])
+    theirs = jnp.where(core == 0, results[:, :, 2:], results[:, :, :2])
     results = in_core_order(mine, swap(theirs), core, 3)
+    results = [jnp.transpose(result, (1, 0, 2)) for result in results]
 
     old_other = swap(old_own)
     fields, old_own, old_other, _ = lax.optimization_barrier(
@@ -398,9 +408,13 @@
     input_grad = pulled_rows.reshape(lat_rows, batch, padded_cols, chans)
     input_grad = jnp.transpose(input_grad[:, :, :lon_cols], (1, 0, 2, 3))
 
-    lat_block = (chans // 4, chans // 4)
-    back = (rows_of(lat_block, 0) == row_channel(rows_of(lat_block, 1))).astype(BF16)
-    new_weights = jnp.transpose(joined(core_ref, back, own, swap(own)), (1, 0, 2))
+    rows = np.arange(chans // 4)
+    back = jnp.asarray(rows[:, None] == row_channel(rows)[None, :], BF16)
+    low = swap(own[: chans // 2])
+    high = swap(own[chans // 2 :])
+    out = joined(core_ref, back, own, low, 0, None)
+    out = joined(core_ref, back, own, high, 2, out)
+    new_weights = jnp.transpose(out, (1, 0, 2))
     return (input_grad, new_weights, *results)
 
 

time: 223 us -> 233 us (1.045)
  local copies, waits for them, and re-layouts: 20 us -> 26.2 us
  other arithmetic: 10.4 us -> 15.8 us
  matrix products: 3.98 us -> 1.04 us
    ppermute x4, waiting for transfers between devices: 0.01 us -> 13.7 us  [around_ring(): below.append(lax.ppermute(below[-1], 'z', up))]
    ppermute x3, waiting for transfers between devices: 7.87 us -> 0.01 us  [around_ring(): above.append(lax.ppermute(above[-1], 'z', down))]
    all_to_all x1, waiting for transfers between devices: 13.9 us -> 10.4 us  [per_device(): parts = lax.all_to_all(pair_sum, PLANE, 0, 0, tiled=True)]
    unnamed x38 -> x49, local copies, waits for them, and re-layouts: 11.4 us -> 14.7 us
    dot_general x1, matrix products: 3.98 us -> 1.04 us  [per_device(): lax.dot_general(order, flat(padded(activations)), (((1,), (1,)), ((), ())...]
    slice x0 -> x1, local copies, waits for them, and re-layouts: none -> 2.85 us  [per_device(): low = swap(own[:chans // 2])]
    ppermute x6 -> x7, waiting for transfers between devices: 2.55 us -> 0.02 us  [swap(): return lax.ppermute(array, 'c', [(0, 1), (1, 0)])]
    ppermute x3, starting transfers between devices: 11.9 us -> 9.45 us  [around_ring(): above.append(lax.ppermute(above[-1], 'z', down))]
  transfers between devices with their start and end apart: 23 -> 24, of which waited for: 12 -> 10; matrix products, arithmetic and copies ran while one was open for 14% -> 15% of each run, Pallas kernels for 8% -> 9%
where the time goes in v4:
time: 233 us; the launch traced here: 231 us
  waiting for transfers between devices  84.8 us (36%)
  starting transfers between devices  65.3 us (28%)
  Pallas kernels  35.9 us (15%)
  local copies, waits for them, and re-layouts  26.2 us (11%)
  other arithmetic  15.8 us (7%)
    all_to_all x4, waiting for transfers between devices, to_all(): return lax.all_to_all(copies, axes, 0, 0, tiled=True)  49.5 us
    all_to_all x4, starting transfers between devices, to_all(): return lax.all_to_all(copies, axes, 0, 0, tiled=True)  27 us
    unnamed x49, local copies, waits for them, and re-layouts  14.7 us
    ppermute x4, waiting for transfers between devices, around_ring(): below.append(lax.ppermute(below[-1], 'z', up))  13.7 us
    pallas_call x1, Pallas kernels, pulled(): pl.pallas_call(lambda *refs: pull_kernel(*refs, block=block), grid=(4,),...  12.8 us
    pallas_call x1, Pallas kernels, side_grads(): pl.pallas_call(lambda *refs: side_kernel(*refs, cols=cols, padded_cols=pa...  11.9 us
    all_to_all x1, waiting for transfers between devices, per_device(): parts = lax.all_to_all(pair_sum, PLANE, 0, 0, tiled=True)  10.4 us
    ppermute x3, starting transfers between devices, around_ring(): above.append(lax.ppermute(above[-1], 'z', down))  9.45 us
  transfers between devices with their start and end apart: 24, of which 10 were waited for; matrix products, arithmetic and copies ran while one was open for 15% of the time, Pallas kernels for 9%

profile of v4, /device:TPU:5, one launch (start us, length us, event | category | flops | bytes accessed | tf_op | source)
XLA Modules:
  0.0 231.0 jit_solution(15281997929410979325)
XLA Ops:
  2.4 3.2 %collective-permute-start = (bf16[1,4,96,512]{3,2,1,0:T(8,128)(2,1)S(1)}, bf16[1,4,96,512]{3,2,1,0:T(8,128)(2,1)S(1)}, u32[]{:S(2)}, u32[]{:S(2)}) collective-permute-start(bf16[1,4,96,512]{3,2,1,0:T(8,128)(2,1)S(1)} %pad.15), channel_id=1, source_target_pairs={{0,32},{32,64},{64,96},{96,128},{128,160},{160,192},{192,224},{1,3... | collective-permute-start | bytes 1179656 | tf_op jit(solution)/shard_map/ppermute | solution.py:60
  11.4 6.0 %collective-permute-done.1 = bf16[1,4,96,512]{3,2,1,0:T(8,128)(2,1)S(1)} collective-permute-done((bf16[1,4,96,512]{3,2,1,0:T(8,128)(2,1)S(1)}, bf16[1,4,96,512]{3,2,1,0:T(8,128)(2,1)S(1)}, u32[]{:S(2)}, u32[]{:S(2)}) %collective-permute-start.1) | collective-permute-done | bytes 393248 | tf_op jit(solution)/shard_map/ppermute | solution.py:60
  17.5 3.4 %collective-permute-start.2 = (bf16[6,4,1,512]{3,2,1,0:T(2,128)(2,1)S(1)}, bf16[6,4,1,512]{3,2,1,0:T(2,128)(2,1)S(1)}, u32[]{:S(2)}, u32[]{:S(2)}) collective-permute-start(bf16[6,4,1,512]{3,2,1,0:T(2,128)(2,1)S(1)} %pad_maximum_fusion.2), channel_id=1, source_target_pairs={{0,1},{1,2},{2,3},{3,4},{4,5},{5,6},{6,7},{7,8},{8,9},{9,10},{10,1... | collective-permute-start | bytes 73736 | tf_op jit(solution)/shard_map/ppermute | solution.py:67
  21.0 4.9 %centre_grads.1 = (f32[512,768]{1,0:T(8,128)S(1)}, bf16[512,768]{1,0:T(8,128)(2,1)S(1)}) custom-call(s32[1]{0:T(128)} %bitcast.core_ref.refs_0_, bf16[512,1536]{1,0:T(8,128)(2,1)S(1)} %fusion.lhs_ref.refs_1_, bf16[384,512]{1,0:T(8,128)(2,1)S(1)} %bitcast.84, bf16[1536,512]{1,0:T(8,128)(2,1)} %bitcast.92, bf16[384,512]{1,0:T(8,128)(2,1)S(1)} %bitcast.86), custom_call_target="tpu_custom_call" | custom-call | flops 2415919104 | bytes 8000000 | tf_op jit(solution)/shard_map/centre_grads/pallas_call | solution.py:113
  27.5 11.9 %side_grads.1 = (bf16[3,2304,512]{2,1,0:T(8,128)(2,1)}, f32[512,1536]{1,0:T(8,128)}, bf16[512,1536]{1,0:T(8,128)(2,1)}) custom-call(s32[1]{0:T(128)} %bitcast.core_ref.refs_0_, bf16[512,1536]{1,0:T(8,128)(2,1)} %copy-done.2, bf16[384,512]{1,0:T(8,128)(2,1)} %bitcast.85, bf16[1536,512]{1,0:T(8,128)(2,1)} %bitcast.93, bf16[384,512]{1,0:T(8,128)(2,1)} %bitcast.87, ...), custom_call_target="tpu_custom_call" | custom-call | flops 4831838208 | bytes 16000000 | tf_op jit(solution)/shard_map/side_grads/pallas_call | solution.py:183
  41.2 9.0 %all-to-all-start = ((bf16[16,2,4608]{2,1,0:T(2,128)(2,1)}), bf16[16,2,4608]{2,1,0:T(2,128)(2,1)S(1)}, u32[]{:S(2)}, u32[]{:S(2)}) async-start(bf16[16,2,4608]{2,1,0:T(2,128)(2,1)} %broadcast_in_dim.26), calls=%async_computation | async-start | bytes 589824 | tf_op jit(solution)/shard_map/all_to_all | solution.py:312
  52.5 4.1 %all-to-all-done = bf16[16,2,4608]{2,1,0:T(2,128)(2,1)S(1)} async-done(((bf16[16,2,4608]{2,1,0:T(2,128)(2,1)}), bf16[16,2,4608]{2,1,0:T(2,128)(2,1)S(1)}, u32[]{:S(2)}, u32[]{:S(2)}) %all-to-all-start) | async-done | bytes 294944 | tf_op jit(solution)/shard_map/all_to_all | solution.py:312
  62.4 5.9 %all-to-all-start.1 = ((bf16[16,32,2304]{2,1,0:T(8,128)(2,1)}), bf16[16,32,2304]{2,1,0:T(8,128)(2,1)}, u32[]{:S(2)}, u32[]{:S(2)}) async-start(bf16[16,32,2304]{2,1,0:T(8,128)(2,1)} %bitcast.11), calls=%async_computation.1 | async-start | bytes 4718592 | tf_op jit(solution)/shard_map/all_to_all | solution.py:378
  71.8 4.0 %collective-permute-start.10 = (bf16[32,4608]{1,0:T(8,128)(2,1)S(1)}, bf16[32,4608]{1,0:T(8,128)(2,1)S(1)}, u32[]{:S(2)}, u32[]{:S(2)}) collective-permute-start(bf16[32,4608]{1,0:T(8,128)(2,1)S(1)} %reshape.153), channel_id=1, source_target_pairs={{0,28},{4,0},{8,4},{12,8},{16,12},{20,16},{24,20},{28,24},{1,29},{... | collective-permute-start | bytes 884744 | tf_op jit(solution)/shard_map/ppermute | solution.py:306
  76.2 7.0 %collective-permute-done.6 = bf16[32,4608]{1,0:T(8,128)(2,1)S(1)} collective-permute-done((bf16[32,4608]{1,0:T(8,128)(2,1)S(1)}, bf16[32,4608]{1,0:T(8,128)(2,1)S(1)}, u32[]{:S(2)}, u32[]{:S(2)}) %collective-permute-start.6) | collective-permute-done | bytes 294944 | tf_op jit(solution)/shard_map/ppermute | solution.py:304
  85.9 6.7 %collective-permute-done.7 = bf16[32,4608]{1,0:T(8,128)(2,1)} collective-permute-done((bf16[32,4608]{1,0:T(8,128)(2,1)S(1)}, bf16[32,4608]{1,0:T(8,128)(2,1)}, u32[]{:S(2)}, u32[]{:S(2)}) %collective-permute-start.7) | collective-permute-done | bytes 294944 | tf_op jit(solution)/shard_map/ppermute | solution.py:304
  92.6 10.4 %all-to-all-done.1 = bf16[16,32,2304]{2,1,0:T(8,128)(2,1)} async-done(((bf16[16,32,2304]{2,1,0:T(8,128)(2,1)}), bf16[16,32,2304]{2,1,0:T(8,128)(2,1)}, u32[]{:S(2)}, u32[]{:S(2)}) %all-to-all-start.1) | async-done | bytes 2359328 | tf_op jit(solution)/shard_map/all_to_all | solution.py:378
  105.7 7.3 %all-to-all-start.2 = ((bf16[8,4,2304]{2,1,0:T(4,128)(2,1)}), bf16[8,4,2304]{2,1,0:T(4,128)(2,1)S(1)}, u32[]{:S(2)}, u32[]{:S(2)}) async-start(bf16[8,4,2304]{2,1,0:T(4,128)(2,1)} %reshape.156), calls=%async_computation.2 | async-start | bytes 294912 | tf_op jit(solution)/shard_map/all_to_all | solution.py:381
  116.7 4.3 %all-to-all-done.2 = bf16[8,4,2304]{2,1,0:T(4,128)(2,1)S(1)} async-done(((bf16[8,4,2304]{2,1,0:T(4,128)(2,1)}), bf16[8,4,2304]{2,1,0:T(4,128)(2,1)S(1)}, u32[]{:S(2)}, u32[]{:S(2)}) %all-to-all-start.2) | async-done | bytes 147488 | tf_op jit(solution)/shard_map/all_to_all | solution.py:381
  123.1 8.2 %all-to-all-start.3 = ((f32[256,1,1]{2,1,0:T(1,128)}), f32[256,1,1]{2,1,0:T(1,128)S(1)}, u32[]{:S(2)}, u32[]{:S(2)}) async-start(f32[256,1,1]{2,1,0:T(1,128)} %broadcast_in_dim.27), calls=%async_computation.3 | async-start | bytes 262144 | tf_op jit(solution)/shard_map/all_to_all | solution.py:312
  132.3 9.8 %all-to-all-done.3 = f32[256,1,1]{2,1,0:T(1,128)S(1)} async-done(((f32[256,1,1]{2,1,0:T(1,128)}), f32[256,1,1]{2,1,0:T(1,128)S(1)}, u32[]{:S(2)}, u32[]{:S(2)}) %all-to-all-start.3) | async-done | bytes 1056 | tf_op jit(solution)/shard_map/all_to_all | solution.py:312
  145.0 3.4 %all-to-all-start.4 = ((bf16[8,4,2304]{2,1,0:T(4,128)(2,1)}), bf16[8,4,2304]{2,1,0:T(4,128)(2,1)S(1)}, u32[]{:S(2)}, u32[]{:S(2)}) async-start(bf16[8,4,2304]{2,1,0:T(4,128)(2,1)} %broadcast_in_dim.28), calls=%async_computation.4 | async-start | bytes 294912 | tf_op jit(solution)/shard_map/all_to_all | solution.py:312
  149.4 6.8 %all-to-all-done.4 = bf16[8,4,2304]{2,1,0:T(4,128)(2,1)S(1)} async-done(((bf16[8,4,2304]{2,1,0:T(4,128)(2,1)}), bf16[8,4,2304]{2,1,0:T(4,128)(2,1)S(1)}, u32[]{:S(2)}, u32[]{:S(2)}) %all-to-all-start.4) | async-done | bytes 147488 | tf_op jit(solution)/shard_map/all_to_all | solution.py:312
  157.9 6.4 %all-to-all-start.5 = ((bf16[16,32,2304]{2,1,0:T(8,128)(2,1)}), bf16[16,32,2304]{2,1,0:T(8,128)(2,1)}, u32[]{:S(2)}, u32[]{:S(2)}) async-start(bf16[16,32,2304]{2,1,0:T(8,128)(2,1)} %broadcast_in_dim.30), calls=%async_computation.5 | async-start | bytes 4718592 | tf_op jit(solution)/shard_map/all_to_all | solution.py:312
  170.1 28.7 %all-to-all-done.5 = bf16[16,32,2304]{2,1,0:T(8,128)(2,1)} async-done(((bf16[16,32,2304]{2,1,0:T(8,128)(2,1)}), bf16[16,32,2304]{2,1,0:T(8,128)(2,1)}, u32[]{:S(2)}, u32[]{:S(2)}) %all-to-all-start.5) | async-done | bytes 2359328 | tf_op jit(solution)/shard_map/all_to_all | solution.py:312
  198.8 2.9 %fusion.33 = (bf16[8,32,2304]{2,1,0:T(8,128)(2,1)S(1)}, bf16[8,32,2304]{2,1,0:T(8,128)(2,1)}) fusion(bf16[16,32,2304]{2,1,0:T(8,128)(2,1)} %all-to-all-done.5), kind=kLoop, calls=%fused_computation.115 | loop fusion | bytes 4718592 | tf_op jit(solution)/shard_map/slice | solution.py:413
  207.5 12.8 %pulled.1 = bf16[1536,512]{1,0:T(8,128)(2,1)S(1)} custom-call(bf16[3,2304,512]{2,1,0:T(8,128)(2,1)} %get-tuple-element.32.refs_0_, bf16[256,4608]{1,0:T(8,128)(2,1)S(1)} %constant_dynamic-update-slice_fusion.refs_1_, bf16[256,4608]{1,0:T(8,128)(2,1)} %collective-permute-done.13.refs_2_, bf16[256,512]{1,0:T(8,128)(2,1)S(1)} %get-tuple-element.112.refs_3_, ...), custom_call_target="tpu_custom_call" | custom-call | flops 7247757312 | bytes 14000000 | tf_op jit(solution)/shard_map/pulled/pallas_call | solution.py:230
  223.5 3.2 %joined.2.refs_0_ = bf16[9,512,512]{2,1,0:T(8,128)(2,1)} custom-call(s32[1]{0:T(128)} %bitcast.core_ref.refs_0_, bf16[128,128]{1,0:T(8,128)(2,1)} %constant.151.clone.order_ref, bf16[512,2304]{1,0:T(8,128)(2,1)} %bitcast.17.own_ref, bf16[256,2304]{1,0:T(8,128)(2,1)} %copy-done.5), custom_call_target="tpu_custom_call" | custom-call | flops 150994944 | bytes 4718592 | tf_op jit(solution)/shard_map/joined/pallas_call | solution.py:278
  227.8 3.2 %joined.3 = bf16[9,512,512]{2,1,0:T(8,128)(2,1)} custom-call(s32[1]{0:T(128)} %bitcast.core_ref.refs_0_, bf16[128,128]{1,0:T(8,128)(2,1)} %constant.151.clone.order_ref, bf16[512,2304]{1,0:T(8,128)(2,1)} %bitcast.17.own_ref, bf16[256,2304]{1,0:T(8,128)(2,1)} %copy-done.4, bf16[9,512,512]{2,1,0:T(8,128)(2,1)} %joined.2.refs_0_), custom_call_target="tpu_custom_call", output_to_operand_aliasing={{}: (4, {})} | custom-call | flops 150994944 | bytes 4718592 | tf_op jit(solution)/shard_map/joined/pallas_call | solution.py:278
  (131 shorter events, 55.8 us)
Async XLA Ops:
  2.4 14.9 %collective-permute-start = (bf16[1,4,96,512]{3,2,1,0:T(8,128)(2,1)S(1)}, bf16[1,4,96,512]{3,2,1,0:T(8,128)(2,1)S(1)}, u32[]{:S(2)}, u32[]{:S(2)}) collective-permute-start(bf16[1,4,96,512]{3,2,1,0:T(8,128)(2,1)S(1)} %pad.15), channel_id=1, source_target_pairs={{0,32},{32,64},{64,96},{96,128},{128,160},{160,192},{192,224},{1,3... | collective-permute-start | bytes 1179656 | tf_op jit(solution)/shard_map/ppermute | solution.py:60
  5.7 11.6 %collective-permute-start.1 = (bf16[1,4,96,512]{3,2,1,0:T(8,128)(2,1)S(1)}, bf16[1,4,96,512]{3,2,1,0:T(8,128)(2,1)S(1)}, u32[]{:S(2)}, u32[]{:S(2)}) collective-permute-start(bf16[1,4,96,512]{3,2,1,0:T(8,128)(2,1)S(1)} %pad.17), channel_id=1, source_target_pairs={{32,0},{64,32},{96,64},{128,96},{160,128},{192,160},{224,192},{33,... | collective-permute-start | bytes 1179656 | tf_op jit(solution)/shard_map/ppermute | solution.py:60
  17.5 8.4 %collective-permute-start.2 = (bf16[6,4,1,512]{3,2,1,0:T(2,128)(2,1)S(1)}, bf16[6,4,1,512]{3,2,1,0:T(2,128)(2,1)S(1)}, u32[]{:S(2)}, u32[]{:S(2)}) collective-permute-start(bf16[6,4,1,512]{3,2,1,0:T(2,128)(2,1)S(1)} %pad_maximum_fusion.2), channel_id=1, source_target_pairs={{0,1},{1,2},{2,3},{3,4},{4,5},{5,6},{6,7},{7,8},{8,9},{9,10},{10,1... | collective-permute-start | bytes 73736 | tf_op jit(solution)/shard_map/ppermute | solution.py:67
  20.9 6.0 %collective-permute-start.3 = (bf16[6,4,1,512]{3,2,1,0:T(2,128)(2,1)S(1)}, bf16[6,4,1,512]{3,2,1,0:T(2,128)(2,1)S(1)}, u32[]{:S(2)}, u32[]{:S(2)}) collective-permute-start(bf16[6,4,1,512]{3,2,1,0:T(2,128)(2,1)S(1)} %pad_maximum_fusion.3), channel_id=1, source_target_pairs={{1,0},{2,1},{3,2},{4,3},{5,4},{6,5},{7,6},{8,7},{9,8},{10,9},{11,1... | collective-permute-start | bytes 73736 | tf_op jit(solution)/shard_map/ppermute | solution.py:67
  39.4 18.8 %collective-permute-start.5 = (bf16[512,1536]{1,0:T(8,128)(2,1)}, bf16[512,1536]{1,0:T(8,128)(2,1)}, u32[]{:S(2)}, u32[]{:S(2)}) collective-permute-start(bf16[512,1536]{1,0:T(8,128)(2,1)} %get-tuple-element.29), channel_id=1, source_target_pairs={{0,1},{1,0},{2,3},{3,2},{4,5},{5,4},{6,7},{7,6},{8,9},{9,8},{10,11... | collective-permute-start | bytes 4718600 | tf_op jit(solution)/shard_map/ppermute | solution.py:71
  40.2 16.5 %collective-permute-start.4 = (bf16[512,768]{1,0:T(8,128)(2,1)S(1)}, bf16[512,768]{1,0:T(8,128)(2,1)}, u32[]{:S(2)}, u32[]{:S(2)}) collective-permute-start(bf16[512,768]{1,0:T(8,128)(2,1)S(1)} %get-tuple-element.27), channel_id=1, source_target_pairs={{0,1},{1,0},{2,3},{3,2},{4,5},{5,4},{6,7},{7,6},{8,9},{9,8},{10,11... | collective-permute-start | bytes 2359304 | tf_op jit(solution)/shard_map/ppermute | solution.py:71
  41.2 15.4 %all-to-all-start = ((bf16[16,2,4608]{2,1,0:T(2,128)(2,1)}), bf16[16,2,4608]{2,1,0:T(2,128)(2,1)S(1)}, u32[]{:S(2)}, u32[]{:S(2)}) async-start(bf16[16,2,4608]{2,1,0:T(2,128)(2,1)} %broadcast_in_dim.26), calls=%async_computation | async-start | bytes 589824 | tf_op jit(solution)/shard_map/all_to_all | solution.py:312
  62.4 40.5 %all-to-all-start.1 = ((bf16[16,32,2304]{2,1,0:T(8,128)(2,1)}), bf16[16,32,2304]{2,1,0:T(8,128)(2,1)}, u32[]{:S(2)}, u32[]{:S(2)}) async-start(bf16[16,32,2304]{2,1,0:T(8,128)(2,1)} %bitcast.11), calls=%async_computation.1 | async-start | bytes 4718592 | tf_op jit(solution)/shard_map/all_to_all | solution.py:378
  68.4 7.4 %collective-permute-start.14 = (f32[3,2,9,256]{3,2,1,0:T(8,128)S(1)}, f32[3,2,9,256]{3,2,1,0:T(8,128)S(1)}, u32[]{:S(2)}, u32[]{:S(2)}) collective-permute-start(f32[3,2,9,256]{3,2,1,0:T(8,128)S(1)} %get-tuple-element.110), channel_id=1, source_target_pairs={{0,1},{1,0},{2,3},{3,2},{4,5},{5,4},{6,7},{7,6},{8,9},{9,8},{10,11... | collective-permute-start | bytes 165896 | tf_op jit(solution)/shard_map/ppermute | solution.py:71
  70.8 12.4 %collective-permute-start.6 = (bf16[32,4608]{1,0:T(8,128)(2,1)S(1)}, bf16[32,4608]{1,0:T(8,128)(2,1)S(1)}, u32[]{:S(2)}, u32[]{:S(2)}) collective-permute-start(bf16[32,4608]{1,0:T(8,128)(2,1)S(1)} %reshape.153), channel_id=1, source_target_pairs={{0,4},{4,8},{8,12},{12,16},{16,20},{20,24},{24,28},{28,0},{1,5},{5... | collective-permute-start | bytes 884744 | tf_op jit(solution)/shard_map/ppermute | solution.py:304
  71.8 11.4 %collective-permute-start.10 = (bf16[32,4608]{1,0:T(8,128)(2,1)S(1)}, bf16[32,4608]{1,0:T(8,128)(2,1)S(1)}, u32[]{:S(2)}, u32[]{:S(2)}) collective-permute-start(bf16[32,4608]{1,0:T(8,128)(2,1)S(1)} %reshape.153), channel_id=1, source_target_pairs={{0,28},{4,0},{8,4},{12,8},{16,12},{20,16},{24,20},{28,24},{1,29},{... | collective-permute-start | bytes 884744 | tf_op jit(solution)/shard_map/ppermute | solution.py:306
  83.2 9.4 %collective-permute-start.7 = (bf16[32,4608]{1,0:T(8,128)(2,1)S(1)}, bf16[32,4608]{1,0:T(8,128)(2,1)}, u32[]{:S(2)}, u32[]{:S(2)}) collective-permute-start(bf16[32,4608]{1,0:T(8,128)(2,1)S(1)} %collective-permute-done.6), channel_id=1, source_target_pairs={{0,4},{4,8},{8,12},{12,16},{16,20},{20,24},{24,28},{28,0},{1,5},{5... | collective-permute-start | bytes 884744 | tf_op jit(solution)/shard_map/ppermute | solution.py:304
  83.2 30.7 %collective-permute-start.11 = (bf16[32,4608]{1,0:T(8,128)(2,1)S(1)}, bf16[32,4608]{1,0:T(8,128)(2,1)S(1)}, u32[]{:S(2)}, u32[]{:S(2)}) collective-permute-start(bf16[32,4608]{1,0:T(8,128)(2,1)S(1)} %collective-permute-done.10), channel_id=1, source_target_pairs={{0,28},{4,0},{8,4},{12,8},{16,12},{20,16},{24,20},{28,24},{1,29},{... | collective-permute-start | bytes 884744 | tf_op jit(solution)/shard_map/ppermute | solution.py:306
  92.6 24.1 %collective-permute-start.8 = (bf16[32,4608]{1,0:T(8,128)(2,1)}, bf16[32,4608]{1,0:T(8,128)(2,1)}, u32[]{:S(2)}, u32[]{:S(2)}) collective-permute-start(bf16[32,4608]{1,0:T(8,128)(2,1)} %collective-permute-done.7), channel_id=1, source_target_pairs={{0,4},{4,8},{8,12},{12,16},{16,20},{20,24},{24,28},{28,0},{1,5},{5... | collective-permute-start | bytes 884744 | tf_op jit(solution)/shard_map/ppermute | solution.py:304
  105.7 15.3 %all-to-all-start.2 = ((bf16[8,4,2304]{2,1,0:T(4,128)(2,1)}), bf16[8,4,2304]{2,1,0:T(4,128)(2,1)S(1)}, u32[]{:S(2)}, u32[]{:S(2)}) async-start(bf16[8,4,2304]{2,1,0:T(4,128)(2,1)} %reshape.156), calls=%async_computation.2 | async-start | bytes 294912 | tf_op jit(solution)/shard_map/all_to_all | solution.py:381
  113.9 50.4 %collective-permute-start.12 = (bf16[32,4608]{1,0:T(8,128)(2,1)S(1)}, bf16[32,4608]{1,0:T(8,128)(2,1)}, u32[]{:S(2)}, u32[]{:S(2)}) collective-permute-start(bf16[32,4608]{1,0:T(8,128)(2,1)S(1)} %collective-permute-done.11), channel_id=1, source_target_pairs={{0,28},{4,0},{8,4},{12,8},{16,12},{20,16},{24,20},{28,24},{1,29},{... | collective-permute-start | bytes 884744 | tf_op jit(solution)/shard_map/ppermute | solution.py:306
  116.7 31.7 %collective-permute-start.9 = (bf16[32,4608]{1,0:T(8,128)(2,1)}, bf16[32,4608]{1,0:T(8,128)(2,1)}, u32[]{:S(2)}, u32[]{:S(2)}) collective-permute-start(bf16[32,4608]{1,0:T(8,128)(2,1)} %collective-permute-done.8), channel_id=1, source_target_pairs={{0,4},{4,8},{8,12},{12,16},{16,20},{20,24},{24,28},{28,0},{1,5},{5... | collective-permute-start | bytes 884744 | tf_op jit(solution)/shard_map/ppermute | solution.py:304
  123.1 19.0 %all-to-all-start.3 = ((f32[256,1,1]{2,1,0:T(1,128)}), f32[256,1,1]{2,1,0:T(1,128)S(1)}, u32[]{:S(2)}, u32[]{:S(2)}) async-start(f32[256,1,1]{2,1,0:T(1,128)} %broadcast_in_dim.27), calls=%async_computation.3 | async-start | bytes 262144 | tf_op jit(solution)/shard_map/all_to_all | solution.py:312
  145.0 11.2 %all-to-all-start.4 = ((bf16[8,4,2304]{2,1,0:T(4,128)(2,1)}), bf16[8,4,2304]{2,1,0:T(4,128)(2,1)S(1)}, u32[]{:S(2)}, u32[]{:S(2)}) async-start(bf16[8,4,2304]{2,1,0:T(4,128)(2,1)} %broadcast_in_dim.28), calls=%async_computation.4 | async-start | bytes 294912 | tf_op jit(solution)/shard_map/all_to_all | solution.py:312
  157.9 40.9 %all-to-all-start.5 = ((bf16[16,32,2304]{2,1,0:T(8,128)(2,1)}), bf16[16,32,2304]{2,1,0:T(8,128)(2,1)}, u32[]{:S(2)}, u32[]{:S(2)}) async-start(bf16[16,32,2304]{2,1,0:T(8,128)(2,1)} %broadcast_in_dim.30), calls=%async_computation.5 | async-start | bytes 4718592 | tf_op jit(solution)/shard_map/all_to_all | solution.py:312
  165.4 42.1 %collective-permute-start.13 = (bf16[256,4608]{1,0:T(8,128)(2,1)S(1)}, bf16[256,4608]{1,0:T(8,128)(2,1)}, u32[]{:S(2)}, u32[]{:S(2)}) collective-permute-start(bf16[256,4608]{1,0:T(8,128)(2,1)S(1)} %constant_dynamic-update-slice_fusion.refs_1_), channel_id=1, source_target_pairs={{0,1},{1,0},{2,3},{3,2},{4,5},{5,4},{6,7},{7,6},{8,9},{9,8},{10,11... | collective-permute-start | bytes 7077896 | tf_op jit(solution)/shard_map/ppermute | solution.py:71
  170.0 33.7 %collective-permute-start.17 = (f32[4,9,2,256]{3,1,2,0:T(8,128)}, f32[4,9,2,256]{3,1,2,0:T(8,128)}, u32[]{:S(2)}, u32[]{:S(2)}) collective-permute-start(f32[4,9,2,256]{3,1,2,0:T(8,128)} %get-tuple-element.90), channel_id=1, source_target_pairs={{0,1},{1,0},{2,3},{3,2},{4,5},{5,4},{6,7},{7,6},{8,9},{9,8},{10,11... | collective-permute-start | bytes 221192 | tf_op jit(solution)/shard_map/ppermute | solution.py:71
  201.7 25.0 %collective-permute-start.15 = (bf16[256,2304]{1,0:T(8,128)(2,1)}, bf16[256,2304]{1,0:T(8,128)(2,1)S(1)}, u32[]{:S(2)}, u32[]{:S(2)}) collective-permute-start(bf16[256,2304]{1,0:T(8,128)(2,1)} %bitcast.18), channel_id=1, source_target_pairs={{0,1},{1,0},{2,3},{3,2},{4,5},{5,4},{6,7},{7,6},{8,9},{9,8},{10,11... | collective-permute-start | bytes 3538952 | tf_op jit(solution)/shard_map/ppermute | solution.py:71
  202.2 20.3 %collective-permute-start.16 = (bf16[256,2304]{1,0:T(8,128)(2,1)S(1)}, bf16[256,2304]{1,0:T(8,128)(2,1)S(1)}, u32[]{:S(2)}, u32[]{:S(2)}) collective-permute-start(bf16[256,2304]{1,0:T(8,128)(2,1)S(1)} %bitcast.96), channel_id=1, source_target_pairs={{0,1},{1,0},{2,3},{3,2},{4,5},{5,4},{6,7},{7,6},{8,9},{9,8},{10,11... | collective-permute-start | bytes 3538952 | tf_op jit(solution)/shard_map/ppermute | solution.py:71
  (16 other events, 171.1 us)

commit v5 on v2

--- a/solution.py
+++ b/solution.py
@@ -2,6 +2,7 @@
 
 import jax
 import jax.numpy as jnp
+import numpy as np
 from jax import lax
 from jax.experimental import pallas as pl
 from jax.experimental.pallas import tpu as pltpu
@@ -327,7 +328,6 @@
     extra = padded_cols - lon_cols
     core = lax.axis_index("c")
     core_ref = core.reshape(1).astype(jnp.int32)
-    square = (chans, chans)
 
     def padded(field):
         return jnp.pad(
@@ -339,15 +339,11 @@
 
     above, below = row_halo(padded(upstream[:, :1]), padded(upstream[:, -1:]))
     up_rows = padded(upstream)
-    order = (row_channel(rows_of(square, 0)) == rows_of(square, 1)).astype(BF16)
+    rows = np.arange(chans)
+    order = jnp.asarray(row_channel(rows)[:, None] == rows[None, :], BF16)
     lhs = lax.dot_general(
         order, flat(padded(activations)), (((1,), (1,)), ((), ())), preferred_element_type=F32
     ).astype(BF16)
-    state = jnp.stack([master, moment_one, moment_two])
-    own_state, other_state = halves(state, core)
-    other_state = swap(other_state)
-    state = in_core_order(own_state, other_state, core, 1)
-    state = jnp.stack([state[:, :, tap] for tap in ORDER], axis=2).reshape(12, wide)
     left, right = col_halo((above, up_rows, below), lon_cols - 1)
     pieces = (flat(above), flat(up_rows), flat(below))
     old_piece = master.astype(BF16).reshape(2, TAPS * outs)
@@ -366,23 +362,32 @@
         ],
         axis=1,
     ).reshape(16, 32, wide)
+    *state, pair_sum = lax.optimization_barrier((master, moment_one, moment_two, pair_sum))
+    state = jnp.stack(state)
+    own_state, other_state = halves(state, core)
+    other_state = swap(other_state)
+    state = in_core_order(own_state, other_state, core, 1)
+    state = jnp.stack([state[:, :, tap] for tap in ORDER], axis=2).reshape(12, wide)
     parts = lax.all_to_all(pair_sum, PLANE, 0, 0, tiled=True)
     old_own = around_ring(old_plane, pair_sum)
     plane_sum = jnp.sum(parts.astype(F32), axis=0).astype(BF16).reshape(8, 4, wide)
     parts = lax.all_to_all(plane_sum, ("z",), 0, 0, tiled=True)
     grad = jnp.sum(parts.astype(F32), axis=0)
 
-    square_sum = jnp.sum(to_all(jnp.sum(grad * grad).reshape(1, 1), ALL, 256)).reshape(1, 1)
+    square_sum = jnp.sum(grad * grad).reshape(1, 1)
+    square_sum = square_sum + swap(square_sum)
+    square_sum = jnp.sum(to_all(square_sum, ("xl", "y", "z", "xh"), 128)).reshape(1, 1)
     clip = clip_factor(square_sum, math.sqrt(float(chans * TAPS * outs)))
     results = jnp.stack(adam(clip, grad, *state.reshape(3, 4, wide)))
     new_line = to_all(results[0].astype(BF16), ("z",), 8).reshape(32, wide)
     own = to_all(new_line, PLANE, 16).reshape(chans, wide)
 
     results = results.reshape(4, 4, TAPS, half)
-    results = jnp.stack([results[:, :, ORDER.index(tap)] for tap in range(TAPS)], axis=2)
-    mine = jnp.where(core == 0, results[:, :2], results[:, 2:])
-    theirs = jnp.where(core == 0, results[:, 2:], results[:, :2])
+    results = jnp.stack([results[:, :, ORDER.index(tap)] for tap in range(TAPS)], axis=1)
+    mine = jnp.where(core == 0, results[:, :, :2], results[:, :, 2:])
+    theirs = jnp.where(core == 0, results[:, :, 2:], results[:, :, :2])
     results = in_core_order(mine, swap(theirs), core, 3)
+    results = [jnp.transpose(result, (1, 0, 2)) for result in results]
 
     old_other = swap(old_own)
     fields, old_own, old_other, _ = lax.optimization_barrier(
@@ -398,9 +403,10 @@
     input_grad = pulled_rows.reshape(lat_rows, batch, padded_cols, chans)
     input_grad = jnp.transpose(input_grad[:, :, :lon_cols], (1, 0, 2, 3))
 
-    lat_block = (chans // 4, chans // 4)
-    back = (rows_of(lat_block, 0) == row_channel(rows_of(lat_block, 1))).astype(BF16)
-    new_weights = jnp.transpose(joined(core_ref, back, own, swap(own)), (1, 0, 2))
+    rows = np.arange(chans // 2)
+    back = jnp.asarray(rows[:, None] == row_channel(rows)[None, :], BF16)
+    out = joined(core_ref, back, own, swap(own))
+    new_weights = jnp.transpose(out, (1, 0, 2))
     return (input_grad, new_weights, *results)
 
 

time: 223 us -> 227 us (1.018)
  waiting for transfers between devices: 83.5 us -> 87.2 us
  matrix products: 3.98 us -> 1.01 us
  starting transfers between devices: 66.6 us -> 69.1 us
    ppermute x6 -> x7, starting transfers between devices: 5.11 us -> 10.8 us  [swap(): return lax.ppermute(array, 'c', [(0, 1), (1, 0)])]
    ppermute x3, waiting for transfers between devices: 7.87 us -> 2.65 us  [around_ring(): above.append(lax.ppermute(above[-1], 'z', down))]
    all_to_all x4, waiting for transfers between devices: 47.3 us -> 51.5 us  [to_all(): return lax.all_to_all(copies, axes, 0, 0, tiled=True)]
    all_to_all x4, starting transfers between devices: 27.2 us -> 24 us  [to_all(): return lax.all_to_all(copies, axes, 0, 0, tiled=True)]
    unnamed x38 -> x39, local copies, waits for them, and re-layouts: 11.4 us -> 14.4 us
    dot_general x1, matrix products: 3.98 us -> 1.01 us  [per_device(): lax.dot_general(order, flat(padded(activations)), (((1,), (1,)), ((), ())...]
    ppermute x6 -> x7, waiting for transfers between devices: 2.55 us -> 5.07 us  [swap(): return lax.ppermute(array, 'c', [(0, 1), (1, 0)])]
  transfers between devices with their start and end apart: 23 -> 24, of which waited for: 12 -> 14; matrix products, arithmetic and copies ran while one was open for 14% -> 11% of each run, Pallas kernels for 8% -> 8%
where the time goes in v5:
time: 227 us; the launch traced here: 226 us
  waiting for transfers between devices  87.2 us (38%)
  starting transfers between devices  69.1 us (30%)
  Pallas kernels  34.2 us (15%)
  local copies, waits for them, and re-layouts  21.3 us (9%)
  other arithmetic  9.68 us (4%)
  between operations  3.1 us (1%)
    all_to_all x4, waiting for transfers between devices, to_all(): return lax.all_to_all(copies, axes, 0, 0, tiled=True)  51.5 us
    all_to_all x4, starting transfers between devices, to_all(): return lax.all_to_all(copies, axes, 0, 0, tiled=True)  24 us
    all_to_all x1, waiting for transfers between devices, per_device(): parts = lax.all_to_all(pair_sum, PLANE, 0, 0, tiled=True)  15 us
    unnamed x39, local copies, waits for them, and re-layouts  14.4 us
    pallas_call x1, Pallas kernels, pulled(): pl.pallas_call(lambda *refs: pull_kernel(*refs, block=block), grid=(4,),...  12.8 us
    pallas_call x1, Pallas kernels, side_grads(): pl.pallas_call(lambda *refs: side_kernel(*refs, cols=cols, padded_cols=pa...  11.9 us
    ppermute x3, starting transfers between devices, around_ring(): above.append(lax.ppermute(above[-1], 'z', down))  11.6 us
    ppermute x7, starting transfers between devices, swap(): return lax.ppermute(array, 'c', [(0, 1), (1, 0)])  10.8 us
  transfers between devices with their start and end apart: 24, of which 14 were waited for; matrix products, arithmetic and copies ran while one was open for 11% of the time, Pallas kernels for 8%

profile of v5, /device:TPU:5, one launch (start us, length us, event | category | flops | bytes accessed | tf_op | source)
XLA Modules:
  0.0 225.5 jit_solution(6113160183220535044)
XLA Ops:
  2.5 3.2 %collective-permute-start = (bf16[1,4,96,512]{3,2,1,0:T(8,128)(2,1)S(1)}, bf16[1,4,96,512]{3,2,1,0:T(8,128)(2,1)S(1)}, u32[]{:S(2)}, u32[]{:S(2)}) collective-permute-start(bf16[1,4,96,512]{3,2,1,0:T(8,128)(2,1)S(1)} %pad.15), channel_id=1, source_target_pairs={{0,32},{32,64},{64,96},{96,128},{128,160},{160,192},{192,224},{1,3... | collective-permute-start | bytes 1179656 | tf_op jit(solution)/shard_map/ppermute | solution.py:60
  13.5 3.9 %collective-permute-done.1 = bf16[1,4,96,512]{3,2,1,0:T(8,128)(2,1)S(1)} collective-permute-done((bf16[1,4,96,512]{3,2,1,0:T(8,128)(2,1)S(1)}, bf16[1,4,96,512]{3,2,1,0:T(8,128)(2,1)S(1)}, u32[]{:S(2)}, u32[]{:S(2)}) %collective-permute-start.1) | collective-permute-done | bytes 393248 | tf_op jit(solution)/shard_map/ppermute | solution.py:60
  17.5 3.4 %collective-permute-start.2 = (bf16[6,4,1,512]{3,2,1,0:T(2,128)(2,1)S(1)}, bf16[6,4,1,512]{3,2,1,0:T(2,128)(2,1)S(1)}, u32[]{:S(2)}, u32[]{:S(2)}) collective-permute-start(bf16[6,4,1,512]{3,2,1,0:T(2,128)(2,1)S(1)} %pad_maximum_fusion.2), channel_id=1, source_target_pairs={{0,1},{1,2},{2,3},{3,4},{4,5},{5,6},{6,7},{7,8},{8,9},{9,10},{10,1... | collective-permute-start | bytes 73736 | tf_op jit(solution)/shard_map/ppermute | solution.py:67
  21.0 4.9 %centre_grads.1 = (f32[512,768]{1,0:T(8,128)S(1)}, bf16[512,768]{1,0:T(8,128)(2,1)S(1)}) custom-call(s32[1]{0:T(128)} %bitcast.core_ref.refs_0_, bf16[512,1536]{1,0:T(8,128)(2,1)S(1)} %fusion.lhs_ref.refs_1_, bf16[384,512]{1,0:T(8,128)(2,1)S(1)} %bitcast.84, bf16[1536,512]{1,0:T(8,128)(2,1)} %bitcast.92, bf16[384,512]{1,0:T(8,128)(2,1)S(1)} %bitcast.86), custom_call_target="tpu_custom_call" | custom-call | flops 2415919104 | bytes 8000000 | tf_op jit(solution)/shard_map/centre_grads/pallas_call | solution.py:113
  27.5 11.9 %side_grads.1 = (bf16[3,2304,512]{2,1,0:T(8,128)(2,1)}, f32[512,1536]{1,0:T(8,128)}, bf16[512,1536]{1,0:T(8,128)(2,1)}) custom-call(s32[1]{0:T(128)} %bitcast.core_ref.refs_0_, bf16[512,1536]{1,0:T(8,128)(2,1)} %copy-done.2, bf16[384,512]{1,0:T(8,128)(2,1)} %bitcast.85, bf16[1536,512]{1,0:T(8,128)(2,1)} %bitcast.93, bf16[384,512]{1,0:T(8,128)(2,1)} %bitcast.87, ...), custom_call_target="tpu_custom_call" | custom-call | flops 4831838208 | bytes 16000000 | tf_op jit(solution)/shard_map/side_grads/pallas_call | solution.py:183
  41.2 9.0 %all-to-all-start = ((bf16[16,2,4608]{2,1,0:T(2,128)(2,1)}), bf16[16,2,4608]{2,1,0:T(2,128)(2,1)S(1)}, u32[]{:S(2)}, u32[]{:S(2)}) async-start(bf16[16,2,4608]{2,1,0:T(2,128)(2,1)} %broadcast_in_dim.29), calls=%async_computation | async-start | bytes 589824 | tf_op jit(solution)/shard_map/all_to_all | solution.py:305
  50.2 6.4 %all-to-all-done = bf16[16,2,4608]{2,1,0:T(2,128)(2,1)S(1)} async-done(((bf16[16,2,4608]{2,1,0:T(2,128)(2,1)}), bf16[16,2,4608]{2,1,0:T(2,128)(2,1)S(1)}, u32[]{:S(2)}, u32[]{:S(2)}) %all-to-all-start) | async-done | bytes 294944 | tf_op jit(solution)/shard_map/all_to_all | solution.py:305
  62.4 5.9 %all-to-all-start.1 = ((bf16[16,32,2304]{2,1,0:T(8,128)(2,1)}), bf16[16,32,2304]{2,1,0:T(8,128)(2,1)}, u32[]{:S(2)}, u32[]{:S(2)}) async-start(bf16[16,32,2304]{2,1,0:T(8,128)(2,1)} %bitcast.11), calls=%async_computation.1 | async-start | bytes 4718592 | tf_op jit(solution)/shard_map/all_to_all | solution.py:371
  68.3 4.6 %collective-permute-start.10 = (bf16[32,4608]{1,0:T(8,128)(2,1)S(1)}, bf16[32,4608]{1,0:T(8,128)(2,1)S(1)}, u32[]{:S(2)}, u32[]{:S(2)}) collective-permute-start(bf16[32,4608]{1,0:T(8,128)(2,1)S(1)} %reshape.154), channel_id=1, source_target_pairs={{0,28},{4,0},{8,4},{12,8},{16,12},{20,16},{24,20},{28,24},{1,29},{... | collective-permute-start | bytes 884744 | tf_op jit(solution)/shard_map/ppermute | solution.py:299
  77.0 3.5 %collective-permute-start.11 = (bf16[32,4608]{1,0:T(8,128)(2,1)S(1)}, bf16[32,4608]{1,0:T(8,128)(2,1)}, u32[]{:S(2)}, u32[]{:S(2)}) collective-permute-start(bf16[32,4608]{1,0:T(8,128)(2,1)S(1)} %collective-permute-done.10), channel_id=1, source_target_pairs={{0,28},{4,0},{8,4},{12,8},{16,12},{20,16},{24,20},{28,24},{1,29},{... | collective-permute-start | bytes 884744 | tf_op jit(solution)/shard_map/ppermute | solution.py:299
  84.1 3.5 %collective-permute-start.12 = (bf16[32,4608]{1,0:T(8,128)(2,1)}, bf16[32,4608]{1,0:T(8,128)(2,1)S(1)}, u32[]{:S(2)}, u32[]{:S(2)}) collective-permute-start(bf16[32,4608]{1,0:T(8,128)(2,1)} %collective-permute-done.11), channel_id=1, source_target_pairs={{0,28},{4,0},{8,4},{12,8},{16,12},{20,16},{24,20},{28,24},{1,29},{... | collective-permute-start | bytes 884744 | tf_op jit(solution)/shard_map/ppermute | solution.py:299
  87.9 15.0 %all-to-all-done.1 = bf16[16,32,2304]{2,1,0:T(8,128)(2,1)} async-done(((bf16[16,32,2304]{2,1,0:T(8,128)(2,1)}), bf16[16,32,2304]{2,1,0:T(8,128)(2,1)}, u32[]{:S(2)}, u32[]{:S(2)}) %all-to-all-start.1) | async-done | bytes 2359328 | tf_op jit(solution)/shard_map/all_to_all | solution.py:371
  105.6 7.3 %all-to-all-start.2 = ((bf16[8,4,2304]{2,1,0:T(4,128)(2,1)}), bf16[8,4,2304]{2,1,0:T(4,128)(2,1)S(1)}, u32[]{:S(2)}, u32[]{:S(2)}) async-start(bf16[8,4,2304]{2,1,0:T(4,128)(2,1)} %reshape.157), calls=%async_computation.2 | async-start | bytes 294912 | tf_op jit(solution)/shard_map/all_to_all | solution.py:374
  115.4 5.5 %all-to-all-done.2 = bf16[8,4,2304]{2,1,0:T(4,128)(2,1)S(1)} async-done(((bf16[8,4,2304]{2,1,0:T(4,128)(2,1)}), bf16[8,4,2304]{2,1,0:T(4,128)(2,1)S(1)}, u32[]{:S(2)}, u32[]{:S(2)}) %all-to-all-start.2) | async-done | bytes 147488 | tf_op jit(solution)/shard_map/all_to_all | solution.py:374
  127.6 5.8 %all-to-all-start.3 = ((f32[128,1,1]{2,1,0:T(1,128)}), f32[128,1,1]{2,1,0:T(1,128)S(1)}, u32[]{:S(2)}, u32[]{:S(2)}) async-start(f32[128,1,1]{2,1,0:T(1,128)} %broadcast_in_dim.31), calls=%async_computation.3 | async-start | bytes 131072 | tf_op jit(solution)/shard_map/all_to_all | solution.py:305
  134.4 8.4 %all-to-all-done.3 = f32[128,1,1]{2,1,0:T(1,128)S(1)} async-done(((f32[128,1,1]{2,1,0:T(1,128)}), f32[128,1,1]{2,1,0:T(1,128)S(1)}, u32[]{:S(2)}, u32[]{:S(2)}) %all-to-all-start.3) | async-done | bytes 544 | tf_op jit(solution)/shard_map/all_to_all | solution.py:305
  145.0 3.4 %all-to-all-start.4 = ((bf16[8,4,2304]{2,1,0:T(4,128)(2,1)}), bf16[8,4,2304]{2,1,0:T(4,128)(2,1)S(1)}, u32[]{:S(2)}, u32[]{:S(2)}) async-start(bf16[8,4,2304]{2,1,0:T(4,128)(2,1)} %broadcast_in_dim.32), calls=%async_computation.4 | async-start | bytes 294912 | tf_op jit(solution)/shard_map/all_to_all | solution.py:305
  149.4 7.0 %all-to-all-done.4 = bf16[8,4,2304]{2,1,0:T(4,128)(2,1)S(1)} async-done(((bf16[8,4,2304]{2,1,0:T(4,128)(2,1)}), bf16[8,4,2304]{2,1,0:T(4,128)(2,1)S(1)}, u32[]{:S(2)}, u32[]{:S(2)}) %all-to-all-start.4) | async-done | bytes 147488 | tf_op jit(solution)/shard_map/all_to_all | solution.py:305
  158.1 5.9 %all-to-all-start.5 = ((bf16[16,32,2304]{2,1,0:T(8,128)(2,1)}), bf16[16,32,2304]{2,1,0:T(8,128)(2,1)}, u32[]{:S(2)}, u32[]{:S(2)}) async-start(bf16[16,32,2304]{2,1,0:T(8,128)(2,1)} %broadcast_in_dim.34), calls=%async_computation.5 | async-start | bytes 4718592 | tf_op jit(solution)/shard_map/all_to_all | solution.py:305
  165.1 3.3 %collective-permute-start.13 = (bf16[256,4608]{1,0:T(8,128)(2,1)S(1)}, bf16[256,4608]{1,0:T(8,128)(2,1)}, u32[]{:S(2)}, u32[]{:S(2)}) collective-permute-start(bf16[256,4608]{1,0:T(8,128)(2,1)S(1)} %constant_dynamic-update-slice_fusion.refs_1_), channel_id=1, source_target_pairs={{0,1},{1,0},{2,3},{3,2},{4,5},{5,4},{6,7},{7,6},{8,9},{9,8},{10,11... | collective-permute-start | bytes 7077896 | tf_op jit(solution)/shard_map/ppermute | solution.py:71
  168.4 29.7 %all-to-all-done.5 = bf16[16,32,2304]{2,1,0:T(8,128)(2,1)} async-done(((bf16[16,32,2304]{2,1,0:T(8,128)(2,1)}), bf16[16,32,2304]{2,1,0:T(8,128)(2,1)}, u32[]{:S(2)}, u32[]{:S(2)}) %all-to-all-start.5) | async-done | bytes 2359328 | tf_op jit(solution)/shard_map/all_to_all | solution.py:305
  200.2 3.1 %collective-permute-done.17 = f32[4,9,2,256]{3,1,2,0:T(8,128)S(1)} collective-permute-done((f32[4,9,2,256]{3,1,2,0:T(8,128)S(1)}, f32[4,9,2,256]{3,1,2,0:T(8,128)S(1)}, u32[]{:S(2)}, u32[]{:S(2)}) %collective-permute-start.17) | collective-permute-done | bytes 73760 | tf_op jit(solution)/shard_map/ppermute | solution.py:71
  205.9 12.8 %pulled.1 = bf16[1536,512]{1,0:T(8,128)(2,1)S(1)} custom-call(bf16[3,2304,512]{2,1,0:T(8,128)(2,1)} %get-tuple-element.32.refs_0_, bf16[256,4608]{1,0:T(8,128)(2,1)S(1)} %constant_dynamic-update-slice_fusion.refs_1_, bf16[256,4608]{1,0:T(8,128)(2,1)} %collective-permute-done.13.refs_2_, bf16[256,512]{1,0:T(8,128)(2,1)S(1)} %get-tuple-element.110.refs_3_, ...), custom_call_target="tpu_custom_call" | custom-call | flops 7247757312 | bytes 14000000 | tf_op jit(solution)/shard_map/pulled/pallas_call | solution.py:230
  220.9 4.6 %joined.1 = bf16[9,512,512]{2,1,0:T(8,128)(2,1)} custom-call(s32[1]{0:T(128)} %bitcast.core_ref.refs_0_, bf16[256,256]{1,0:T(8,128)(2,1)} %constant.151.clone.order_ref, bf16[512,2304]{1,0:T(8,128)(2,1)} %bitcast.19.own_ref, bf16[512,2304]{1,0:T(8,128)(2,1)} %collective-permute-done.16.other_ref), custom_call_target="tpu_custom_call" | custom-call | tf_op jit(solution)/shard_map/joined/pallas_call | solution.py:276
  (119 shorter events, 50.6 us)
Async XLA Ops:
  2.5 11.0 %collective-permute-start = (bf16[1,4,96,512]{3,2,1,0:T(8,128)(2,1)S(1)}, bf16[1,4,96,512]{3,2,1,0:T(8,128)(2,1)S(1)}, u32[]{:S(2)}, u32[]{:S(2)}) collective-permute-start(bf16[1,4,96,512]{3,2,1,0:T(8,128)(2,1)S(1)} %pad.15), channel_id=1, source_target_pairs={{0,32},{32,64},{64,96},{96,128},{128,160},{160,192},{192,224},{1,3... | collective-permute-start | bytes 1179656 | tf_op jit(solution)/shard_map/ppermute | solution.py:60
  5.7 11.6 %collective-permute-start.1 = (bf16[1,4,96,512]{3,2,1,0:T(8,128)(2,1)S(1)}, bf16[1,4,96,512]{3,2,1,0:T(8,128)(2,1)S(1)}, u32[]{:S(2)}, u32[]{:S(2)}) collective-permute-start(bf16[1,4,96,512]{3,2,1,0:T(8,128)(2,1)S(1)} %pad.17), channel_id=1, source_target_pairs={{32,0},{64,32},{96,64},{128,96},{160,128},{192,160},{224,192},{33,... | collective-permute-start | bytes 1179656 | tf_op jit(solution)/shard_map/ppermute | solution.py:60
  17.5 8.4 %collective-permute-start.2 = (bf16[6,4,1,512]{3,2,1,0:T(2,128)(2,1)S(1)}, bf16[6,4,1,512]{3,2,1,0:T(2,128)(2,1)S(1)}, u32[]{:S(2)}, u32[]{:S(2)}) collective-permute-start(bf16[6,4,1,512]{3,2,1,0:T(2,128)(2,1)S(1)} %pad_maximum_fusion.2), channel_id=1, source_target_pairs={{0,1},{1,2},{2,3},{3,4},{4,5},{5,6},{6,7},{7,8},{8,9},{9,10},{10,1... | collective-permute-start | bytes 73736 | tf_op jit(solution)/shard_map/ppermute | solution.py:67
  20.9 6.0 %collective-permute-start.3 = (bf16[6,4,1,512]{3,2,1,0:T(2,128)(2,1)S(1)}, bf16[6,4,1,512]{3,2,1,0:T(2,128)(2,1)S(1)}, u32[]{:S(2)}, u32[]{:S(2)}) collective-permute-start(bf16[6,4,1,512]{3,2,1,0:T(2,128)(2,1)S(1)} %pad_maximum_fusion.3), channel_id=1, source_target_pairs={{1,0},{2,1},{3,2},{4,3},{5,4},{6,5},{7,6},{8,7},{9,8},{10,9},{11,1... | collective-permute-start | bytes 73736 | tf_op jit(solution)/shard_map/ppermute | solution.py:67
  39.4 18.8 %collective-permute-start.5 = (bf16[512,1536]{1,0:T(8,128)(2,1)}, bf16[512,1536]{1,0:T(8,128)(2,1)}, u32[]{:S(2)}, u32[]{:S(2)}) collective-permute-start(bf16[512,1536]{1,0:T(8,128)(2,1)} %get-tuple-element.29), channel_id=1, source_target_pairs={{0,1},{1,0},{2,3},{3,2},{4,5},{5,4},{6,7},{7,6},{8,9},{9,8},{10,11... | collective-permute-start | bytes 4718600 | tf_op jit(solution)/shard_map/ppermute | solution.py:71
  40.2 16.5 %collective-permute-start.4 = (bf16[512,768]{1,0:T(8,128)(2,1)S(1)}, bf16[512,768]{1,0:T(8,128)(2,1)}, u32[]{:S(2)}, u32[]{:S(2)}) collective-permute-start(bf16[512,768]{1,0:T(8,128)(2,1)S(1)} %get-tuple-element.27), channel_id=1, source_target_pairs={{0,1},{1,0},{2,3},{3,2},{4,5},{5,4},{6,7},{7,6},{8,9},{9,8},{10,11... | collective-permute-start | bytes 2359304 | tf_op jit(solution)/shard_map/ppermute | solution.py:71
  41.2 15.4 %all-to-all-start = ((bf16[16,2,4608]{2,1,0:T(2,128)(2,1)}), bf16[16,2,4608]{2,1,0:T(2,128)(2,1)S(1)}, u32[]{:S(2)}, u32[]{:S(2)}) async-start(bf16[16,2,4608]{2,1,0:T(2,128)(2,1)} %broadcast_in_dim.29), calls=%async_computation | async-start | bytes 589824 | tf_op jit(solution)/shard_map/all_to_all | solution.py:305
  62.4 40.5 %all-to-all-start.1 = ((bf16[16,32,2304]{2,1,0:T(8,128)(2,1)}), bf16[16,32,2304]{2,1,0:T(8,128)(2,1)}, u32[]{:S(2)}, u32[]{:S(2)}) async-start(bf16[16,32,2304]{2,1,0:T(8,128)(2,1)} %bitcast.11), calls=%async_computation.1 | async-start | bytes 4718592 | tf_op jit(solution)/shard_map/all_to_all | solution.py:371
  68.3 8.7 %collective-permute-start.10 = (bf16[32,4608]{1,0:T(8,128)(2,1)S(1)}, bf16[32,4608]{1,0:T(8,128)(2,1)S(1)}, u32[]{:S(2)}, u32[]{:S(2)}) collective-permute-start(bf16[32,4608]{1,0:T(8,128)(2,1)S(1)} %reshape.154), channel_id=1, source_target_pairs={{0,28},{4,0},{8,4},{12,8},{16,12},{20,16},{24,20},{28,24},{1,29},{... | collective-permute-start | bytes 884744 | tf_op jit(solution)/shard_map/ppermute | solution.py:299
  72.9 7.6 %collective-permute-start.6 = (bf16[32,4608]{1,0:T(8,128)(2,1)S(1)}, bf16[32,4608]{1,0:T(8,128)(2,1)}, u32[]{:S(2)}, u32[]{:S(2)}) collective-permute-start(bf16[32,4608]{1,0:T(8,128)(2,1)S(1)} %reshape.154), channel_id=1, source_target_pairs={{0,4},{4,8},{8,12},{12,16},{16,20},{20,24},{24,28},{28,0},{1,5},{5... | collective-permute-start | bytes 884744 | tf_op jit(solution)/shard_map/ppermute | solution.py:297
  73.0 3.6 %collective-permute-start.14 = (f32[3,2,9,256]{3,2,1,0:T(8,128)S(1)}, f32[3,2,9,256]{3,2,1,0:T(8,128)S(1)}, u32[]{:S(2)}, u32[]{:S(2)}) collective-permute-start(f32[3,2,9,256]{3,2,1,0:T(8,128)S(1)} %get-tuple-element.108), channel_id=1, source_target_pairs={{0,1},{1,0},{2,3},{3,2},{4,5},{5,4},{6,7},{7,6},{8,9},{9,8},{10,11... | collective-permute-start | bytes 165896 | tf_op jit(solution)/shard_map/ppermute | solution.py:71
  77.0 7.1 %collective-permute-start.11 = (bf16[32,4608]{1,0:T(8,128)(2,1)S(1)}, bf16[32,4608]{1,0:T(8,128)(2,1)}, u32[]{:S(2)}, u32[]{:S(2)}) collective-permute-start(bf16[32,4608]{1,0:T(8,128)(2,1)S(1)} %collective-permute-done.10), channel_id=1, source_target_pairs={{0,28},{4,0},{8,4},{12,8},{16,12},{20,16},{24,20},{28,24},{1,29},{... | collective-permute-start | bytes 884744 | tf_op jit(solution)/shard_map/ppermute | solution.py:299
  80.5 7.4 %collective-permute-start.7 = (bf16[32,4608]{1,0:T(8,128)(2,1)}, bf16[32,4608]{1,0:T(8,128)(2,1)}, u32[]{:S(2)}, u32[]{:S(2)}) collective-permute-start(bf16[32,4608]{1,0:T(8,128)(2,1)} %collective-permute-done.6), channel_id=1, source_target_pairs={{0,4},{4,8},{8,12},{12,16},{16,20},{20,24},{24,28},{28,0},{1,5},{5... | collective-permute-start | bytes 884744 | tf_op jit(solution)/shard_map/ppermute | solution.py:297
  84.1 80.9 %collective-permute-start.12 = (bf16[32,4608]{1,0:T(8,128)(2,1)}, bf16[32,4608]{1,0:T(8,128)(2,1)S(1)}, u32[]{:S(2)}, u32[]{:S(2)}) collective-permute-start(bf16[32,4608]{1,0:T(8,128)(2,1)} %collective-permute-done.11), channel_id=1, source_target_pairs={{0,28},{4,0},{8,4},{12,8},{16,12},{20,16},{24,20},{28,24},{1,29},{... | collective-permute-start | bytes 884744 | tf_op jit(solution)/shard_map/ppermute | solution.py:299
  87.9 26.0 %collective-permute-start.8 = (bf16[32,4608]{1,0:T(8,128)(2,1)}, bf16[32,4608]{1,0:T(8,128)(2,1)}, u32[]{:S(2)}, u32[]{:S(2)}) collective-permute-start(bf16[32,4608]{1,0:T(8,128)(2,1)} %collective-permute-done.7), channel_id=1, source_target_pairs={{0,4},{4,8},{8,12},{12,16},{16,20},{20,24},{24,28},{28,0},{1,5},{5... | collective-permute-start | bytes 884744 | tf_op jit(solution)/shard_map/ppermute | solution.py:297
  105.6 15.3 %all-to-all-start.2 = ((bf16[8,4,2304]{2,1,0:T(4,128)(2,1)}), bf16[8,4,2304]{2,1,0:T(4,128)(2,1)S(1)}, u32[]{:S(2)}, u32[]{:S(2)}) async-start(bf16[8,4,2304]{2,1,0:T(4,128)(2,1)} %reshape.157), calls=%async_computation.2 | async-start | bytes 294912 | tf_op jit(solution)/shard_map/all_to_all | solution.py:374
  113.9 34.5 %collective-permute-start.9 = (bf16[32,4608]{1,0:T(8,128)(2,1)}, bf16[32,4608]{1,0:T(8,128)(2,1)}, u32[]{:S(2)}, u32[]{:S(2)}) collective-permute-start(bf16[32,4608]{1,0:T(8,128)(2,1)} %collective-permute-done.8), channel_id=1, source_target_pairs={{0,4},{4,8},{8,12},{12,16},{16,20},{20,24},{24,28},{28,0},{1,5},{5... | collective-permute-start | bytes 884744 | tf_op jit(solution)/shard_map/ppermute | solution.py:297
  121.6 4.1 %collective-permute-start.15 = (f32[1,1]{1,0:T(1,128)}, f32[1,1]{1,0:T(1,128)}, u32[]{:S(2)}, u32[]{:S(2)}) collective-permute-start(f32[1,1]{1,0:T(1,128)} %bitcast.17), channel_id=1, source_target_pairs={{0,1},{1,0},{2,3},{3,2},{4,5},{5,4},{6,7},{7,6},{8,9},{9,8},{10,11... | collective-permute-start | bytes 20 | tf_op jit(solution)/shard_map/ppermute | solution.py:71
  127.6 15.1 %all-to-all-start.3 = ((f32[128,1,1]{2,1,0:T(1,128)}), f32[128,1,1]{2,1,0:T(1,128)S(1)}, u32[]{:S(2)}, u32[]{:S(2)}) async-start(f32[128,1,1]{2,1,0:T(1,128)} %broadcast_in_dim.31), calls=%async_computation.3 | async-start | bytes 131072 | tf_op jit(solution)/shard_map/all_to_all | solution.py:305
  145.0 11.4 %all-to-all-start.4 = ((bf16[8,4,2304]{2,1,0:T(4,128)(2,1)}), bf16[8,4,2304]{2,1,0:T(4,128)(2,1)S(1)}, u32[]{:S(2)}, u32[]{:S(2)}) async-start(bf16[8,4,2304]{2,1,0:T(4,128)(2,1)} %broadcast_in_dim.32), calls=%async_computation.4 | async-start | bytes 294912 | tf_op jit(solution)/shard_map/all_to_all | solution.py:305
  158.1 39.9 %all-to-all-start.5 = ((bf16[16,32,2304]{2,1,0:T(8,128)(2,1)}), bf16[16,32,2304]{2,1,0:T(8,128)(2,1)}, u32[]{:S(2)}, u32[]{:S(2)}) async-start(bf16[16,32,2304]{2,1,0:T(8,128)(2,1)} %broadcast_in_dim.34), calls=%async_computation.5 | async-start | bytes 4718592 | tf_op jit(solution)/shard_map/all_to_all | solution.py:305
  165.1 40.8 %collective-permute-start.13 = (bf16[256,4608]{1,0:T(8,128)(2,1)S(1)}, bf16[256,4608]{1,0:T(8,128)(2,1)}, u32[]{:S(2)}, u32[]{:S(2)}) collective-permute-start(bf16[256,4608]{1,0:T(8,128)(2,1)S(1)} %constant_dynamic-update-slice_fusion.refs_1_), channel_id=1, source_target_pairs={{0,1},{1,0},{2,3},{3,2},{4,5},{5,4},{6,7},{7,6},{8,9},{9,8},{10,11... | collective-permute-start | bytes 7077896 | tf_op jit(solution)/shard_map/ppermute | solution.py:71
  198.1 22.8 %collective-permute-start.16 = (bf16[512,2304]{1,0:T(8,128)(2,1)}, bf16[512,2304]{1,0:T(8,128)(2,1)}, u32[]{:S(2)}, u32[]{:S(2)}) collective-permute-start(bf16[512,2304]{1,0:T(8,128)(2,1)} %bitcast.19.own_ref), channel_id=1, source_target_pairs={{0,1},{1,0},{2,3},{3,2},{4,5},{5,4},{6,7},{7,6},{8,9},{9,8},{10,11... | collective-permute-start | bytes 7077896 | tf_op jit(solution)/shard_map/ppermute | solution.py:71
  199.2 4.0 %collective-permute-start.17 = (f32[4,9,2,256]{3,1,2,0:T(8,128)S(1)}, f32[4,9,2,256]{3,1,2,0:T(8,128)S(1)}, u32[]{:S(2)}, u32[]{:S(2)}) collective-permute-start(f32[4,9,2,256]{3,1,2,0:T(8,128)S(1)} %get-tuple-element.88), channel_id=1, source_target_pairs={{0,1},{1,0},{2,3},{3,2},{4,5},{5,4},{6,7},{7,6},{8,9},{9,8},{10,11... | collective-permute-start | bytes 221192 | tf_op jit(solution)/shard_map/ppermute | solution.py:71
  (11 other events, 76.4 us)
